TPU v7x, 32 devices: a whole 2x2x4 slice. The times are simulated.
32 devices in a mesh: rep: 2 (over y), seq: 4 (over z), section: 2 (over core), head: 2 (over x).
Axes of the slice: x: 2, y: 2, z: 4, core: 2. Of those that a mesh axis runs over, the one named last changes fastest.
Arguments:
- hidden: bfloat16 [6, 256, 2048], P('rep', 'seq'), parts along dimension 0, may hold values from -6 to 6
- lengths: int32 [6], P('rep'), parts along dimension 0, may hold values from 1 to 256, 576 in all
- attn_gain: float32 [2, 2048], P('section'), may hold values from 0.1 to 1.9
- w_query: bfloat16 [2, 2048, 2048], P('section', None, 'head'), may hold values from -2 to 2
- w_latent: bfloat16 [2, 2048, 512], P('section'), may hold values from -0.125 to 0.125
- latent_gain: float32 [2, 512], P('section'), may hold values from 0.1 to 1.9
- w_key: bfloat16 [2, 512, 2048], P('section', None, 'head'), may hold values from -0.25 to 0.25
- w_value: bfloat16 [2, 512, 2048], P('section', None, 'head'), may hold values from -0.25 to 0.25
- w_out: bfloat16 [2, 2048, 2048], P('section', 'head'), may hold values from -0.125 to 0.125
Outputs:
- final: float32 [6, 256, 2048], P('rep', ('seq', 'head'), 'section'), parts along dimension 0
- latents: float32 [2, 6, 256, 512], P('section', 'rep', 'seq'), parts along dimension 1
There are 2 independent parts, one for each index of `rep`. A program takes and returns all parts, laid end to end along the dimension named above; an argument that names none is the same for every part. Nothing has to cross between parts.
Inputs may be any that keep to these rules, and one draw needn't show every extreme that they name: lengths sum to 576 and one block holds exactly 256; the live tokens of a block are its first slots.
All inputs are finite; a program needn't handle non-finite values.
Results may differ from a plain program's by a relative error of at most 0.015.
The roundings to bfloat16 on the way count: a program that leaves them out, or rounds other values in their place, can miss the bound.
Values may be sent and summed in bfloat16 or wider, within the bound.
No kernel may reach another device: no remote copies, remote signals or barrier semaphores. Data moves between devices by JAX's collectives and lax.ppermute only.
A program may use at most 128 MiB of HBM per device.

v0:
```python
import jax
import jax.numpy as jnp
from jax import lax
from jax.sharding import PartitionSpec as P

HD = 128


def shifted(value, axis, by):
    length = lax.axis_size(axis)
    pairs = [(i, i + by) for i in range(length) if 0 <= i + by < length]
    return lax.ppermute(value, axis, pairs)


def broadcast(value, axis, root):
    mine = lax.axis_index(axis) == root
    return lax.psum(jnp.where(mine, value, jnp.zeros_like(value)), axis)


def rms_scale(values, gain):
    mean_sq = jnp.mean(values * values, axis=-1, keepdims=True)
    return values * lax.rsqrt(mean_sq + 1e-06) * gain


def visible(group, lengths, query_pos, key_pos, blocks):
    block_ids = jnp.arange(blocks, dtype=jnp.int32)
    past = (block_ids < group)[:, None] & (key_pos[None, :] < lengths[:blocks, None])
    same = (block_ids == group)[None, :, None] & (
        key_pos[None, None, :] <= query_pos[:, None, None]
    )
    return past[None] | same


def online_step(carry, scores, mask, latent_piece):
    top, total, accum = carry
    scores = jnp.where(mask[None], scores, -1e30)
    new_top = jnp.maximum(top, jnp.max(scores, axis=(2, 3)))
    weights = jnp.where(mask[None], jnp.exp(scores - new_top[:, :, None, None]), 0.0)
    total = jnp.sum(weights, axis=(2, 3))
    rounded = weights.astype(jnp.bfloat16)
    gained = jnp.einsum("hqck,ckr->hqr", rounded, latent_piece, preferred_element_type=jnp.float32)
    accum = gained
    return (new_top, total, accum)


def shards(hidden, lengths, attn_gain, w_query, w_latent, latent_gain, w_key, w_value, w_out):
    sections = lax.axis_size("section")
    section_id = lax.axis_index("section")
    seq_id = lax.axis_index("seq")
    head_count = lax.axis_size("head")
    head_id = lax.axis_index("head")
    groups, rows, width = hidden.shape
    layers_here = w_query.shape[0]
    rank = w_latent.shape[2]
    heads_here = w_key.shape[2] // HD
    query_cols = heads_here * HD
    share = rows // head_count
    scale = 1.0 / HD**0.5
    query_pos = seq_id * rows + jnp.arange(rows, dtype=jnp.int32)
    own_cache = jnp.zeros((layers_here, groups, rows, rank), jnp.bfloat16)
    own_store = jnp.zeros((layers_here, groups, rows, rank), jnp.float32)
    finals = jnp.zeros((groups, share, width), jnp.float32)
    incoming = jnp.zeros((share, width), jnp.float32)
    ticks = groups + sections - 1
    for tick in range(ticks):
        blocks = min(tick, groups - 1) + 1
        group = tick - section_id
        active = (group >= 0) & (group < groups)
        group_at = jnp.clip(group, 0, groups - 1)
        own = lax.dynamic_index_in_dim(hidden, group_at, 0, keepdims=False)
        own = lax.dynamic_slice_in_dim(own, head_id * share, share, 0)
        state = jnp.where(section_id == 0, own.astype(jnp.float32), incoming)
        normed_part = rms_scale(state, attn_gain[0]).astype(jnp.bfloat16)
        query_weight = w_query[0]
        latent_weight = w_latent[0]
        piece = lax.all_gather(normed_part, "head", axis=0, tiled=True)
        first = jnp.dot(piece, query_weight, preferred_element_type=jnp.float32)
        second = jnp.dot(piece, latent_weight, preferred_element_type=jnp.float32)
        projected = jnp.concatenate((first, second), axis=1)
        query_full = projected[:, :query_cols]
        raw = projected[:, query_cols:]
        query = query_full.astype(jnp.bfloat16).reshape(rows, heads_here, HD)
        latent_full = rms_scale(raw, latent_gain[0])
        latent = latent_full.astype(jnp.bfloat16)
        kept = own_store[0, group_at]
        own_store = own_store.at[0, group_at].set(jnp.where(active, latent_full, kept))
        key_map = w_key[0].reshape(rank, heads_here, HD)
        value_map = w_value[0].reshape(rank, heads_here, HD)
        absorbed = jnp.einsum("qhd,rhd->hqr", query, key_map, preferred_element_type=jnp.float32)
        absorbed = (absorbed * scale).astype(jnp.bfloat16)
        init = (
            jnp.full((heads_here, rows), -1e30, jnp.float32),
            jnp.zeros((heads_here, rows), jnp.float32),
            jnp.zeros((heads_here, rows, rank), jnp.float32),
        )
        current = own_cache[0, group_at]
        own_cache = own_cache.at[0, group_at].set(jnp.where(active, latent, current))
        attend_piece = lax.all_gather(own_cache[0, :blocks], "seq", axis=1, tiled=True)
        key_pos = jnp.arange(attend_piece.shape[1], dtype=jnp.int32)
        mask = visible(group, lengths, query_pos, key_pos, attend_piece.shape[0])
        scores = jnp.einsum(
            "hqr,ckr->hqck", absorbed, attend_piece, preferred_element_type=jnp.float32
        )
        top, total, accum = online_step(init, scores, mask, attend_piece)
        context = (accum / total[:, :, None]).astype(jnp.bfloat16)
        attn = jnp.einsum("hqr,rhd->qhd", context, value_map, preferred_element_type=jnp.float32)
        attn = attn.astype(jnp.bfloat16).reshape(rows, query_cols)
        out_weight = w_out[0]
        summed = lax.psum_scatter(
            jnp.dot(attn, out_weight, preferred_element_type=jnp.float32).astype(jnp.bfloat16),
            "head",
            scatter_dimension=0,
            tiled=True,
        ).astype(jnp.float32)
        state = state + summed
        keep_final = active & (section_id == sections - 1)
        finals = finals.at[group_at].set(jnp.where(keep_final, state, finals[group_at]))
        if tick + 1 < ticks:
            incoming = shifted(state.astype(jnp.bfloat16), "section", 1).astype(state.dtype)
    mine = finals
    mine = broadcast(mine.astype(jnp.bfloat16), "section", sections - 1).astype(mine.dtype)
    out_pos = seq_id * rows + head_id * share + jnp.arange(share, dtype=jnp.int32)
    live_rows = out_pos[None, :] < lengths[:, None]
    mine = jnp.where(live_rows[:, :, None], mine, jnp.zeros_like(mine))
    part_width = width // sections
    final = lax.dynamic_slice_in_dim(mine, section_id * part_width, part_width, 2)
    live = query_pos[None, :] < lengths[:, None]
    stored = jnp.where(live[None, :, :, None], own_store, jnp.zeros_like(own_store))
    return (final, stored)


def solution(mesh):
    return jax.shard_map(
        shards,
        mesh=mesh,
        in_specs=(
            P("rep", "seq", None),
            P("rep"),
            P("section", None),
            P("section", None, "head"),
            P("section", None, None),
            P("section", None),
            P("section", None, "head"),
            P("section", None, "head"),
            P("section", "head", None),
        ),
        out_specs=(P("rep", ("seq", "head"), "section"), P("section", "rep", "seq", None)),
        check_vma=False,
    )
```

profile of v0, /device:TPU:0, one launch (start us, length us, event | category | flops | bytes accessed | tf_op | source)
XLA Modules:
  0.0 264.4 jit_solution(2058537801430797938)
XLA Ops:
  9.5 7.1 %all_gather.24 = bf16[64,2048]{1,0:T(8,128)(2,1)S(1)} all-gather(bf16[32,2048]{1,0:T(8,128)(2,1)S(1)} %fusion.141), channel_id=1, replica_groups=mesh['rep'=2,'seq'=4,'section'=2,'head'=2] {'head'}, dimensions={0}, use_global_device_ids=true | all-gather | bytes 393216 | tf_op jit(solution)/shard_map/all_gather | solution.py:76
  18.8 14.4 %all-gather = bf16[1,1,256,512]{3,2,1,0:T(8,128)(2,1)S(1)} all-gather(bf16[1,1,64,512]{3,2,1,0:T(8,128)(2,1)S(1)} %get-tuple-element.155), channel_id=2, replica_groups=mesh['rep'=2,'seq'=4,'section'=2,'head'=2] {'seq'}, dimensions={2}, use_global_device_ids=true | all-gather | bytes 327680 | tf_op jit(solution)/shard_map/all_gather | solution.py:98
  33.2 3.0 %fusion.73 = bf16[8,8,8,128]{3,2,1,0:T(8,128)(2,1)S(1)} fusion(bf16[64,2048]{1,0:T(8,128)(2,1)S(1)} %all_gather.24, bf16[1,2048,1024]{2,1,0:T(8,128)(2,1)} %param.36), kind=kOutput, calls=%fused_computation.67 | convolution fusion | flops 268500992 | bytes 4587520 | tf_op jit(solution)/shard_map/dot_general | solution.py:77
  36.3 2.3 copy.34
  38.7 1.8 fusion.213
  40.5 2.5 copy.43
  43.2 1.8 fusion.76
  45.1 3.8 %fusion.16 = bf16[64,2048]{1,0:T(8,128)(2,1)} fusion(bf16[1,1024,2048]{2,1,0:T(8,128)(2,1)} %param.41, bf16[8,8,8,128]{3,2,1,0:T(8,128)(2,1)S(1)} %fusion.76), kind=kOutput, calls=%fused_computation.16 | convolution fusion | flops 268566528 | bytes 4587520 | tf_op jit(solution)/shard_map/dot_general | solution.py:110
  52.7 1.6 bitcast_dynamic-update-slice_fusion.1
  54.3 7.5 %reduce-scatter.5.cloned.1.call-done = bf16[32,2048]{1,0:T(8,128)(2,1)} async-done(((bf16[64,2048]{1,0:T(8,128)(2,1)}), bf16[32,2048]{1,0:T(8,128)(2,1)}) %reduce-scatter.5.cloned.1.call-update) | async-done | bytes 131088 | tf_op jit(solution)/shard_map/reduce_scatter | solution.py:109
  61.8 1.6 fusion.148
  63.4 2.2 collective-permute-start
  69.9 5.6 %all_gather.26 = bf16[64,2048]{1,0:T(8,128)(2,1)S(1)} all-gather(bf16[32,2048]{1,0:T(8,128)(2,1)S(1)} %multiply_convert_fusion.2), channel_id=1, replica_groups=mesh['rep'=2,'seq'=4,'section'=2,'head'=2] {'head'}, dimensions={0}, use_global_device_ids=true | all-gather | bytes 393216 | tf_op jit(solution)/shard_map/all_gather | solution.py:76
  76.1 3.7 %fusion.70 = bf16[8,8,8,128]{3,2,1,0:T(8,128)(2,1)} fusion(bf16[64,2048]{1,0:T(8,128)(2,1)S(1)} %all_gather.26, bf16[1,2048,1024]{2,1,0:T(8,128)(2,1)} %param.36), kind=kOutput, calls=%fused_computation.66 | convolution fusion | flops 268500992 | bytes 4587520 | tf_op jit(solution)/shard_map/dot_general | solution.py:77
  80.6 16.4 %all-gather.1 = bf16[1,2,256,512]{3,2,1,0:T(8,128)(2,1)} all-gather(bf16[1,2,64,512]{3,2,1,0:T(8,128)(2,1)S(1)} %slice.305), channel_id=3, replica_groups=mesh['rep'=2,'seq'=4,'section'=2,'head'=2] {'seq'}, dimensions={2}, use_global_device_ids=true | all-gather | bytes 655360 | tf_op jit(solution)/shard_map/all_gather | solution.py:98
  97.0 3.0 %fusion.216 = (f32[8,64]{1,0:T(8,128)S(1)}, f32[8,64,2,256]{3,1,2,0:T(8,128)}) fusion(bf16[1,2,256,512]{3,2,1,0:T(8,128)(2,1)} %all-gather.1, bf16[512,8,128]{0,2,1:T(8,128)(2,1)} %bitcast.347, bf16[8,8,8,128]{3,2,1,0:T(8,128)(2,1)} %fusion.70, pred[64,2,256]{2,0,1:T(8,128)(4,1)} %and_or_fusion.2), kind=kOutput, calls=%fused_computation.281 | convolution fusion | flops 336592384 | bytes 2787328 | tf_op jit(solution)/shard_map/hqr,ckr->hqck/dot_general | solution.py:101
  100.1 1.6 fusion.84
  101.6 2.4 fusion.77
  104.1 3.7 %fusion.19 = bf16[64,2048]{1,0:T(8,128)(2,1)} fusion(bf16[1,1024,2048]{2,1,0:T(8,128)(2,1)} %param.41, bf16[8,8,8,128]{3,2,1,0:T(8,128)(2,1)S(1)} %fusion.77), kind=kOutput, calls=%fused_computation.17 | convolution fusion | flops 268566528 | bytes 4587520 | tf_op jit(solution)/shard_map/dot_general | solution.py:110
  107.9 1.6 bitcast_dynamic-update-slice_fusion
  110.2 2.3 fusion.177
  112.5 6.5 %reduce-scatter.7.cloned.1.call-done = bf16[32,2048]{1,0:T(8,128)(2,1)} async-done(((bf16[64,2048]{1,0:T(8,128)(2,1)}), bf16[32,2048]{1,0:T(8,128)(2,1)}) %reduce-scatter.7.cloned.1.call-update) | async-done | bytes 131088 | tf_op jit(solution)/shard_map/reduce_scatter | solution.py:109
  120.2 1.7 collective-permute-start.1
  121.9 1.6 constant_dynamic-slice_fusion.1
  124.2 5.8 %all_gather.28 = bf16[64,2048]{1,0:T(8,128)(2,1)S(1)} all-gather(bf16[32,2048]{1,0:T(8,128)(2,1)S(1)} %multiply_convert_fusion.1), channel_id=1, replica_groups=mesh['rep'=2,'seq'=4,'section'=2,'head'=2] {'head'}, dimensions={0}, use_global_device_ids=true | all-gather | bytes 393216 | tf_op jit(solution)/shard_map/all_gather | solution.py:76
  132.9 19.7 %all-gather.2 = bf16[1,3,256,512]{3,2,1,0:T(8,128)(2,1)} all-gather(bf16[1,3,64,512]{3,2,1,0:T(8,128)(2,1)S(1)} %fusion.190), channel_id=4, replica_groups=mesh['rep'=2,'seq'=4,'section'=2,'head'=2] {'seq'}, dimensions={2}, use_global_device_ids=true | all-gather | bytes 983040 | tf_op jit(solution)/shard_map/all_gather | solution.py:98
  152.6 3.4 %fusion.219 = (f32[8,64]{1,0:T(8,128)S(1)}, f32[8,64,3,256]{3,1,2,0:T(8,128)}) fusion(bf16[1,3,256,512]{3,2,1,0:T(8,128)(2,1)} %all-gather.2, bf16[512,8,128]{0,2,1:T(8,128)(2,1)} %bitcast.348, bf16[8,8,8,128]{3,2,1,0:T(8,128)(2,1)} %fusion.67, pred[64,3,256]{2,0,1:T(8,128)(4,1)S(1)} %copy-done.13), kind=kOutput, calls=%fused_computation.282 | convolution fusion | flops 471072256 | bytes 3590144 | tf_op jit(solution)/shard_map/hqr,ckr->hqck/dot_general | solution.py:101
  156.0 1.9 fusion.41
  157.9 3.5 %fusion.78 = bf16[8,8,8,128]{3,2,1,0:T(8,128)(2,1)} fusion(bf16[512,8,128]{2,1,0:T(8,128)(2,1)} %bitcast.353, f32[8,64,3,256]{3,1,2,0:T(8,128)} %get-tuple-element.175, bf16[1,3,256,512]{3,2,1,0:T(8,128)(2,1)} %all-gather.2, f32[8,64]{1,0:T(8,128)S(1)} %broadcast_maximum_fusion.1, pred[64,3,256]{2,0,1:T(8,128)(4,1)S(1)} %copy-done.13, f32[8,64]{1,0:T(8,128)S(1)} %fusion.41), kind=kOutput, calls=%fused_computation.70 | convolution fusion | flops 471531520 | bytes 3592192 | tf_op jit(solution)/shard_map/hqr,rhd->qhd/dot_general | solution.py:106
  161.3 3.8 %fusion.22 = bf16[64,2048]{1,0:T(8,128)(2,1)} fusion(bf16[1,1024,2048]{2,1,0:T(8,128)(2,1)} %param.41, bf16[8,8,8,128]{3,2,1,0:T(8,128)(2,1)} %fusion.78), kind=kOutput, calls=%fused_computation.18 | convolution fusion | flops 268566528 | bytes 4587520 | tf_op jit(solution)/shard_map/dot_general | solution.py:110
  165.2 1.8 fusion.138
  167.6 8.7 %reduce-scatter.9.cloned.1.call-done = bf16[32,2048]{1,0:T(8,128)(2,1)} async-done(((bf16[64,2048]{1,0:T(8,128)(2,1)}), bf16[32,2048]{1,0:T(8,128)(2,1)}) %reduce-scatter.9.cloned.1.call-update) | async-done | bytes 131088 | tf_op jit(solution)/shard_map/reduce_scatter | solution.py:109
  177.4 1.6 collective-permute-start.2
  178.9 2.3 fusion.176
  181.3 1.7 constant_dynamic-slice_fusion
  183.8 5.6 %all_gather.30 = bf16[64,2048]{1,0:T(8,128)(2,1)S(1)} all-gather(bf16[32,2048]{1,0:T(8,128)(2,1)S(1)} %multiply_convert_fusion), channel_id=1, replica_groups=mesh['rep'=2,'seq'=4,'section'=2,'head'=2] {'head'}, dimensions={0}, use_global_device_ids=true | all-gather | bytes 393216 | tf_op jit(solution)/shard_map/all_gather | solution.py:76
  192.2 19.0 %all_gather.31 = bf16[3,256,512]{2,1,0:T(8,128)(2,1)} all-gather(bf16[3,64,512]{2,1,0:T(8,128)(2,1)S(1)} %fusion.186), channel_id=1, replica_groups=mesh['rep'=2,'seq'=4,'section'=2,'head'=2] {'seq'}, dimensions={1}, use_global_device_ids=true | all-gather | bytes 983040 | tf_op jit(solution)/shard_map/all_gather | solution.py:98
  211.2 3.4 %fusion.222 = (f32[8,64]{1,0:T(8,128)S(1)}, f32[8,64,3,256]{3,1,2,0:T(8,128)}) fusion(bf16[3,256,512]{2,1,0:T(8,128)(2,1)} %all_gather.31, bf16[512,8,128]{0,2,1:T(8,128)(2,1)} %bitcast.349, bf16[8,8,8,128]{3,2,1,0:T(8,128)(2,1)} %fusion.64, pred[64,3,256]{2,0,1:T(8,128)(4,1)S(1)} %copy-done.12), kind=kOutput, calls=%fused_computation.283 | convolution fusion | flops 471072256 | bytes 3590144 | tf_op jit(solution)/shard_map/hqr,ckr->hqck/dot_general | solution.py:101
  214.7 1.9 fusion.43
  216.5 3.5 %fusion.79 = bf16[8,8,8,128]{3,2,1,0:T(8,128)(2,1)} fusion(bf16[512,8,128]{2,1,0:T(8,128)(2,1)} %bitcast.354, f32[8,64,3,256]{3,1,2,0:T(8,128)} %get-tuple-element.179, bf16[3,256,512]{2,1,0:T(8,128)(2,1)} %all_gather.31, f32[8,64]{1,0:T(8,128)S(1)} %broadcast_maximum_fusion, pred[64,3,256]{2,0,1:T(8,128)(4,1)S(1)} %copy-done.12, f32[8,64]{1,0:T(8,128)S(1)} %fusion.43), kind=kOutput, calls=%fused_computation.71 | convolution fusion | flops 471531520 | bytes 3592192 | tf_op jit(solution)/shard_map/hqr,rhd->qhd/dot_general | solution.py:106
  220.0 3.8 %fusion.25 = bf16[64,2048]{1,0:T(8,128)(2,1)} fusion(bf16[1,1024,2048]{2,1,0:T(8,128)(2,1)} %param.41, bf16[8,8,8,128]{3,2,1,0:T(8,128)(2,1)} %fusion.79), kind=kOutput, calls=%fused_computation.19 | convolution fusion | flops 268566528 | bytes 4587520 | tf_op jit(solution)/shard_map/dot_general | solution.py:110
  223.9 1.8 fusion.137
  225.7 9.2 %reduce-scatter.11.cloned.1.call-done = bf16[32,2048]{1,0:T(8,128)(2,1)} async-done(((bf16[64,2048]{1,0:T(8,128)(2,1)}), bf16[32,2048]{1,0:T(8,128)(2,1)}) %reduce-scatter.11.cloned.1.call-update) | async-done | bytes 131088 | tf_op jit(solution)/shard_map/reduce_scatter | solution.py:109
  234.9 1.7 fusion.136
  237.4 2.3 fusion.175
  239.7 1.8 broadcast_select_fusion
  241.6 14.5 %all-reduce.2.cloned.1.call-done = bf16[3,32,2048]{2,1,0:T(8,128)(2,1)} async-done(((bf16[3,32,2048]{2,1,0:T(8,128)(2,1)}), bf16[3,32,2048]{2,1,0:T(8,128)(2,1)}) %all-reduce.2.cloned.1.call-update) | async-done | bytes 393232 | tf_op jit(solution)/shard_map/psum | solution.py:17
  256.1 1.8 convert_select_fusion
  (119 shorter events, 25.8 us)
Async XLA Ops:
  7.2 9.5 %copy-start = (bf16[1,2048,512]{2,1,0:T(8,128)(2,1)S(1)}, bf16[1,2048,512]{2,1,0:T(8,128)(2,1)}, u32[]{:S(2)}) copy-start(bf16[1,2048,512]{2,1,0:T(8,128)(2,1)} %param.37) | copy-start | bytes 6291460
  7.2 10.1 %copy-start.18 = (s32[4]{0:T(128)S(1)}, s32[4]{0:T(128)}, u32[]{:S(2)}) copy-start(s32[4]{0:T(128)} %constant.384.clone.1) | copy-start | bytes 52
  7.2 10.8 %copy-start.14 = (f32[1,512]{1,0:T(1,128)S(1)}, f32[1,512]{1,0:T(1,128)}, u32[]{:S(2)}) copy-start(f32[1,512]{1,0:T(1,128)} %param.38) | copy-start | bytes 6148
  7.2 54.6 %reduce-scatter.5.cloned.1.call-start = ((), (), s32[]{:S(2)}) async-start(), calls=%async_computation.4 | async-start | bytes 393216 | tf_op jit(solution)/shard_map/reduce_scatter | solution.py:109
  17.2 19.0 %copy-start.11 = (f32[64,512]{1,0:T(8,128)}, f32[64,512]{1,0:T(8,128)S(1)}, u32[]{:S(2)}) copy-start(f32[64,512]{1,0:T(8,128)S(1)} %get-tuple-element.165) | copy-start | bytes 393220
  36.2 2.3 copy-start.17
  45.1 6.0 %copy-start.20 = (s32[3]{0:T(128)S(1)}, s32[3]{0:T(128)}, u32[]{:S(2)}) copy-start(s32[3]{0:T(128)} %constant.377.clone.1) | copy-start | bytes 40
  45.1 16.8 %copy-start.3 = (bf16[3,64,2048]{2,1,0:T(8,128)(2,1)S(1)}, bf16[3,64,2048]{2,1,0:T(8,128)(2,1)}, u32[]{:S(2)}) copy-start(bf16[3,64,2048]{2,1,0:T(8,128)(2,1)} %param.33) | copy-start | bytes 2359300
  48.9 20.0 %copy-start.15 = (f32[1,2048]{1,0:T(1,128)S(1)}, f32[1,2048]{1,0:T(1,128)}, u32[]{:S(2)}) copy-start(f32[1,2048]{1,0:T(1,128)} %param.35) | copy-start | bytes 24580
  48.9 70.1 %reduce-scatter.7.cloned.1.call-start = ((), (), s32[]{:S(2)}) async-start(), calls=%async_computation.5 | async-start | bytes 393216 | tf_op jit(solution)/shard_map/reduce_scatter | solution.py:109
  54.3 21.8 %copy-start.4 = (f32[1,3,64,512]{3,2,1,0:T(8,128)}, f32[1,3,64,512]{3,2,1,0:T(8,128)S(1)}, u32[]{:S(2)}) copy-start(f32[1,3,64,512]{3,2,1,0:T(8,128)S(1)} %bitcast_dynamic-update-slice_fusion.1) | copy-start | bytes 1179652
  63.4 4.3 %collective-permute-start = (bf16[32,2048]{1,0:T(8,128)(2,1)}, bf16[32,2048]{1,0:T(8,128)(2,1)}, u32[]{:S(2)}, u32[]{:S(2)}) collective-permute-start(bf16[32,2048]{1,0:T(8,128)(2,1)} %fusion.148), channel_id=1, source_target_pairs={{0,2},{1,3},{4,6},{5,7},{8,10},{9,11},{12,14},{13,15},{16,18},{17,... | collective-permute-start | bytes 393224 | tf_op jit(solution)/shard_map/ppermute | solution.py:12
  76.1 3.8 %copy-start.10 = (f32[64,512]{1,0:T(8,128)}, f32[64,512]{1,0:T(8,128)S(1)}, u32[]{:S(2)}) copy-start(f32[64,512]{1,0:T(8,128)S(1)} %get-tuple-element.169) | copy-start | bytes 393220
  79.8 20.2 %copy-start.16 = (pred[64,2,256]{2,0,1:T(8,128)(4,1)S(1)}, pred[64,2,256]{2,0,1:T(8,128)(4,1)}, u32[]{:S(2)}) copy-start(pred[64,2,256]{2,0,1:T(8,128)(4,1)} %and_or_fusion.2) | copy-start | bytes 98308
  107.8 68.5 %reduce-scatter.9.cloned.1.call-start = ((), (), s32[]{:S(2)}) async-start(), calls=%async_computation.6 | async-start | bytes 393216 | tf_op jit(solution)/shard_map/reduce_scatter | solution.py:109
  119.0 11.6 %copy-start.1 = (bf16[1,2048,1024]{2,1,0:T(8,128)(2,1)S(1)}, bf16[1,2048,1024]{2,1,0:T(8,128)(2,1)}, u32[]{:S(2)}) copy-start(bf16[1,2048,1024]{2,1,0:T(8,128)(2,1)} %param.36) | copy-start | bytes 12582916
  120.2 3.3 %collective-permute-start.1 = (bf16[32,2048]{1,0:T(8,128)(2,1)S(1)}, bf16[32,2048]{1,0:T(8,128)(2,1)S(1)}, u32[]{:S(2)}, u32[]{:S(2)}) collective-permute-start(bf16[32,2048]{1,0:T(8,128)(2,1)S(1)} %fusion.149), channel_id=1, source_target_pairs={{0,2},{1,3},{4,6},{5,7},{8,10},{9,11},{12,14},{13,15},{16,18},{17,... | collective-permute-start | bytes 393224 | tf_op jit(solution)/shard_map/ppermute | solution.py:12
  123.5 0.7 copy-start.5
  130.6 1.5 copy-start.9
  130.6 21.9 %copy-start.13 = (pred[64,3,256]{2,0,1:T(8,128)(4,1)S(1)}, pred[64,3,256]{2,0,1:T(8,128)(4,1)}, u32[]{:S(2)}) copy-start(pred[64,3,256]{2,0,1:T(8,128)(4,1)} %get-tuple-element.157) | copy-start | bytes 147460
  165.2 69.7 %reduce-scatter.11.cloned.1.call-start = ((), (), s32[]{:S(2)}) async-start(), calls=%async_computation.7 | async-start | bytes 393216 | tf_op jit(solution)/shard_map/reduce_scatter | solution.py:109
  177.4 5.7 %collective-permute-start.2 = (bf16[32,2048]{1,0:T(8,128)(2,1)S(1)}, bf16[32,2048]{1,0:T(8,128)(2,1)S(1)}, u32[]{:S(2)}, u32[]{:S(2)}) collective-permute-start(bf16[32,2048]{1,0:T(8,128)(2,1)S(1)} %fusion.150), channel_id=1, source_target_pairs={{0,2},{1,3},{4,6},{5,7},{8,10},{9,11},{12,14},{13,15},{16,18},{17,... | collective-permute-start | bytes 393224 | tf_op jit(solution)/shard_map/ppermute | solution.py:12
  181.3 8.7 %copy-start.2 = (bf16[1,2048,1024]{2,1,0:T(8,128)(2,1)S(1)}, bf16[1,2048,1024]{2,1,0:T(8,128)(2,1)}, u32[]{:S(2)}) copy-start(bf16[1,2048,1024]{2,1,0:T(8,128)(2,1)} %param.36) | copy-start | bytes 12582916
  183.0 0.7 copy-start.7
  190.0 1.5 copy-start.8
  190.0 21.2 %copy-start.12 = (pred[64,3,256]{2,0,1:T(8,128)(4,1)S(1)}, pred[64,3,256]{2,0,1:T(8,128)(4,1)}, u32[]{:S(2)}) copy-start(pred[64,3,256]{2,0,1:T(8,128)(4,1)} %get-tuple-element.156) | copy-start | bytes 147460
  220.0 3.9 %copy-start.6 = (bf16[32,2048]{1,0:T(8,128)(2,1)S(1)}, bf16[32,2048]{1,0:T(8,128)(2,1)}, u32[]{:S(2)}) copy-start(bf16[32,2048]{1,0:T(8,128)(2,1)} %copy-done.5) | copy-start | bytes 393220
  223.8 15.9 %copy-start.21 = (pred[3,64]{1,0:T(4,128)(4,1)S(1)}, pred[3,64]{1,0:T(4,128)(4,1)}, u32[]{:S(2)}) copy-start(pred[3,64]{1,0:T(4,128)(4,1)} %broadcast_compare_fusion) | copy-start | bytes 580
  223.8 32.3 %copy-start.19 = (pred[3,32]{1,0:T(4,128)(4,1)S(1)}, pred[3,32]{1,0:T(4,128)(4,1)}, u32[]{:S(2)}) copy-start(pred[3,32]{1,0:T(4,128)(4,1)} %broadcast_compare_fusion.1) | copy-start | bytes 292
  223.9 32.3 %all-reduce.2.cloned.1.call-start = ((), (), s32[]{:S(2)}) async-start(), calls=%async_computation.8 | async-start | bytes 786432 | tf_op jit(solution)/shard_map/psum | solution.py:17
Sparse Core Ops, SparseCore 0:
  49.0 12.7 reduce-scatter.4
  107.9 11.0 reduce-scatter.6
  165.3 10.9 reduce-scatter.8
  224.0 10.8 reduce-scatter.10
  237.7 18.3 all-reduce.1
where the time goes:
time: 266 us; the launch traced here: 264 us
  blocking collectives  93.7 us (35%)
  matrix products  50.1 us (19%)
  waiting for transfers between devices  46.5 us (17%)
  other arithmetic  43 us (16%)
  between operations  14.3 us (5%)
  local copies, waits for them, and re-layouts  11.2 us (4%)
  starting transfers between devices  5.73 us (2%)
    all_gather x4, blocking collectives, shards(): lax.all_gather(own_cache[0, :blocks], 'seq', axis=1, tiled=True)  69.5 us
    reduce_scatter x4, waiting for transfers between devices, shards(): lax.psum_scatter(jnp.dot(attn, out_weight, preferred_element_type=jnp.flo...  31.8 us
    all_gather x4, blocking collectives, shards(): piece = lax.all_gather(normed_part, 'head', axis=0, tiled=True)  24.2 us
    dot_general x4, matrix products, shards(): jnp.dot(attn, out_weight, preferred_element_type=jnp.float32)  15.2 us
    psum x1, waiting for transfers between devices, broadcast(): return lax.psum(jnp.where(mine, value, jnp.zeros_like(value)), axis)  14.5 us
    dot_general x4, matrix products, shards(): jnp.einsum('hqr,ckr->hqck', absorbed, attend_piece, preferred_element_typ...  11.7 us
    dot_general x4, matrix products, shards(): jnp.einsum('hqr,rhd->qhd', context, value_map, preferred_element_type=jnp...  11.1 us
    dot_general x4, matrix products, shards(): first = jnp.dot(piece, query_weight, preferred_element_type=jnp.float32)  9.77 us
  transfers between devices with their start and end apart: 8, of which 5 were waited for; matrix products, arithmetic and copies ran while one was open for 10% of the time, Pallas kernels for 0%

commit v1 on v0

v1 whole, which is shorter than its diff:
```python
import functools

import jax
import jax.numpy as jnp
from jax import lax
from jax.experimental import pallas as pl
from jax.experimental.pallas import tpu as pltpu
from jax.sharding import PartitionSpec as P

HD = 128
AXES = ("seq", "section", "head")
F32 = jnp.float32
BF16 = jnp.bfloat16
VMEM = pl.BlockSpec(memory_space=pltpu.VMEM)
SMEM = pl.BlockSpec(memory_space=pltpu.SMEM)
MIB = 1 << 20


def permute(value, sizes, target):
    pairs = []
    for s in range(sizes[0]):
        for c in range(sizes[1]):
            for h in range(sizes[2]):
                ts, tc, th = target(s, c, h)
                at = (s * sizes[1] + c) * sizes[2] + h
                to = (ts * sizes[1] + tc) * sizes[2] + th
                pairs.append((at, to))
    return lax.ppermute(value, AXES, pairs)


def rms(values, gain):
    mean_sq = jnp.mean(values * values, axis=-1, keepdims=True)
    return values * lax.rsqrt(mean_sq + 1e-06) * gain


def dot(a, b, dims=((1,), (0,))):
    return lax.dot_general(a, b, (dims, ((), ())), preferred_element_type=F32)


def tree_sum(terms):
    terms = [t.astype(F32) for t in terms]
    while len(terms) > 1:
        terms = [sum(terms[i : i + 2]) for i in range(0, len(terms), 2)]
    return terms[0]


def latent_body(n_parts, *refs):
    x_ref = refs[0]
    parts = refs[1 : 1 + n_parts]
    gain_ref, w_ref, lgain_ref, normed_ref, full_ref, latent_ref = refs[1 + n_parts :]
    state = x_ref[...].astype(F32)
    if n_parts:
        state = state + tree_sum([p[...] for p in parts])
    normed = rms(state, gain_ref[...]).astype(BF16)
    normed_ref[...] = normed
    full = rms(dot(normed, w_ref[...]), lgain_ref[...])
    full_ref[...] = full
    latent_ref[...] = full.astype(BF16)


def query_body(scale, normed_ref, wq_ref, wk_ref, out_ref):
    heads = out_ref.shape[0]
    query = dot(normed_ref[...], wq_ref[...]).astype(BF16)
    for h in range(heads):
        cols = slice(h * HD, (h + 1) * HD)
        one = dot(query[:, cols], wk_ref[:, cols], ((1,), (1,)))
        out_ref[h] = (one * scale).astype(BF16)


def attend_body(groups, rows, n_pieces, *refs):
    seq_ref, lengths_ref, absorbed_ref = refs[:3]
    pieces = refs[3 : 3 + n_pieces]
    wv_ref, wo_ref, out_ref, kv, attn = refs[3 + n_pieces :]
    heads = absorbed_ref.shape[0]
    rank = kv.shape[1]
    block = n_pieces * rows
    me = seq_ref[0]
    for g in range(groups):
        for k in range(n_pieces):
            kv[pl.ds(g * block + k * rows, rows), :] = pieces[k][pl.ds(g * rows, rows), :]
    col = lax.broadcasted_iota(jnp.int32, (rows, block), 1)
    row = lax.broadcasted_iota(jnp.int32, (rows, block), 0)
    key_pos = jnp.bitwise_xor(me, col // rows) * rows + col % rows
    query_pos = me * rows + row
    causal = key_pos <= query_pos
    for g in range(groups):
        keys = kv[: (g + 1) * block, :]
        absorbed = absorbed_ref[:, g * rows : (g + 1) * rows, :].reshape(heads * rows, rank)
        scores = dot(absorbed, keys, ((1,), (1,)))
        mask = [key_pos < lengths_ref[b] for b in range(g)] + [causal]
        mask = jnp.concatenate(mask, axis=1)[None]
        scores = scores.reshape(heads, rows, (g + 1) * block)
        scores = jnp.where(mask, scores, -1e30)
        top = jnp.max(scores, axis=2, keepdims=True)
        weights = jnp.where(mask, jnp.exp(scores - top), 0.0)
        total = jnp.sum(weights, axis=2, keepdims=True).reshape(heads * rows, 1)
        rounded = weights.astype(BF16).reshape(heads * rows, (g + 1) * block)
        context = (dot(rounded, keys) / total).astype(BF16)
        for h in range(heads):
            cols = slice(h * HD, (h + 1) * HD)
            one = dot(context[h * rows : (h + 1) * rows], wv_ref[:, cols])
            attn[g * rows : (g + 1) * rows, cols] = one.astype(BF16)
    out_ref[...] = dot(attn[...], wo_ref[...]).astype(BF16)


def params(limit):
    return pltpu.CompilerParams(vmem_limit_bytes=limit * MIB)


def shards(hidden, lengths, attn_gain, w_query, w_latent, latent_gain, w_key, w_value, w_out):
    n_seq = lax.axis_size("seq")
    n_sec = lax.axis_size("section")
    n_head = lax.axis_size("head")
    sizes = (n_seq, n_sec, n_head)
    seq_id = lax.axis_index("seq")
    section_id = lax.axis_index("section")
    head_id = lax.axis_index("head")
    groups, rows, width = hidden.shape
    rank = w_latent.shape[2]
    heads = w_key.shape[2] // HD
    total_rows = groups * rows
    share = rows // n_head
    part_width = width // n_sec
    x = hidden.reshape(total_rows, width)
    seq_arr = seq_id.astype(jnp.int32).reshape(1)
    wq, wl, wk, wv, wo = w_query[0], w_latent[0], w_key[0], w_value[0], w_out[0]
    latents = []
    parts = []
    for tick in range(n_sec):
        normed, full, latent = pl.pallas_call(
            functools.partial(latent_body, len(parts)),
            out_shape=(
                jax.ShapeDtypeStruct((total_rows, width), BF16),
                jax.ShapeDtypeStruct((total_rows, rank), F32),
                jax.ShapeDtypeStruct((total_rows, rank), BF16),
            ),
            in_specs=[VMEM] * (4 + len(parts)),
            out_specs=(VMEM, VMEM, VMEM),
            compiler_params=params(16),
            cost_estimate=pl.CostEstimate(
                flops=2 * total_rows * width * rank,
                bytes_accessed=2 * width * (rank + 2 * total_rows),
                transcendentals=0,
            ),
            name=f"latent{tick}",
        )(x, *parts, attn_gain, wl, latent_gain)
        latents.append(full)
        pieces = [latent] + [
            permute(latent, sizes, lambda s, c, h, k=k: (s ^ k, c, h) if c == tick else (s, c, h))
            for k in range(1, n_seq)
        ]
        absorbed = pl.pallas_call(
            functools.partial(query_body, 1.0 / HD**0.5),
            out_shape=jax.ShapeDtypeStruct((heads, total_rows, rank), BF16),
            in_specs=[VMEM] * 3,
            out_specs=VMEM,
            compiler_params=params(16),
            cost_estimate=pl.CostEstimate(
                flops=2 * total_rows * heads * HD * (width + rank),
                bytes_accessed=2 * heads * HD * (width + rank + total_rows),
                transcendentals=0,
            ),
            name=f"query{tick}",
        )(normed, wq, wk)
        partial = pl.pallas_call(
            functools.partial(attend_body, groups, rows, n_seq),
            out_shape=jax.ShapeDtypeStruct((total_rows, width), BF16),
            in_specs=[SMEM, SMEM] + [VMEM] * (3 + n_seq),
            out_specs=VMEM,
            scratch_shapes=[
                pltpu.VMEM((groups * n_seq * rows, rank), BF16),
                pltpu.VMEM((total_rows, heads * HD), BF16),
            ],
            compiler_params=params(32),
            cost_estimate=pl.CostEstimate(
                flops=4 * heads * total_rows * groups * n_seq * rows * rank,
                bytes_accessed=2 * heads * HD * (width + rank),
                transcendentals=heads * total_rows * groups * n_seq * rows,
            ),
            name=f"attend{tick}",
        )(seq_arr, lengths, absorbed, *pieces, wv, wo)
        if tick + 1 < n_sec:
            parts = [permute(partial, sizes, lambda s, c, h: (s, (c + 1) % n_sec, h))] + [
                permute(
                    partial,
                    sizes,
                    lambda s, c, h, k=k: (s, c + 1, h ^ k) if c + 1 < n_sec else (s, 0, h),
                )
                for k in range(1, n_head)
            ]
    state = x.astype(F32) + tree_sum(parts)
    mine = partial.reshape(groups, n_head, share, width)
    base = state.reshape(groups, n_head, share, width)
    is_mine = (jnp.arange(n_head) == head_id)[None, :, None, None]
    both = jnp.where(is_mine, base + mine.astype(F32), mine.astype(F32))
    left = both[..., :part_width].astype(BF16)
    came = permute(left, sizes, lambda s, c, h: (s, (c + 1) % n_sec, h))
    half = jnp.where(section_id == n_sec - 1, both[..., part_width:], came.astype(F32))
    own = lax.dynamic_index_in_dim(half, head_id, 1, keepdims=False)
    others = [
        permute(
            lax.dynamic_index_in_dim(half, head_id ^ k, 1, keepdims=False).astype(BF16),
            sizes,
            lambda s, c, h, k=k: (s, c, h ^ k),
        ).astype(F32)
        for k in range(1, n_head)
    ]
    final = sum(others, own)
    out_pos = seq_id * rows + head_id * share + jnp.arange(share, dtype=jnp.int32)
    final = jnp.where((out_pos[None, :] < lengths[:, None])[:, :, None], final, 0.0)
    stored = latents[0]
    for tick in range(1, n_sec):
        stored = jnp.where(section_id == tick, latents[tick], stored)
    query_pos = seq_id * rows + jnp.arange(rows, dtype=jnp.int32)
    live = query_pos[None, :] < lengths[:, None]
    stored = jnp.where(live[..., None], stored.reshape(groups, rows, rank), 0.0)[None]
    return (final, stored)


def solution(mesh):
    return jax.shard_map(
        shards,
        mesh=mesh,
        in_specs=(
            P("rep", "seq", None),
            P("rep"),
            P("section", None),
            P("section", None, "head"),
            P("section", None, None),
            P("section", None),
            P("section", None, "head"),
            P("section", None, "head"),
            P("section", "head", None),
        ),
        out_specs=(P("rep", ("seq", "head"), "section"), P("section", "rep", "seq", None)),
        check_vma=False,
    )
```

time: 266 us -> 78 us (0.29)
  blocking collectives: 93.7 us -> 0 us
  matrix products: 50.1 us -> 0 us
  other arithmetic: 43 us -> 4.14 us
  waiting for transfers between devices: 46.5 us -> 18.4 us
  starting transfers between devices: 5.73 us -> 24.6 us
  Pallas kernels: 0 us -> 17.2 us
  between operations: 14.3 us -> 0.91 us
    all_gather x8 -> x0, blocking collectives: 93.7 us -> none  [the longest x4 69.5 us: shards(): lax.all_gather(own_cache[0, :blocks], 'seq', axis=1, tiled=True)]
    dot_general x20 -> x0, matrix products: 50.1 us -> none  [the longest x4 15.2 us: shards(): jnp.dot(attn, out_weight, preferred_element_type=jnp.float32)]
    reduce_scatter x4 -> x0, waiting for transfers between devices: 31.8 us -> none  [shards(): lax.psum_scatter(jnp.dot(attn, out_weight, preferred_element_type=jnp.flo...]
    ppermute x3 -> x10, starting transfers between devices: 5.52 us -> 24.6 us  [permute(): return lax.ppermute(value, AXES, pairs)]
    ppermute x3 -> x10, waiting for transfers between devices: 0.01 us -> 18.4 us  [permute(): return lax.ppermute(value, AXES, pairs)]
    scatter x12 -> x0, other arithmetic: 18.3 us -> none  [the longest x4 8.61 us: shards(): own_store.at[0, group_at].set(jnp.where(active, latent_full, kept))]
    pallas_call x0 -> x6, Pallas kernels: none -> 17.2 us  [the longest x2 10.9 us: shards(): pl.pallas_call(functools.partial(attend_body, groups, rows, n_seq), out_s...]
    psum x1 -> x0, waiting for transfers between devices: 14.5 us -> none  [broadcast(): return lax.psum(jnp.where(mine, value, jnp.zeros_like(value)), axis)]
  transfers between devices with their start and end apart: 8 -> 10, of which waited for: 5 -> 5; matrix products, arithmetic and copies ran while one was open for 10% -> 4% of each run, Pallas kernels for 0% -> 4%
where the time goes in v1:
time: 78 us; the launch traced here: 77.4 us
  starting transfers between devices  24.6 us (32%)
  waiting for transfers between devices  18.4 us (24%)
  Pallas kernels  17.2 us (22%)
  local copies, waits for them, and re-layouts  12.2 us (16%)
  other arithmetic  4.14 us (5%)
  between operations  0.91 us (1%)
    ppermute x10, starting transfers between devices, permute(): return lax.ppermute(value, AXES, pairs)  24.6 us
    ppermute x10, waiting for transfers between devices, permute(): return lax.ppermute(value, AXES, pairs)  18.4 us
    unnamed x46, local copies, waits for them, and re-layouts  12.1 us
    pallas_call x2, Pallas kernels, shards(): pl.pallas_call(functools.partial(attend_body, groups, rows, n_seq), out_s...  10.9 us
    pallas_call x2, Pallas kernels, shards(): pl.pallas_call(functools.partial(latent_body, len(parts)), out_shape=(jax...  3.47 us
    pallas_call x2, Pallas kernels, shards(): pl.pallas_call(functools.partial(query_body, 1.0 / HD ** 0.5), out_shape=...  2.84 us
    add x1, other arithmetic, shards(): state = x.astype(F32) + tree_sum(parts)  1.77 us
  transfers between devices with their start and end apart: 10, of which 5 were waited for; matrix products, arithmetic and copies ran while one was open for 4% of the time, Pallas kernels for 4%

profile of v1, /device:TPU:0, one launch (start us, length us, event | category | flops | bytes accessed | tf_op | source)
XLA Modules:
  0.0 77.4 jit_solution(9074465622146868782)
XLA Ops:
  0.6 0.0 copy-start.2
  0.6 1.6 %copy-done.2 = bf16[1,2048,512]{2,1,0:T(8,128)(2,1)S(1)} copy-done((bf16[1,2048,512]{2,1,0:T(8,128)(2,1)S(1)}, bf16[1,2048,512]{2,1,0:T(8,128)(2,1)}, u32[]{:S(2)}) %copy-start.2) | copy-done | bytes 2097176
  2.2 1.1 %copy-done.4 = bf16[3,64,2048]{2,1,0:T(8,128)(2,1)S(1)} copy-done((bf16[3,64,2048]{2,1,0:T(8,128)(2,1)S(1)}, bf16[3,64,2048]{2,1,0:T(8,128)(2,1)}, u32[]{:S(2)}) %copy-start.4) | copy-done | bytes 786456
  3.4 0.7 copy-done.8
  4.1 0.7 copy-done.10
  4.7 0.9 %latent0.1 = (bf16[192,2048]{1,0:T(8,128)(2,1)S(1)}, f32[192,512]{1,0:T(8,128)S(1)}, bf16[192,512]{1,0:T(8,128)(2,1)S(1)}) custom-call(bf16[192,2048]{1,0:T(8,128)(2,1)S(1)} %bitcast.22, f32[1,2048]{1,0:T(1,128)S(1)} %copy-done.8, bf16[2048,512]{1,0:T(8,128)(2,1)S(1)} %bitcast.20, f32[1,512]{1,0:T(1,128)S(1)} %copy-done.10), custom_call_target="tpu_custom_call" | custom-call | flops 402653184 | bytes 3670016 | tf_op jit(solution)/shard_map/latent0/pallas_call | solution.py:130
  5.6 7.0 %collective-permute-start.2 = (bf16[192,512]{1,0:T(8,128)(2,1)S(1)}, bf16[192,512]{1,0:T(8,128)(2,1)S(1)}, u32[]{:S(2)}, u32[]{:S(2)}) collective-permute-start(bf16[192,512]{1,0:T(8,128)(2,1)S(1)} %get-tuple-element.9.refs_3_), channel_id=1, source_target_pairs={{0,12},{1,13},{2,2},{3,3},{4,8},{5,9},{6,6},{7,7},{8,4},{9,5},{10,... | collective-permute-start | bytes 589832 | tf_op jit(solution)/shard_map/ppermute | solution.py:28
  12.6 1.9 %collective-permute-start.1 = (bf16[192,512]{1,0:T(8,128)(2,1)S(1)}, bf16[192,512]{1,0:T(8,128)(2,1)S(1)}, u32[]{:S(2)}, u32[]{:S(2)}) collective-permute-start(bf16[192,512]{1,0:T(8,128)(2,1)S(1)} %get-tuple-element.9.refs_3_), channel_id=1, source_target_pairs={{0,8},{1,9},{2,2},{3,3},{4,12},{5,13},{6,6},{7,7},{8,0},{9,1},{10,... | collective-permute-start | bytes 589832 | tf_op jit(solution)/shard_map/ppermute | solution.py:28
  14.5 2.5 %collective-permute-start = (bf16[192,512]{1,0:T(8,128)(2,1)S(1)}, bf16[192,512]{1,0:T(8,128)(2,1)S(1)}, u32[]{:S(2)}, u32[]{:S(2)}) collective-permute-start(bf16[192,512]{1,0:T(8,128)(2,1)S(1)} %get-tuple-element.9.refs_3_), channel_id=1, source_target_pairs={{0,4},{1,5},{2,2},{3,3},{4,0},{5,1},{6,6},{7,7},{8,12},{9,13},{10,... | collective-permute-start | bytes 589832 | tf_op jit(solution)/shard_map/ppermute | solution.py:28
  17.0 0.0 copy-start
  17.0 2.2 %copy-done = bf16[1,2048,1024]{2,1,0:T(8,128)(2,1)S(1)} copy-done((bf16[1,2048,1024]{2,1,0:T(8,128)(2,1)S(1)}, bf16[1,2048,1024]{2,1,0:T(8,128)(2,1)}, u32[]{:S(2)}) %copy-start) | copy-done | bytes 4194328
  19.2 1.4 %query0.1.refs_2_ = bf16[8,192,512]{2,1,0:T(8,128)(2,1)S(1)} custom-call(bf16[192,2048]{1,0:T(8,128)(2,1)S(1)} %get-tuple-element.8.normed_ref, bf16[2048,1024]{1,0:T(8,128)(2,1)S(1)} %bitcast.18, bf16[512,1024]{1,0:T(8,128)(2,1)S(1)} %bitcast.24), custom_call_target="tpu_custom_call" | custom-call | flops 1006632960 | bytes 5636096 | tf_op jit(solution)/shard_map/query0/pallas_call | solution.py:152
  20.7 0.7 copy-done.16
  21.3 0.9 %collective-permute-done.1.refs_5_ = bf16[192,512]{1,0:T(8,128)(2,1)S(1)} collective-permute-done((bf16[192,512]{1,0:T(8,128)(2,1)S(1)}, bf16[192,512]{1,0:T(8,128)(2,1)S(1)}, u32[]{:S(2)}, u32[]{:S(2)}) %collective-permute-start.1) | collective-permute-done | bytes 196640 | tf_op jit(solution)/shard_map/ppermute | solution.py:28
  22.3 0.7 copy-done.18
  22.9 1.2 %collective-permute-done.refs_4_ = bf16[192,512]{1,0:T(8,128)(2,1)S(1)} collective-permute-done((bf16[192,512]{1,0:T(8,128)(2,1)S(1)}, bf16[192,512]{1,0:T(8,128)(2,1)S(1)}, u32[]{:S(2)}, u32[]{:S(2)}) %collective-permute-start) | collective-permute-done | bytes 196640 | tf_op jit(solution)/shard_map/ppermute | solution.py:28
  24.1 0.7 copy-done.20
  24.8 0.9 %copy-done.17 = bf16[192,512]{1,0:T(8,128)(2,1)S(1)} copy-done((bf16[192,512]{1,0:T(8,128)(2,1)S(1)}, bf16[192,512]{1,0:T(8,128)(2,1)}, u32[]{:S(2)}) %copy-start.17) | copy-done | bytes 196632
  25.7 0.9 %copy-done.19 = bf16[192,512]{1,0:T(8,128)(2,1)S(1)} copy-done((bf16[192,512]{1,0:T(8,128)(2,1)S(1)}, bf16[192,512]{1,0:T(8,128)(2,1)}, u32[]{:S(2)}) %copy-start.19) | copy-done | bytes 196632
  26.6 0.9 %copy-done.21 = bf16[192,512]{1,0:T(8,128)(2,1)S(1)} copy-done((bf16[192,512]{1,0:T(8,128)(2,1)S(1)}, bf16[192,512]{1,0:T(8,128)(2,1)}, u32[]{:S(2)}) %copy-start.21) | copy-done | bytes 196632
  27.6 5.9 %attend0.1 = bf16[192,2048]{1,0:T(8,128)(2,1)} custom-call(s32[1]{0:T(128)} %bitcast.1.refs_0_, s32[3]{0:T(128)S(1)} %copy-done.22, bf16[8,192,512]{2,1,0:T(8,128)(2,1)S(1)} %query0.1.refs_2_, bf16[192,512]{1,0:T(8,128)(2,1)S(1)} %get-tuple-element.9.refs_3_, bf16[192,512]{1,0:T(8,128)(2,1)S(1)} %copy-done.21, bf16[192,512]{1,0:T(8,128)(2,1)S(1)} %copy-done.19, ...), custom_call_target="tpu_custom_call" | custom-call | flops 2415919104 | bytes 5242880 | tf_op jit(solution)/shard_map/attend0/pallas_call | solution.py:165
  33.5 0.5 collective-permute-start.3
  34.0 0.1 broadcast_compare_fusion
  34.1 9.2 %collective-permute-done.4.refs_2_ = bf16[192,2048]{1,0:T(8,128)(2,1)} collective-permute-done((bf16[192,2048]{1,0:T(8,128)(2,1)}, bf16[192,2048]{1,0:T(8,128)(2,1)}, u32[]{:S(2)}, u32[]{:S(2)}) %collective-permute-start.4) | collective-permute-done | bytes 786464 | tf_op jit(solution)/shard_map/ppermute | solution.py:28
  43.4 0.0 copy-start.1
  43.4 2.6 %latent1.1 = (bf16[192,2048]{1,0:T(8,128)(2,1)S(1)}, f32[192,512]{1,0:T(8,128)S(1)}, bf16[192,512]{1,0:T(8,128)(2,1)S(1)}) custom-call(bf16[192,2048]{1,0:T(8,128)(2,1)S(1)} %bitcast.23, bf16[192,2048]{1,0:T(8,128)(2,1)} %collective-permute-done.3.refs_1_, bf16[192,2048]{1,0:T(8,128)(2,1)} %collective-permute-done.4.refs_2_, f32[1,2048]{1,0:T(1,128)S(1)} %copy-done.9, ...), custom_call_target="tpu_custom_call" | custom-call | flops 402653184 | bytes 3670016 | tf_op jit(solution)/shard_map/latent1/pallas_call | solution.py:130
  46.0 0.0 copy-start.7
  46.0 0.8 %collective-permute-start.7 = (bf16[192,512]{1,0:T(8,128)(2,1)S(1)}, bf16[192,512]{1,0:T(8,128)(2,1)S(1)}, u32[]{:S(2)}, u32[]{:S(2)}) collective-permute-start(bf16[192,512]{1,0:T(8,128)(2,1)S(1)} %get-tuple-element.11.refs_3_), channel_id=1, source_target_pairs={{0,0},{1,1},{2,14},{3,15},{4,4},{5,5},{6,10},{7,11},{8,8},{9,9},{1... | collective-permute-start | bytes 589832 | tf_op jit(solution)/shard_map/ppermute | solution.py:28
  46.8 0.7 collective-permute-start.6
  47.5 0.9 %collective-permute-start.5 = (bf16[192,512]{1,0:T(8,128)(2,1)S(1)}, bf16[192,512]{1,0:T(8,128)(2,1)S(1)}, u32[]{:S(2)}, u32[]{:S(2)}) collective-permute-start(bf16[192,512]{1,0:T(8,128)(2,1)S(1)} %get-tuple-element.11.refs_3_), channel_id=1, source_target_pairs={{0,0},{1,1},{2,6},{3,7},{4,4},{5,5},{6,2},{7,3},{8,8},{9,9},{10,14... | collective-permute-start | bytes 589832 | tf_op jit(solution)/shard_map/ppermute | solution.py:28
  48.4 1.8 %add_add_fusion = f32[192,2048]{1,0:T(8,128)S(1)} fusion(bf16[192,2048]{1,0:T(8,128)(2,1)} %collective-permute-done.4.refs_2_, bf16[192,2048]{1,0:T(8,128)(2,1)} %collective-permute-done.3.refs_1_, bf16[3,64,2048]{2,1,0:T(8,128)(2,1)S(1)} %copy-done.5), kind=kLoop, calls=%fused_computation.1 | loop fusion | flops 1966080 | bytes 3932160 | tf_op jit(solution)/shard_map/add | solution.py:191
  50.1 0.0 copy-start.13
  50.2 0.0 copy-start.15
  50.2 1.4 %query1.1.refs_2_ = bf16[8,192,512]{2,1,0:T(8,128)(2,1)S(1)} custom-call(bf16[192,2048]{1,0:T(8,128)(2,1)S(1)} %get-tuple-element.10.normed_ref, bf16[2048,1024]{1,0:T(8,128)(2,1)S(1)} %bitcast.19, bf16[512,1024]{1,0:T(8,128)(2,1)S(1)} %bitcast.25), custom_call_target="tpu_custom_call" | custom-call | flops 1006632960 | bytes 5636096 | tf_op jit(solution)/shard_map/query1/pallas_call | solution.py:152
  51.6 0.7 copy-done.13
  52.3 0.3 copy-done.15
  52.6 5.0 %attend1.1 = bf16[192,2048]{1,0:T(8,128)(2,1)S(1)} custom-call(s32[1]{0:T(128)} %bitcast.1.refs_0_, s32[3]{0:T(128)S(1)} %copy-done.22, bf16[8,192,512]{2,1,0:T(8,128)(2,1)S(1)} %query1.1.refs_2_, bf16[192,512]{1,0:T(8,128)(2,1)S(1)} %get-tuple-element.11.refs_3_, bf16[192,512]{1,0:T(8,128)(2,1)S(1)} %collective-permute-done.5.refs_4_, ...), custom_call_target="tpu_custom_call" | custom-call | flops 2415919104 | bytes 5242880 | tf_op jit(solution)/shard_map/attend1/pallas_call | solution.py:165
  57.6 0.4 add_select_fusion
  58.0 0.1 slice.13
  58.1 9.8 %collective-permute-start.8 = (bf16[3,2,32,1024]{3,2,0,1:T(8,128)(2,1)S(1)}, bf16[3,2,32,1024]{3,2,0,1:T(8,128)(2,1)S(1)}, u32[]{:S(2)}, u32[]{:S(2)}) collective-permute-start(bf16[3,2,32,1024]{3,2,0,1:T(8,128)(2,1)S(1)} %slice.13), channel_id=1, source_target_pairs={{0,2},{1,3},{2,0},{3,1},{4,6},{5,7},{6,4},{7,5},{8,10},{9,11},{10,... | collective-permute-start | bytes 1179656 | tf_op jit(solution)/shard_map/ppermute | solution.py:28
  67.9 0.1 broadcast_compare_fusion.1
  67.9 0.1 broadcast_select_fusion.1
  68.0 1.2 %collective-permute-done.8 = bf16[3,2,32,1024]{3,2,0,1:T(8,128)(2,1)S(1)} collective-permute-done((bf16[3,2,32,1024]{3,2,0,1:T(8,128)(2,1)S(1)}, bf16[3,2,32,1024]{3,2,0,1:T(8,128)(2,1)S(1)}, u32[]{:S(2)}, u32[]{:S(2)}) %collective-permute-start.8) | collective-permute-done | bytes 393248 | tf_op jit(solution)/shard_map/ppermute | solution.py:28
  69.2 0.1 slice_select_fusion
  69.4 0.6 collective-permute-start.9
  70.0 0.8 %broadcast_select_fusion = f32[1,3,64,512]{3,2,1,0:T(8,128)} fusion(f32[1,3,64,512]{3,2,1,0:T(8,128)S(1)} %bitcast.32, pred[3,64]{1,0:T(4,128)(4,1)S(1)} %broadcast_compare_fusion), kind=kLoop, calls=%fused_computation.8 | loop fusion | flops 98304 | bytes 786624 | tf_op jit(solution)/shard_map/jit(_where)/select_n | solution.py:216
  70.8 5.8 %collective-permute-done.9 = bf16[3,32,1024]{2,1,0:T(8,128)(2,1)S(1)} collective-permute-done((bf16[3,32,1024]{2,1,0:T(8,128)(2,1)S(1)}, bf16[3,32,1024]{2,1,0:T(8,128)(2,1)S(1)}, u32[]{:S(2)}, u32[]{:S(2)}) %collective-permute-start.9) | collective-permute-done | bytes 196640 | tf_op jit(solution)/shard_map/ppermute | solution.py:28
  76.6 0.8 %fusion = f32[3,32,1024]{2,1,0:T(8,128)} fusion(bf16[3,32,1024]{2,1,0:T(8,128)(2,1)S(1)} %collective-permute-done.9, f32[3,2,32,1024]{3,2,0,1:T(8,128)S(1)} %slice_select_fusion, s32[]{:T(128)S(6)} %select_n.45, pred[3,32]{1,0:T(4,128)(4,1)S(1)} %broadcast_compare_fusion.1), kind=kLoop, calls=%fused_computation.5 | loop fusion | flops 294912 | bytes 983140 | tf_op jit(solution)/shard_map/jit(_where)/select_n | solution.py:210
  (37 shorter events, 0.1 us)
Async XLA Ops:
  0.6 1.6 %copy-start.2 = (bf16[1,2048,512]{2,1,0:T(8,128)(2,1)S(1)}, bf16[1,2048,512]{2,1,0:T(8,128)(2,1)}, u32[]{:S(2)}) copy-start(bf16[1,2048,512]{2,1,0:T(8,128)(2,1)} %param.13) | copy-start | bytes 6291460
  2.2 1.1 %copy-start.4 = (bf16[3,64,2048]{2,1,0:T(8,128)(2,1)S(1)}, bf16[3,64,2048]{2,1,0:T(8,128)(2,1)}, u32[]{:S(2)}) copy-start(bf16[3,64,2048]{2,1,0:T(8,128)(2,1)} %param.9) | copy-start | bytes 2359300
  3.4 0.7 copy-start.8
  4.1 0.7 copy-start.10
  4.7 12.3 %copy-start.6 = (bf16[1,512,1024]{2,1,0:T(8,128)(2,1)S(1)}, bf16[1,512,1024]{2,1,0:T(8,128)(2,1)}, u32[]{:S(2)}) copy-start(bf16[1,512,1024]{2,1,0:T(8,128)(2,1)} %param.15) | copy-start | bytes 3145732
  5.6 15.0 %collective-permute-start.2 = (bf16[192,512]{1,0:T(8,128)(2,1)S(1)}, bf16[192,512]{1,0:T(8,128)(2,1)S(1)}, u32[]{:S(2)}, u32[]{:S(2)}) collective-permute-start(bf16[192,512]{1,0:T(8,128)(2,1)S(1)} %get-tuple-element.9.refs_3_), channel_id=1, source_target_pairs={{0,12},{1,13},{2,2},{3,3},{4,8},{5,9},{6,6},{7,7},{8,4},{9,5},{10,... | collective-permute-start | bytes 589832 | tf_op jit(solution)/shard_map/ppermute | solution.py:28
  12.6 9.7 %collective-permute-start.1 = (bf16[192,512]{1,0:T(8,128)(2,1)S(1)}, bf16[192,512]{1,0:T(8,128)(2,1)S(1)}, u32[]{:S(2)}, u32[]{:S(2)}) collective-permute-start(bf16[192,512]{1,0:T(8,128)(2,1)S(1)} %get-tuple-element.9.refs_3_), channel_id=1, source_target_pairs={{0,8},{1,9},{2,2},{3,3},{4,12},{5,13},{6,6},{7,7},{8,0},{9,1},{10,... | collective-permute-start | bytes 589832 | tf_op jit(solution)/shard_map/ppermute | solution.py:28
  14.5 9.6 %collective-permute-start = (bf16[192,512]{1,0:T(8,128)(2,1)S(1)}, bf16[192,512]{1,0:T(8,128)(2,1)S(1)}, u32[]{:S(2)}, u32[]{:S(2)}) collective-permute-start(bf16[192,512]{1,0:T(8,128)(2,1)S(1)} %get-tuple-element.9.refs_3_), channel_id=1, source_target_pairs={{0,4},{1,5},{2,2},{3,3},{4,0},{5,1},{6,6},{7,7},{8,12},{9,13},{10,... | collective-permute-start | bytes 589832 | tf_op jit(solution)/shard_map/ppermute | solution.py:28
  17.0 2.2 %copy-start = (bf16[1,2048,1024]{2,1,0:T(8,128)(2,1)S(1)}, bf16[1,2048,1024]{2,1,0:T(8,128)(2,1)}, u32[]{:S(2)}) copy-start(bf16[1,2048,1024]{2,1,0:T(8,128)(2,1)} %param.12) | copy-start | bytes 12582916
  19.2 5.6 %copy-start.12 = (bf16[1,1024,2048]{2,1,0:T(8,128)(2,1)S(1)}, bf16[1,1024,2048]{2,1,0:T(8,128)(2,1)}, u32[]{:S(2)}) copy-start(bf16[1,1024,2048]{2,1,0:T(8,128)(2,1)} %param.17) | copy-start | bytes 12582916
  19.2 5.6 %copy-start.14 = (bf16[1,512,1024]{2,1,0:T(8,128)(2,1)S(1)}, bf16[1,512,1024]{2,1,0:T(8,128)(2,1)}, u32[]{:S(2)}) copy-start(bf16[1,512,1024]{2,1,0:T(8,128)(2,1)} %param.16) | copy-start | bytes 3145732
  19.2 5.6 %copy-start.22 = (s32[3]{0:T(128)S(1)}, s32[3]{0:T(128)}, u32[]{:S(2)}) copy-start(s32[3]{0:T(128)} %refs_1_.5) | copy-start | bytes 40
  20.6 0.7 copy-start.16
  22.3 0.7 copy-start.18
  24.1 0.7 copy-start.20
  24.8 0.9 %copy-start.17 = (bf16[192,512]{1,0:T(8,128)(2,1)S(1)}, bf16[192,512]{1,0:T(8,128)(2,1)}, u32[]{:S(2)}) copy-start(bf16[192,512]{1,0:T(8,128)(2,1)} %copy-done.16) | copy-start | bytes 589828
  25.7 0.9 %copy-start.19 = (bf16[192,512]{1,0:T(8,128)(2,1)S(1)}, bf16[192,512]{1,0:T(8,128)(2,1)}, u32[]{:S(2)}) copy-start(bf16[192,512]{1,0:T(8,128)(2,1)} %copy-done.18) | copy-start | bytes 589828
  26.6 0.9 %copy-start.21 = (bf16[192,512]{1,0:T(8,128)(2,1)S(1)}, bf16[192,512]{1,0:T(8,128)(2,1)}, u32[]{:S(2)}) copy-start(bf16[192,512]{1,0:T(8,128)(2,1)} %copy-done.20) | copy-start | bytes 589828
  27.6 15.8 %copy-start.3 = (bf16[1,2048,512]{2,1,0:T(8,128)(2,1)S(1)}, bf16[1,2048,512]{2,1,0:T(8,128)(2,1)}, u32[]{:S(2)}) copy-start(bf16[1,2048,512]{2,1,0:T(8,128)(2,1)} %param.13) | copy-start | bytes 6291460
  27.6 15.8 %copy-start.5 = (bf16[3,64,2048]{2,1,0:T(8,128)(2,1)S(1)}, bf16[3,64,2048]{2,1,0:T(8,128)(2,1)}, u32[]{:S(2)}) copy-start(bf16[3,64,2048]{2,1,0:T(8,128)(2,1)} %param.9) | copy-start | bytes 2359300
  27.6 15.8 %copy-start.9 = (f32[1,2048]{1,0:T(1,128)S(1)}, f32[1,2048]{1,0:T(1,128)}, u32[]{:S(2)}) copy-start(f32[1,2048]{1,0:T(1,128)} %refs_3_.3) | copy-start | bytes 24580
  27.6 15.8 %copy-start.11 = (f32[1,512]{1,0:T(1,128)S(1)}, f32[1,512]{1,0:T(1,128)}, u32[]{:S(2)}) copy-start(f32[1,512]{1,0:T(1,128)} %refs_5_.1) | copy-start | bytes 6148
  33.5 9.8 %collective-permute-start.4 = (bf16[192,2048]{1,0:T(8,128)(2,1)}, bf16[192,2048]{1,0:T(8,128)(2,1)}, u32[]{:S(2)}, u32[]{:S(2)}) collective-permute-start(bf16[192,2048]{1,0:T(8,128)(2,1)} %attend0.1), channel_id=1, source_target_pairs={{0,3},{1,2},{2,0},{3,1},{4,7},{5,6},{6,4},{7,5},{8,11},{9,10},{10,... | collective-permute-start | bytes 2359304 | tf_op jit(solution)/shard_map/ppermute | solution.py:28
  33.5 9.8 %collective-permute-start.3 = (bf16[192,2048]{1,0:T(8,128)(2,1)}, bf16[192,2048]{1,0:T(8,128)(2,1)}, u32[]{:S(2)}, u32[]{:S(2)}) collective-permute-start(bf16[192,2048]{1,0:T(8,128)(2,1)} %attend0.1), channel_id=1, source_target_pairs={{0,2},{1,3},{2,0},{3,1},{4,6},{5,7},{6,4},{7,5},{8,10},{9,11},{10,... | collective-permute-start | bytes 2359304 | tf_op jit(solution)/shard_map/ppermute | solution.py:28
  43.4 6.8 %copy-start.1 = (bf16[1,2048,1024]{2,1,0:T(8,128)(2,1)S(1)}, bf16[1,2048,1024]{2,1,0:T(8,128)(2,1)}, u32[]{:S(2)}) copy-start(bf16[1,2048,1024]{2,1,0:T(8,128)(2,1)} %param.12) | copy-start | bytes 12582916
  46.0 4.2 %copy-start.7 = (bf16[1,512,1024]{2,1,0:T(8,128)(2,1)S(1)}, bf16[1,512,1024]{2,1,0:T(8,128)(2,1)}, u32[]{:S(2)}) copy-start(bf16[1,512,1024]{2,1,0:T(8,128)(2,1)} %param.15) | copy-start | bytes 3145732
  46.0 5.6 %collective-permute-start.7 = (bf16[192,512]{1,0:T(8,128)(2,1)S(1)}, bf16[192,512]{1,0:T(8,128)(2,1)S(1)}, u32[]{:S(2)}, u32[]{:S(2)}) collective-permute-start(bf16[192,512]{1,0:T(8,128)(2,1)S(1)} %get-tuple-element.11.refs_3_), channel_id=1, source_target_pairs={{0,0},{1,1},{2,14},{3,15},{4,4},{5,5},{6,10},{7,11},{8,8},{9,9},{1... | collective-permute-start | bytes 589832 | tf_op jit(solution)/shard_map/ppermute | solution.py:28
  46.8 4.8 %collective-permute-start.6 = (bf16[192,512]{1,0:T(8,128)(2,1)S(1)}, bf16[192,512]{1,0:T(8,128)(2,1)S(1)}, u32[]{:S(2)}, u32[]{:S(2)}) collective-permute-start(bf16[192,512]{1,0:T(8,128)(2,1)S(1)} %get-tuple-element.11.refs_3_), channel_id=1, source_target_pairs={{0,0},{1,1},{2,10},{3,11},{4,4},{5,5},{6,14},{7,15},{8,8},{9,9},{1... | collective-permute-start | bytes 589832 | tf_op jit(solution)/shard_map/ppermute | solution.py:28
  47.5 4.1 %collective-permute-start.5 = (bf16[192,512]{1,0:T(8,128)(2,1)S(1)}, bf16[192,512]{1,0:T(8,128)(2,1)S(1)}, u32[]{:S(2)}, u32[]{:S(2)}) collective-permute-start(bf16[192,512]{1,0:T(8,128)(2,1)S(1)} %get-tuple-element.11.refs_3_), channel_id=1, source_target_pairs={{0,0},{1,1},{2,6},{3,7},{4,4},{5,5},{6,2},{7,3},{8,8},{9,9},{10,14... | collective-permute-start | bytes 589832 | tf_op jit(solution)/shard_map/ppermute | solution.py:28
  50.1 2.2 %copy-start.13 = (bf16[1,1024,2048]{2,1,0:T(8,128)(2,1)S(1)}, bf16[1,1024,2048]{2,1,0:T(8,128)(2,1)}, u32[]{:S(2)}) copy-start(bf16[1,1024,2048]{2,1,0:T(8,128)(2,1)} %param.17) | copy-start | bytes 12582916
  50.2 2.5 %copy-start.15 = (bf16[1,512,1024]{2,1,0:T(8,128)(2,1)S(1)}, bf16[1,512,1024]{2,1,0:T(8,128)(2,1)}, u32[]{:S(2)}) copy-start(bf16[1,512,1024]{2,1,0:T(8,128)(2,1)} %param.16) | copy-start | bytes 3145732
  58.1 11.1 %collective-permute-start.8 = (bf16[3,2,32,1024]{3,2,0,1:T(8,128)(2,1)S(1)}, bf16[3,2,32,1024]{3,2,0,1:T(8,128)(2,1)S(1)}, u32[]{:S(2)}, u32[]{:S(2)}) collective-permute-start(bf16[3,2,32,1024]{3,2,0,1:T(8,128)(2,1)S(1)} %slice.13), channel_id=1, source_target_pairs={{0,2},{1,3},{2,0},{3,1},{4,6},{5,7},{6,4},{7,5},{8,10},{9,11},{10,... | collective-permute-start | bytes 1179656 | tf_op jit(solution)/shard_map/ppermute | solution.py:28
  69.4 7.2 %collective-permute-start.9 = (bf16[3,32,1024]{2,1,0:T(8,128)(2,1)S(1)}, bf16[3,32,1024]{2,1,0:T(8,128)(2,1)S(1)}, u32[]{:S(2)}, u32[]{:S(2)}) collective-permute-start(bf16[3,32,1024]{2,1,0:T(8,128)(2,1)S(1)} %fusion.1), channel_id=1, source_target_pairs={{0,1},{1,0},{2,3},{3,2},{4,5},{5,4},{6,7},{7,6},{8,9},{9,8},{10,11... | collective-permute-start | bytes 589832 | tf_op jit(solution)/shard_map/ppermute | solution.py:28

commit v2 on v1

v2 whole, which is shorter than its diff:
```python
import functools

import jax
import jax.numpy as jnp
from jax import lax
from jax.experimental import pallas as pl
from jax.experimental.pallas import tpu as pltpu
from jax.sharding import PartitionSpec as P


HD = 128
AXES = ("seq", "section", "head")
F32 = jnp.float32
BF16 = jnp.bfloat16
VMEM = pl.BlockSpec(memory_space=pltpu.VMEM)
HBM = pl.BlockSpec(memory_space=pltpu.HBM)
SMEM = pl.BlockSpec(memory_space=pltpu.SMEM)
MIB = 1 << 20


def permute(value, sizes, target):
    pairs = []
    for s in range(sizes[0]):
        for c in range(sizes[1]):
            for h in range(sizes[2]):
                ts, tc, th = target(s, c, h)
                at = (s * sizes[1] + c) * sizes[2] + h
                to = (ts * sizes[1] + tc) * sizes[2] + th
                pairs.append((at, to))
    return lax.ppermute(value, AXES, pairs)


def rms(values, gain):
    mean_sq = jnp.mean(values * values, axis=-1, keepdims=True)
    return values * lax.rsqrt(mean_sq + 1e-06) * gain


def dot(a, b, dims=((1,), (0,))):
    return lax.dot_general(a, b, (dims, ((), ())), preferred_element_type=F32)


def tree_sum(terms):
    terms = [t.astype(F32) for t in terms]
    while len(terms) > 1:
        terms = [sum(terms[i : i + 2]) for i in range(0, len(terms), 2)]
    return terms[0]


def masked(values, first, length):
    at = first + lax.broadcasted_iota(jnp.int32, values.shape, 0)
    return jnp.where(at < length, values, 0.0)


def first_latent_body(spans, rows, *refs):
    x_hbm, gain_hbm, w_hbm, lgain_hbm, normed_ref, full_ref = refs[:6]
    latent_refs = refs[6 : 6 + len(spans)]
    x_ref, gain_ref, lgain_ref, w_ref, sems = refs[6 + len(spans) :]
    copies = [
        pltpu.make_async_copy(source, to, sems.at[i])
        for i, (source, to) in enumerate(
            ((x_hbm, x_ref), (gain_hbm, gain_ref), (lgain_hbm, lgain_ref), (w_hbm, w_ref))
        )
    ]
    for copy in copies:
        copy.start()
    copies[0].wait()
    copies[1].wait()
    normed = rms(x_ref[...].astype(F32), gain_ref[...]).astype(BF16)
    normed_ref[...] = normed
    copies[2].wait()
    copies[3].wait()
    full = rms(dot(normed, w_ref[...]), lgain_ref[...])
    full_ref[...] = full
    latent = full.astype(BF16)
    for (low, high), latent_ref in zip(spans, latent_refs):
        latent_ref[...] = latent[low * rows : high * rows]


def next_latent_body(span, rows, n_parts, where_ref, lengths_ref, *refs):
    x_ref = refs[0]
    parts = refs[1 : 1 + n_parts]
    refs = refs[1 + n_parts :]
    gain_ref, w_ref, lgain_ref, before_ref, state_ref, normed_ref, live_ref, latent_ref = refs
    low, high = span
    span_rows = slice(low * rows, high * rows)
    state = x_ref[span_rows].astype(F32) + tree_sum([p[...] for p in parts])
    state_ref[...] = state
    normed = rms(state, gain_ref[...]).astype(BF16)
    normed_ref[...] = normed
    full = rms(dot(normed, w_ref[...]), lgain_ref[...])
    latent_ref[...] = full.astype(BF16)
    second = jnp.broadcast_to(where_ref[1], (rows, full.shape[1])) == 1
    for g in range(low, high):
        at = slice((g - low) * rows, (g - low + 1) * rows)
        mine = jnp.where(second, full[at], before_ref[g * rows : (g + 1) * rows])
        live_ref[at] = masked(mine, where_ref[0] * rows, lengths_ref[g])


def query_body(scale, normed_ref, wq_ref, wk_ref, out_ref):
    heads = out_ref.shape[0]
    query = dot(normed_ref[...], wq_ref[...]).astype(BF16)
    for h in range(heads):
        cols = slice(h * HD, (h + 1) * HD)
        one = dot(query[:, cols], wk_ref[:, cols], ((1,), (1,)))
        out_ref[h] = (one * scale).astype(BF16)


def attention(spans, rows, n_pieces, offset, where_ref, lengths_ref, absorbed_ref, pieces, wv, kv, attn):
    heads = absorbed_ref.shape[0]
    rank = kv.shape[1]
    block = n_pieces * rows
    me = where_ref[0]
    for i, (low, high) in enumerate(spans):
        for g in range(low, high):
            for k in range(n_pieces):
                piece = pieces[i * n_pieces + k]
                kv[pl.ds(g * block + k * rows, rows), :] = piece[pl.ds((g - low) * rows, rows), :]
    col = lax.broadcasted_iota(jnp.int32, (rows, block), 1)
    row = lax.broadcasted_iota(jnp.int32, (rows, block), 0)
    key_pos = jnp.bitwise_xor(me, col // rows) * rows + col % rows
    query_pos = me * rows + row
    causal = key_pos <= query_pos
    low, high = spans[-1]
    for g in range(low, high):
        keys = kv[: (g + 1) * block, :]
        at = g * rows - offset
        absorbed = absorbed_ref[:, at : at + rows, :].reshape(heads * rows, rank)
        scores = dot(absorbed, keys, ((1,), (1,)))
        mask = [key_pos < lengths_ref[b] for b in range(g)] + [causal]
        mask = jnp.concatenate(mask, axis=1)[None]
        scores = scores.reshape(heads, rows, (g + 1) * block)
        scores = jnp.where(mask, scores, -1e30)
        top = jnp.max(scores, axis=2, keepdims=True)
        weights = jnp.where(mask, jnp.exp(scores - top), 0.0)
        total = jnp.sum(weights, axis=2, keepdims=True).reshape(heads * rows, 1)
        rounded = weights.astype(BF16).reshape(heads * rows, (g + 1) * block)
        context = (dot(rounded, keys) / total).astype(BF16)
        at = (g - low) * rows
        for h in range(heads):
            cols = slice(h * HD, (h + 1) * HD)
            one = dot(context[h * rows : (h + 1) * rows], wv[:, cols])
            attn[at : at + rows, cols] = one.astype(BF16)


def attend_body(spans, rows, n_pieces, offset, where_ref, lengths_ref, absorbed_ref, *refs):
    n_in = len(spans) * n_pieces
    pieces = refs[:n_in]
    wv, wo, out_ref, kv, attn = refs[n_in:]
    attention(
        spans, rows, n_pieces, offset, where_ref, lengths_ref, absorbed_ref, pieces, wv, kv, attn
    )
    out_ref[...] = dot(attn[...], wo[...]).astype(BF16)


def attend_last_body(
    spans, rows, n_pieces, offset, n_head, n_sec, where_ref, lengths_ref, absorbed_ref, *refs
):
    n_in = len(spans) * n_pieces
    pieces = refs[:n_in]
    wv, wo, state_ref, keep_ref, give_ref = refs[n_in : n_in + 5]
    sends = refs[n_in + 5 : n_in + 4 + n_head]
    kv, attn, total = refs[n_in + 4 + n_head :]
    attention(
        spans, rows, n_pieces, offset, where_ref, lengths_ref, absorbed_ref, pieces, wv, kv, attn
    )
    total[...] = dot(attn[...], wo[...])
    low, high = spans[-1]
    share = rows // n_head
    width = total.shape[1]
    part = width // n_sec
    for g in range(high - low):
        to = slice(g * share, (g + 1) * share)

        def at(h):
            return pl.ds(pl.multiple_of(g * rows + h * share, share), share)

        own = at(where_ref[2])
        mine = state_ref[own, :] + total[own, :]
        give_ref[to] = mine[:, : width - part].astype(BF16)
        keep_ref[to] = mine[:, width - part :]
        for k in range(1, n_head):
            sends[k - 1][to] = total[at(jnp.bitwise_xor(where_ref[2], k)), :].astype(BF16)


def final_body(spans, rows, n_head, n_sec, where_ref, lengths_ref, *refs):
    out_ref = refs[-1]
    per = 2 + 2 * (n_head - 1)
    share = rows // n_head
    part = out_ref.shape[2]
    first = where_ref[0] * rows + where_ref[2] * share
    for i, (low, high) in enumerate(spans):
        keep, given = refs[i * per : i * per + 2]
        came = refs[i * per + 2 : i * per + 1 + n_head]
        relay = refs[i * per + 1 + n_head : (i + 1) * per]
        last = jnp.broadcast_to(where_ref[1], (share, part)) == n_sec - 1
        for g in range(low, high):
            at = slice((g - low) * share, (g - low + 1) * share)
            here = keep[at]
            there = given[at].astype(F32)
            for k in range(n_head - 1):
                here = here + relay[k][at, (n_sec - 1) * part :].astype(F32)
                there = there + came[k][at, :part].astype(F32)
            out_ref[g] = masked(jnp.where(last, here, there), first, lengths_ref[g])


def in_hbm(value):
    return pltpu.with_memory_space_constraint(value, pltpu.HBM)


def params(limit):
    return pltpu.CompilerParams(vmem_limit_bytes=limit * MIB)


def array(dtype, *shape):
    return jax.ShapeDtypeStruct(shape, dtype)


def cost(flops, moved, exps=0):
    return pl.CostEstimate(flops=flops, bytes_accessed=moved, transcendentals=exps)


def after(value, *others):
    return lax.optimization_barrier((value, *others))[0]


def shards(hidden, lengths, attn_gain, w_query, w_latent, latent_gain, w_key, w_value, w_out):
    n_seq = lax.axis_size("seq")
    n_sec = lax.axis_size("section")
    n_head = lax.axis_size("head")
    assert n_sec == 2
    sizes = (n_seq, n_sec, n_head)
    where = jnp.stack([lax.axis_index(axis) for axis in AXES]).astype(jnp.int32)
    groups, rows, width = hidden.shape
    rank = w_latent.shape[2]
    heads = w_key.shape[2] // HD
    total_rows = groups * rows
    share = rows // n_head
    part_width = width // n_sec
    x = hidden.reshape(total_rows, width)
    wl, wq, wk, wv, wo = w_latent[0], w_query[0], w_key[0], w_value[0], w_out[0]
    cut = max(1, groups - 1)
    spans = [(0, cut), (cut, groups)] if cut < groups else [(0, groups)]
    span_size = [(high - low) * rows for low, high in spans]

    def first_latent():
        out = pl.pallas_call(
            functools.partial(first_latent_body, spans, rows),
            out_shape=(
                array(BF16, total_rows, width),
                array(F32, total_rows, rank),
                *(array(BF16, size, rank) for size in span_size),
            ),
            in_specs=[HBM] * 4,
            out_specs=(VMEM,) * (2 + len(spans)),
            scratch_shapes=[
                pltpu.VMEM((total_rows, width), BF16),
                pltpu.VMEM((1, width), F32),
                pltpu.VMEM((1, rank), F32),
                pltpu.VMEM((width, rank), BF16),
                pltpu.SemaphoreType.DMA((4,)),
            ],
            compiler_params=params(12),
            name="first_latent",
        )(*(in_hbm(value) for value in (x, attn_gain, wl, latent_gain)))
        return out[0], out[1], list(out[2:])

    def next_latent(i, parts, before):
        size = span_size[i]
        return pl.pallas_call(
            functools.partial(next_latent_body, spans[i], rows, len(parts)),
            out_shape=(
                array(F32, size, width),
                array(BF16, size, width),
                array(F32, size, rank),
                array(BF16, size, rank),
            ),
            in_specs=[SMEM] * 2 + [VMEM] * (5 + len(parts)),
            out_specs=(VMEM,) * 4,
            compiler_params=params(8),
            cost_estimate=cost(2 * size * width * rank, 2 * width * (rank + 2 * size)),
        )(where, lengths, x, *parts, attn_gain, wl, latent_gain, before)

    def project(normed):
        size = normed.shape[0]
        return pl.pallas_call(
            functools.partial(query_body, 1.0 / HD**0.5),
            out_shape=array(BF16, heads, size, rank),
            in_specs=[VMEM] * 3,
            out_specs=VMEM,
            compiler_params=params(8),
            cost_estimate=cost(
                2 * size * heads * HD * (width + rank), 2 * heads * HD * (width + rank + size)
            ),
        )(normed, wq, wk)

    def attend(i, absorbed, offset, pieces, state=None):
        which = spans[: i + 1]
        high = spans[i][1]
        size = span_size[i]
        flat = [piece for of_span in pieces[: i + 1] for piece in of_span]
        scratch = [
            pltpu.VMEM((high * n_seq * rows, rank), BF16),
            pltpu.VMEM((size, heads * HD), BF16),
        ]
        common = dict(
            compiler_params=params(20),
            cost_estimate=cost(
                4 * heads * size * high * n_seq * rows * rank,
                2 * heads * HD * (width + rank),
                heads * size * high * n_seq * rows,
            ),
        )
        if state is None:
            return pl.pallas_call(
                functools.partial(attend_body, which, rows, n_seq, offset),
                out_shape=array(BF16, size, width),
                in_specs=[SMEM, SMEM] + [VMEM] * (3 + len(flat)),
                out_specs=VMEM,
                scratch_shapes=scratch,
                **common,
            )(where, lengths, absorbed, *flat, wv, wo)
        small = size // n_head
        return pl.pallas_call(
            functools.partial(attend_last_body, which, rows, n_seq, offset, n_head, n_sec),
            out_shape=(
                array(F32, small, part_width),
                array(BF16, small, width - part_width),
                *(array(BF16, small, width) for _ in range(n_head - 1)),
            ),
            in_specs=[SMEM, SMEM] + [VMEM] * (4 + len(flat)),
            out_specs=(VMEM,) * (1 + n_head),
            scratch_shapes=scratch + [pltpu.VMEM((size, width), F32)],
            **common,
        )(where, lengths, absorbed, *flat, wv, wo, state)

    def swap(value):
        return permute(value, sizes, lambda s, c, h: (s, 1 - c, h))

    def cross(value, source, k):
        return permute(
            value, sizes, lambda s, c, h: (s, 1 - c, h ^ k) if c == source else (s, 1 - c, h)
        )

    def gather(latent, tick):
        there = swap(latent)
        return [latent] + [
            permute(
                there, sizes, lambda s, c, h, k=k: (s, 1 - c, h) if c == tick else (s ^ k, tick, h)
            )
            for k in range(1, n_seq)
        ]

    def hand_on(partial):
        return [swap(partial)] + [cross(partial, 0, k) for k in range(1, n_head)]

    normed, full, latents = first_latent()
    pieces = [gather(latent, 0) for latent in latents]
    absorbed = project(normed)
    parts = [hand_on(attend(i, absorbed, 0, pieces)) for i in range(len(spans))]
    pieces, queries, states, lives = [], [], [], []
    for i in range(len(spans)):
        part = parts[i]
        if i:
            part = [after(p, queries[-1]) for p in part]
        state, normed, stored, latent = next_latent(i, part, full)
        states.append(state)
        lives.append(stored)
        pieces.append(gather(latent, 1))
        queries.append(project(normed))
    ends = []
    for i in range(len(spans)):
        keep, give, *sends = attend(i, queries[i], spans[i][0] * rows, pieces, states[i])
        given = swap(give)
        came = [cross(sends[k - 1], 1, k) for k in range(1, n_head)]
        relay = [swap(one) for one in came]
        ends += [keep, given, *came, *relay]
    final = pl.pallas_call(
        functools.partial(final_body, spans, rows, n_head, n_sec),
        out_shape=array(F32, groups, share, part_width),
        in_specs=[SMEM] * 2 + [VMEM] * len(ends),
        out_specs=VMEM,
        compiler_params=params(12),
        name="final",
    )(where, lengths, *ends)
    stored = jnp.concatenate(lives, 0).reshape(1, groups, rows, rank)
    return (final, stored)


def solution(mesh):
    return jax.shard_map(
        shards,
        mesh=mesh,
        in_specs=(
            P("rep", "seq", None),
            P("rep"),
            P("section", None),
            P("section", None, "head"),
            P("section", None, None),
            P("section", None),
            P("section", None, "head"),
            P("section", None, "head"),
            P("section", "head", None),
        ),
        out_specs=(P("rep", ("seq", "head"), "section"), P("section", "rep", "seq", None)),
        check_vma=False,
    )
```

time: 78 us -> 75.1 us (0.963)
  Pallas kernels: 17.2 us -> 23.5 us
  other arithmetic: 4.14 us -> 0.85 us
  starting transfers between devices: 24.6 us -> 22.5 us
  local copies, waits for them, and re-layouts: 12.2 us -> 10.4 us
  waiting for transfers between devices: 18.4 us -> 16.7 us
    pallas_call x6 -> x11, Pallas kernels: 17.2 us -> 23.5 us  [the longest x2 7.11 us: attend(): pl.pallas_call(functools.partial(attend_body, which, rows, n_seq, offset)...]
    select_n x5 -> x0, other arithmetic: 2.21 us -> none  [the longest x1 0.84 us: shards(): jnp.where(live[..., None], stored.reshape(groups, rows, rank), 0.0)[None]]
    ppermute x10 -> x26, starting transfers between devices: 24.6 us -> 22.5 us  [permute(): return lax.ppermute(value, AXES, pairs)]
    add x3 -> x0, other arithmetic: 1.77 us -> none  [the longest x1 1.77 us: shards(): state = x.astype(F32) + tree_sum(parts)]
    unnamed x46 -> x38, local copies, waits for them, and re-layouts: 12.1 us -> 10.4 us
    ppermute x10 -> x26, waiting for transfers between devices: 18.4 us -> 16.7 us  [permute(): return lax.ppermute(value, AXES, pairs)]
  transfers between devices with their start and end apart: 10 -> 26, of which waited for: 5 -> 12; matrix products, arithmetic and copies ran while one was open for 4% -> 1% of each run, Pallas kernels for 4% -> 19%
where the time goes in v2:
time: 75.1 us; the launch traced here: 74.8 us
  Pallas kernels  23.5 us (31%)
  starting transfers between devices  22.5 us (30%)
  waiting for transfers between devices  16.7 us (22%)
  local copies, waits for them, and re-layouts  10.4 us (14%)
  other arithmetic  0.85 us (1%)
  between operations  0.85 us (1%)
    ppermute x26, starting transfers between devices, permute(): return lax.ppermute(value, AXES, pairs)  22.5 us
    ppermute x26, waiting for transfers between devices, permute(): return lax.ppermute(value, AXES, pairs)  16.7 us
    unnamed x38, local copies, waits for them, and re-layouts  10.4 us
    pallas_call x2, Pallas kernels, attend(): pl.pallas_call(functools.partial(attend_body, which, rows, n_seq, offset)...  7.11 us
    pallas_call x2, Pallas kernels, attend(): pl.pallas_call(functools.partial(attend_last_body, which, rows, n_seq, of...  6.05 us
    pallas_call x3, Pallas kernels, project(): pl.pallas_call(functools.partial(query_body, 1.0 / HD ** 0.5), out_shape=...  3.63 us
    pallas_call x2, Pallas kernels, next_latent(): pl.pallas_call(functools.partial(next_latent_body, spans[i], rows, len(pa...  2.7 us
    pallas_call x1, Pallas kernels, first_latent(): pl.pallas_call(functools.partial(first_latent_body, spans, rows), out_sha...  2.66 us
  transfers between devices with their start and end apart: 26, of which 12 were waited for; matrix products, arithmetic and copies ran while one was open for 1% of the time, Pallas kernels for 19%

profile of v2, /device:TPU:0, one launch (start us, length us, event | category | flops | bytes accessed | tf_op | source)
XLA Modules:
  0.0 74.8 jit_solution(4964700101743872533)
XLA Ops:
  0.6 2.7 %first_latent.1 = (bf16[192,2048]{1,0:T(8,128)(2,1)S(1)}, f32[192,512]{1,0:T(8,128)S(1)}, bf16[128,512]{1,0:T(8,128)(2,1)S(1)}, bf16[64,512]{1,0:T(8,128)(2,1)S(1)}) custom-call(bf16[192,2048]{1,0:T(8,128)(2,1)} %bitcast.27, f32[1,2048]{1,0:T(1,128)} %refs_3_.5, bf16[2048,512]{1,0:T(8,128)(2,1)} %bitcast.17, f32[1,512]{1,0:T(1,128)} %refs_5_.3), custom_call_target="tpu_custom_call" | custom-call | tf_op jit(solution)/shard_map/first_latent/pallas_call | solution.py:246
  3.3 0.6 copy-done.15
  3.9 0.5 collective-permute-start
  4.4 0.7 copy-done.12
  5.1 0.5 collective-permute-done
  5.6 0.4 collective-permute-start.3
  5.9 4.7 %collective-permute-start.2 = (bf16[128,512]{1,0:T(8,128)(2,1)}, bf16[128,512]{1,0:T(8,128)(2,1)}, u32[]{:S(2)}, u32[]{:S(2)}) collective-permute-start(bf16[128,512]{1,0:T(8,128)(2,1)} %collective-permute-done), channel_id=1, source_target_pairs={{0,2},{1,3},{2,8},{3,9},{4,6},{5,7},{6,12},{7,13},{8,10},{9,11},{1... | collective-permute-start | bytes 393224 | tf_op jit(solution)/shard_map/ppermute | solution.py:30
  10.6 2.2 %copy-done.2 = bf16[1,2048,1024]{2,1,0:T(8,128)(2,1)S(1)} copy-done((bf16[1,2048,1024]{2,1,0:T(8,128)(2,1)S(1)}, bf16[1,2048,1024]{2,1,0:T(8,128)(2,1)}, u32[]{:S(2)}) %copy-start.2) | copy-done | bytes 4194328
  12.8 1.2 %copy-done.9 = bf16[1,512,1024]{2,1,0:T(8,128)(2,1)S(1)} copy-done((bf16[1,512,1024]{2,1,0:T(8,128)(2,1)S(1)}, bf16[1,512,1024]{2,1,0:T(8,128)(2,1)}, u32[]{:S(2)}) %copy-start.9) | copy-done | bytes 1048600
  14.0 1.4 %shard_map.104.absorbed_ref = bf16[8,192,512]{2,1,0:T(8,128)(2,1)S(1)} custom-call(bf16[192,2048]{1,0:T(8,128)(2,1)S(1)} %get-tuple-element.22.normed_ref, bf16[2048,1024]{1,0:T(8,128)(2,1)S(1)} %bitcast.14, bf16[512,1024]{1,0:T(8,128)(2,1)S(1)} %bitcast.24), custom_call_target="tpu_custom_call" | custom-call | flops 1006632960 | bytes 5636096 | tf_op jit(solution)/shard_map/pallas_call | solution.py:285
  15.5 1.2 %copy-done.6 = bf16[8,192,512]{2,1,0:T(8,128)(2,1)} copy-done((bf16[8,192,512]{2,1,0:T(8,128)(2,1)}, bf16[8,192,512]{2,1,0:T(8,128)(2,1)S(1)}, u32[]{:S(2)}) %copy-start.6) | copy-done | bytes 1572888
  16.7 0.1 collective-permute-done.2.refs_2_
  16.9 2.2 %copy-done = bf16[1,1024,2048]{2,1,0:T(8,128)(2,1)S(1)} copy-done((bf16[1,1024,2048]{2,1,0:T(8,128)(2,1)S(1)}, bf16[1,1024,2048]{2,1,0:T(8,128)(2,1)}, u32[]{:S(2)}) %copy-start) | copy-done | bytes 4194328
  19.0 1.4 %copy-done.7 = bf16[8,192,512]{2,1,0:T(8,128)(2,1)S(1)} copy-done((bf16[8,192,512]{2,1,0:T(8,128)(2,1)S(1)}, bf16[8,192,512]{2,1,0:T(8,128)(2,1)}, u32[]{:S(2)}) %copy-start.7) | copy-done | bytes 1572888
  20.5 0.9 %copy-done.13 = bf16[128,512]{1,0:T(8,128)(2,1)S(1)} copy-done((bf16[128,512]{1,0:T(8,128)(2,1)S(1)}, bf16[128,512]{1,0:T(8,128)(2,1)}, u32[]{:S(2)}) %copy-start.13) | copy-done | bytes 131096
  21.4 3.8 %shard_map.105 = bf16[128,2048]{1,0:T(8,128)(2,1)S(1)} custom-call(s32[3]{0:T(128)S(1)} %pad_add_fusion.where_ref, s32[3]{0:T(128)S(1)} %copy-done.17, bf16[8,192,512]{2,1,0:T(8,128)(2,1)S(1)} %copy-done.7, bf16[128,512]{1,0:T(8,128)(2,1)S(1)} %copy-done.13, bf16[128,512]{1,0:T(8,128)(2,1)} %collective-permute-done.1.refs_1_, ...), custom_call_target="tpu_custom_call" | custom-call | flops 1073741824 | bytes 5242880 | tf_op jit(solution)/shard_map/pallas_call | solution.py:314
  25.2 1.0 %collective-permute-start.5 = (bf16[128,2048]{1,0:T(8,128)(2,1)S(1)}, bf16[128,2048]{1,0:T(8,128)(2,1)S(1)}, u32[]{:S(2)}, u32[]{:S(2)}) collective-permute-start(bf16[128,2048]{1,0:T(8,128)(2,1)S(1)} %shard_map.105), channel_id=1, source_target_pairs={{0,3},{1,2},{2,0},{3,1},{4,7},{5,6},{6,4},{7,5},{8,11},{9,10},{10,... | collective-permute-start | bytes 1572872 | tf_op jit(solution)/shard_map/ppermute | solution.py:30
  26.2 6.7 %collective-permute-done.5.refs_2_ = bf16[128,2048]{1,0:T(8,128)(2,1)S(1)} collective-permute-done((bf16[128,2048]{1,0:T(8,128)(2,1)S(1)}, bf16[128,2048]{1,0:T(8,128)(2,1)S(1)}, u32[]{:S(2)}, u32[]{:S(2)}) %collective-permute-start.5) | collective-permute-done | bytes 524320 | tf_op jit(solution)/shard_map/ppermute | solution.py:30
  32.9 1.4 %shard_map.106 = (f32[128,2048]{1,0:T(8,128)S(1)}, bf16[128,2048]{1,0:T(8,128)(2,1)S(1)}, f32[128,512]{1,0:T(8,128)S(1)}, bf16[128,512]{1,0:T(8,128)(2,1)S(1)}) custom-call(s32[3]{0:T(128)S(1)} %pad_add_fusion.where_ref, s32[3]{0:T(128)S(1)} %copy-done.17, bf16[192,2048]{1,0:T(8,128)(2,1)S(1)} %bitcast.28, ...), custom_call_target="tpu_custom_call" | custom-call | flops 268435456 | bytes 3145728 | tf_op jit(solution)/shard_map/pallas_call | solution.py:269
  34.4 0.9 %collective-permute-start.6 = (bf16[128,512]{1,0:T(8,128)(2,1)S(1)}, bf16[128,512]{1,0:T(8,128)(2,1)S(1)}, u32[]{:S(2)}, u32[]{:S(2)}) collective-permute-start(bf16[128,512]{1,0:T(8,128)(2,1)S(1)} %get-tuple-element.26.refs_0_), channel_id=1, source_target_pairs={{0,2},{1,3},{2,0},{3,1},{4,6},{5,7},{6,4},{7,5},{8,10},{9,11},{10,... | collective-permute-start | bytes 393224 | tf_op jit(solution)/shard_map/ppermute | solution.py:30
  35.3 0.1 collective-permute-start.13
  35.3 1.2 %collective-permute-done.13 = bf16[64,512]{1,0:T(8,128)(2,1)S(1)} collective-permute-done((bf16[64,512]{1,0:T(8,128)(2,1)S(1)}, bf16[64,512]{1,0:T(8,128)(2,1)S(1)}, u32[]{:S(2)}, u32[]{:S(2)}) %collective-permute-start.13) | collective-permute-done | bytes 65568 | tf_op jit(solution)/shard_map/ppermute | solution.py:30
  36.5 0.2 collective-permute-start.16
  36.7 2.4 %collective-permute-start.15 = (bf16[64,512]{1,0:T(8,128)(2,1)S(1)}, bf16[64,512]{1,0:T(8,128)(2,1)S(1)}, u32[]{:S(2)}, u32[]{:S(2)}) collective-permute-start(bf16[64,512]{1,0:T(8,128)(2,1)S(1)} %collective-permute-done.13), channel_id=1, source_target_pairs={{0,2},{1,3},{2,8},{3,9},{4,6},{5,7},{6,12},{7,13},{8,10},{9,11},{1... | collective-permute-start | bytes 196616 | tf_op jit(solution)/shard_map/ppermute | solution.py:30
  39.1 2.3 %collective-permute-start.9 = (bf16[128,512]{1,0:T(8,128)(2,1)S(1)}, bf16[128,512]{1,0:T(8,128)(2,1)S(1)}, u32[]{:S(2)}, u32[]{:S(2)}) collective-permute-start(bf16[128,512]{1,0:T(8,128)(2,1)S(1)} %collective-permute-done.6), channel_id=1, source_target_pairs={{0,14},{1,15},{2,0},{3,1},{4,10},{5,11},{6,4},{7,5},{8,6},{9,7},{1... | collective-permute-start | bytes 393224 | tf_op jit(solution)/shard_map/ppermute | solution.py:30
  41.4 0.7 collective-permute-done.16.refs_7_
  42.1 1.8 %collective-permute-done.15.refs_6_ = bf16[64,512]{1,0:T(8,128)(2,1)S(1)} collective-permute-done((bf16[64,512]{1,0:T(8,128)(2,1)S(1)}, bf16[64,512]{1,0:T(8,128)(2,1)S(1)}, u32[]{:S(2)}, u32[]{:S(2)}) %collective-permute-start.15) | collective-permute-done | bytes 65568 | tf_op jit(solution)/shard_map/ppermute | solution.py:30
  43.9 3.3 %shard_map.109 = bf16[64,2048]{1,0:T(8,128)(2,1)S(1)} custom-call(s32[3]{0:T(128)S(1)} %pad_add_fusion.where_ref, s32[3]{0:T(128)S(1)} %copy-done.17, bf16[8,192,512]{2,1,0:T(8,128)(2,1)S(1)} %copy-done.8, bf16[128,512]{1,0:T(8,128)(2,1)S(1)} %copy-done.13, bf16[128,512]{1,0:T(8,128)(2,1)} %collective-permute-done.1.refs_1_, ...), custom_call_target="tpu_custom_call" | custom-call | flops 805306368 | bytes 5242880 | tf_op jit(solution)/shard_map/pallas_call | solution.py:314
  47.3 0.5 collective-permute-start.17
  47.8 1.0 %shard_map.107.absorbed_ref = bf16[8,128,512]{2,1,0:T(8,128)(2,1)S(1)} custom-call(bf16[128,2048]{1,0:T(8,128)(2,1)S(1)} %get-tuple-element.25.normed_ref, bf16[2048,1024]{1,0:T(8,128)(2,1)S(1)} %bitcast.15, bf16[512,1024]{1,0:T(8,128)(2,1)S(1)} %bitcast.25), custom_call_target="tpu_custom_call" | custom-call | flops 671088640 | bytes 5505024 | tf_op jit(solution)/shard_map/pallas_call | solution.py:285
  48.8 3.2 %shard_map.108 = (f32[64,1024]{1,0:T(8,128)S(1)}, bf16[64,1024]{1,0:T(8,128)(2,1)S(1)}, bf16[64,2048]{1,0:T(8,128)(2,1)S(1)}) custom-call(s32[3]{0:T(128)S(1)} %pad_add_fusion.where_ref, s32[3]{0:T(128)S(1)} %copy-done.17, bf16[8,128,512]{2,1,0:T(8,128)(2,1)S(1)} %shard_map.107.absorbed_ref, bf16[128,512]{1,0:T(8,128)(2,1)S(1)} %get-tuple-element.26.refs_0_, ...), custom_call_target="tpu_custom_call" | custom-call | flops 1073741824 | bytes 5242880 | tf_op jit(solution)/shard_map/pallas_call | solution.py:323
  52.0 0.7 collective-permute-start.11
  52.7 1.3 %shard_map.110 = (f32[64,2048]{1,0:T(8,128)S(1)}, bf16[64,2048]{1,0:T(8,128)(2,1)S(1)}, f32[64,512]{1,0:T(8,128)S(1)}, bf16[64,512]{1,0:T(8,128)(2,1)S(1)}) custom-call(s32[3]{0:T(128)S(1)} %pad_add_fusion.where_ref, s32[3]{0:T(128)S(1)} %copy-done.17, bf16[192,2048]{1,0:T(8,128)(2,1)S(1)} %bitcast.29, bf16[64,2048]{1,0:T(8,128)(2,1)S(1)} %collective-permute-done.17.refs_1_, ...), custom_call_target="tpu_custom_call" | custom-call | flops 134217728 | bytes 2621440 | tf_op jit(solution)/shard_map/pallas_call | solution.py:269
  54.0 5.0 %collective-permute-start.19 = (bf16[64,512]{1,0:T(8,128)(2,1)S(1)}, bf16[64,512]{1,0:T(8,128)(2,1)S(1)}, u32[]{:S(2)}, u32[]{:S(2)}) collective-permute-start(bf16[64,512]{1,0:T(8,128)(2,1)S(1)} %get-tuple-element.35.refs_4_), channel_id=1, source_target_pairs={{0,2},{1,3},{2,0},{3,1},{4,6},{5,7},{6,4},{7,5},{8,10},{9,11},{10,... | collective-permute-start | bytes 196616 | tf_op jit(solution)/shard_map/ppermute | solution.py:30
  59.0 0.9 %collective-permute-done.19 = bf16[64,512]{1,0:T(8,128)(2,1)S(1)} collective-permute-done((bf16[64,512]{1,0:T(8,128)(2,1)S(1)}, bf16[64,512]{1,0:T(8,128)(2,1)S(1)}, u32[]{:S(2)}, u32[]{:S(2)}) %collective-permute-start.19) | collective-permute-done | bytes 65568 | tf_op jit(solution)/shard_map/ppermute | solution.py:30
  60.0 1.2 %shard_map.111.absorbed_ref = bf16[8,64,512]{2,1,0:T(8,128)(2,1)S(1)} custom-call(bf16[64,2048]{1,0:T(8,128)(2,1)S(1)} %get-tuple-element.34.normed_ref, bf16[2048,1024]{1,0:T(8,128)(2,1)S(1)} %bitcast.16, bf16[512,1024]{1,0:T(8,128)(2,1)S(1)} %bitcast.26), custom_call_target="tpu_custom_call" | custom-call | flops 335544320 | bytes 5373952 | tf_op jit(solution)/shard_map/pallas_call | solution.py:285
  61.2 0.7 collective-permute-done.22.refs_7_
  61.9 0.6 collective-permute-done.21.refs_6_
  62.5 0.7 collective-permute-done.20.refs_5_
  63.1 2.9 %shard_map.112 = (f32[32,1024]{1,0:T(8,128)S(1)}, bf16[32,1024]{1,0:T(8,128)(2,1)S(1)}, bf16[32,2048]{1,0:T(8,128)(2,1)S(1)}) custom-call(s32[3]{0:T(128)S(1)} %pad_add_fusion.where_ref, s32[3]{0:T(128)S(1)} %copy-done.17, bf16[8,64,512]{2,1,0:T(8,128)(2,1)S(1)} %shard_map.111.absorbed_ref, bf16[128,512]{1,0:T(8,128)(2,1)S(1)} %get-tuple-element.26.refs_0_, ...), custom_call_target="tpu_custom_call" | custom-call | flops 805306368 | bytes 5242880 | tf_op jit(solution)/shard_map/pallas_call | solution.py:323
  66.0 2.7 %collective-permute-start.24 = (bf16[32,2048]{1,0:T(8,128)(2,1)S(1)}, bf16[32,2048]{1,0:T(8,128)(2,1)S(1)}, u32[]{:S(2)}, u32[]{:S(2)}) collective-permute-start(bf16[32,2048]{1,0:T(8,128)(2,1)S(1)} %get-tuple-element.39), channel_id=1, source_target_pairs={{0,2},{1,3},{2,1},{3,0},{4,6},{5,7},{6,5},{7,4},{8,10},{9,11},{10,... | collective-permute-start | bytes 393224 | tf_op jit(solution)/shard_map/ppermute | solution.py:30
  68.7 0.1 collective-permute-start.12
  68.8 0.4 collective-permute-start.10
  69.2 2.7 %collective-permute-done.24.refs_6_ = bf16[32,2048]{1,0:T(8,128)(2,1)S(1)} collective-permute-done((bf16[32,2048]{1,0:T(8,128)(2,1)S(1)}, bf16[32,2048]{1,0:T(8,128)(2,1)S(1)}, u32[]{:S(2)}, u32[]{:S(2)}) %collective-permute-start.24) | collective-permute-done | bytes 131104 | tf_op jit(solution)/shard_map/ppermute | solution.py:30
  72.0 0.5 collective-permute-start.23
  72.5 0.8 %pad_maximum_fusion = f32[192,512]{1,0:T(8,128)} fusion(f32[64,512]{1,0:T(8,128)S(1)} %get-tuple-element.41, f32[128,512]{1,0:T(8,128)S(1)} %get-tuple-element.40), kind=kLoop, calls=%fused_computation | loop fusion | flops 98304 | bytes 786432 | tf_op jit(solution)/shard_map/concatenate | solution.py:385
  73.2 0.2 collective-permute-done.23.refs_5_
  73.4 1.4 %final.1 = f32[3,32,1024]{2,1,0:T(8,128)} custom-call(s32[3]{0:T(128)S(1)} %pad_add_fusion.where_ref, s32[3]{0:T(128)S(1)} %copy-done.17, f32[64,1024]{1,0:T(8,128)S(1)} %get-tuple-element.28.refs_0_, bf16[64,1024]{1,0:T(8,128)(2,1)S(1)} %collective-permute-done.10.refs_1_, bf16[64,2048]{1,0:T(8,128)(2,1)S(1)} %collective-permute-done.11.refs_2_, ...), custom_call_target="tpu_custom_call" | custom-call | tf_op jit(solution)/shard_map/final/pallas_call | solution.py:377
  (55 shorter events, 0.3 us)
Async XLA Ops:
  0.6 16.2 %copy-start.5 = (bf16[1,512,1024]{2,1,0:T(8,128)(2,1)S(1)}, bf16[1,512,1024]{2,1,0:T(8,128)(2,1)}, u32[]{:S(2)}) copy-start(bf16[1,512,1024]{2,1,0:T(8,128)(2,1)} %param.16) | copy-start | bytes 3145732
  3.3 0.6 copy-start.15
  3.9 12.9 %copy-start.17 = (s32[3]{0:T(128)S(1)}, s32[3]{0:T(128)}, u32[]{:S(2)}) copy-start(s32[3]{0:T(128)} %lengths_ref.13) | copy-start | bytes 40
  3.9 1.6 %collective-permute-start = (bf16[128,512]{1,0:T(8,128)(2,1)S(1)}, bf16[128,512]{1,0:T(8,128)(2,1)}, u32[]{:S(2)}, u32[]{:S(2)}) collective-permute-start(bf16[128,512]{1,0:T(8,128)(2,1)S(1)} %get-tuple-element.23.refs_0_), channel_id=1, source_target_pairs={{0,2},{1,3},{2,0},{3,1},{4,6},{5,7},{6,4},{7,5},{8,10},{9,11},{10,... | collective-permute-start | bytes 393224 | tf_op jit(solution)/shard_map/ppermute | solution.py:30
  4.4 0.7 copy-start.12
  5.6 11.2 %collective-permute-start.3 = (bf16[128,512]{1,0:T(8,128)(2,1)}, bf16[128,512]{1,0:T(8,128)(2,1)}, u32[]{:S(2)}, u32[]{:S(2)}) collective-permute-start(bf16[128,512]{1,0:T(8,128)(2,1)} %collective-permute-done), channel_id=1, source_target_pairs={{0,2},{1,3},{2,12},{3,13},{4,6},{5,7},{6,8},{7,9},{8,10},{9,11},{1... | collective-permute-start | bytes 393224 | tf_op jit(solution)/shard_map/ppermute | solution.py:30
  5.9 10.9 %collective-permute-start.2 = (bf16[128,512]{1,0:T(8,128)(2,1)}, bf16[128,512]{1,0:T(8,128)(2,1)}, u32[]{:S(2)}, u32[]{:S(2)}) collective-permute-start(bf16[128,512]{1,0:T(8,128)(2,1)} %collective-permute-done), channel_id=1, source_target_pairs={{0,2},{1,3},{2,8},{3,9},{4,6},{5,7},{6,12},{7,13},{8,10},{9,11},{1... | collective-permute-start | bytes 393224 | tf_op jit(solution)/shard_map/ppermute | solution.py:30
  10.6 6.2 %collective-permute-start.1 = (bf16[128,512]{1,0:T(8,128)(2,1)}, bf16[128,512]{1,0:T(8,128)(2,1)}, u32[]{:S(2)}, u32[]{:S(2)}) collective-permute-start(bf16[128,512]{1,0:T(8,128)(2,1)} %collective-permute-done), channel_id=1, source_target_pairs={{0,2},{1,3},{2,4},{3,5},{4,6},{5,7},{6,0},{7,1},{8,10},{9,11},{10,... | collective-permute-start | bytes 393224 | tf_op jit(solution)/shard_map/ppermute | solution.py:30
  10.6 2.2 %copy-start.2 = (bf16[1,2048,1024]{2,1,0:T(8,128)(2,1)S(1)}, bf16[1,2048,1024]{2,1,0:T(8,128)(2,1)}, u32[]{:S(2)}) copy-start(bf16[1,2048,1024]{2,1,0:T(8,128)(2,1)} %param.12) | copy-start | bytes 12582916
  12.8 1.2 %copy-start.9 = (bf16[1,512,1024]{2,1,0:T(8,128)(2,1)S(1)}, bf16[1,512,1024]{2,1,0:T(8,128)(2,1)}, u32[]{:S(2)}) copy-start(bf16[1,512,1024]{2,1,0:T(8,128)(2,1)} %param.15) | copy-start | bytes 3145732
  14.0 18.9 %copy-start.4 = (bf16[1,2048,512]{2,1,0:T(8,128)(2,1)S(1)}, bf16[1,2048,512]{2,1,0:T(8,128)(2,1)}, u32[]{:S(2)}) copy-start(bf16[1,2048,512]{2,1,0:T(8,128)(2,1)} %param.13) | copy-start | bytes 6291460
  15.4 1.2 %copy-start.6 = (bf16[8,192,512]{2,1,0:T(8,128)(2,1)}, bf16[8,192,512]{2,1,0:T(8,128)(2,1)S(1)}, u32[]{:S(2)}) copy-start(bf16[8,192,512]{2,1,0:T(8,128)(2,1)S(1)} %shard_map.104.absorbed_ref) | copy-start | bytes 4718596
  16.6 16.3 %copy-start.14 = (f32[1,2048]{1,0:T(1,128)S(1)}, f32[1,2048]{1,0:T(1,128)}, u32[]{:S(2)}) copy-start(f32[1,2048]{1,0:T(1,128)} %refs_3_.5) | copy-start | bytes 24580
  16.6 16.3 %copy-start.18 = (f32[1,512]{1,0:T(1,128)S(1)}, f32[1,512]{1,0:T(1,128)}, u32[]{:S(2)}) copy-start(f32[1,512]{1,0:T(1,128)} %refs_5_.3) | copy-start | bytes 6148
  16.9 2.2 %copy-start = (bf16[1,1024,2048]{2,1,0:T(8,128)(2,1)S(1)}, bf16[1,1024,2048]{2,1,0:T(8,128)(2,1)}, u32[]{:S(2)}) copy-start(bf16[1,1024,2048]{2,1,0:T(8,128)(2,1)} %param.17) | copy-start | bytes 12582916
  19.0 1.4 %copy-start.7 = (bf16[8,192,512]{2,1,0:T(8,128)(2,1)S(1)}, bf16[8,192,512]{2,1,0:T(8,128)(2,1)}, u32[]{:S(2)}) copy-start(bf16[8,192,512]{2,1,0:T(8,128)(2,1)} %copy-done.6) | copy-start | bytes 4718596
  20.4 0.9 %copy-start.13 = (bf16[128,512]{1,0:T(8,128)(2,1)S(1)}, bf16[128,512]{1,0:T(8,128)(2,1)}, u32[]{:S(2)}) copy-start(bf16[128,512]{1,0:T(8,128)(2,1)} %copy-done.12) | copy-start | bytes 393220
  21.4 11.6 %copy-start.11 = (bf16[3,64,2048]{2,1,0:T(8,128)(2,1)S(1)}, bf16[3,64,2048]{2,1,0:T(8,128)(2,1)}, u32[]{:S(2)}) copy-start(bf16[3,64,2048]{2,1,0:T(8,128)(2,1)} %param.9) | copy-start | bytes 2359300
  21.4 13.9 %copy-start.16 = (bf16[64,512]{1,0:T(8,128)(2,1)S(1)}, bf16[64,512]{1,0:T(8,128)(2,1)}, u32[]{:S(2)}) copy-start(bf16[64,512]{1,0:T(8,128)(2,1)} %copy-done.15) | copy-start | bytes 196612
  21.4 22.5 %copy-start.1 = (bf16[1,1024,2048]{2,1,0:T(8,128)(2,1)S(1)}, bf16[1,1024,2048]{2,1,0:T(8,128)(2,1)}, u32[]{:S(2)}) copy-start(bf16[1,1024,2048]{2,1,0:T(8,128)(2,1)} %param.17) | copy-start | bytes 12582916
  21.4 22.5 %copy-start.8 = (bf16[8,192,512]{2,1,0:T(8,128)(2,1)S(1)}, bf16[8,192,512]{2,1,0:T(8,128)(2,1)}, u32[]{:S(2)}) copy-start(bf16[8,192,512]{2,1,0:T(8,128)(2,1)} %copy-done.6) | copy-start | bytes 4718596
  25.2 7.7 %collective-permute-start.5 = (bf16[128,2048]{1,0:T(8,128)(2,1)S(1)}, bf16[128,2048]{1,0:T(8,128)(2,1)S(1)}, u32[]{:S(2)}, u32[]{:S(2)}) collective-permute-start(bf16[128,2048]{1,0:T(8,128)(2,1)S(1)} %shard_map.105), channel_id=1, source_target_pairs={{0,3},{1,2},{2,0},{3,1},{4,7},{5,6},{6,4},{7,5},{8,11},{9,10},{10,... | collective-permute-start | bytes 1572872 | tf_op jit(solution)/shard_map/ppermute | solution.py:30
  26.2 6.7 %collective-permute-start.4 = (bf16[128,2048]{1,0:T(8,128)(2,1)S(1)}, bf16[128,2048]{1,0:T(8,128)(2,1)S(1)}, u32[]{:S(2)}, u32[]{:S(2)}) collective-permute-start(bf16[128,2048]{1,0:T(8,128)(2,1)S(1)} %shard_map.105), channel_id=1, source_target_pairs={{0,2},{1,3},{2,0},{3,1},{4,6},{5,7},{6,4},{7,5},{8,10},{9,11},{10,... | collective-permute-start | bytes 1572872 | tf_op jit(solution)/shard_map/ppermute | solution.py:30
  34.3 13.4 %copy-start.3 = (bf16[1,2048,1024]{2,1,0:T(8,128)(2,1)S(1)}, bf16[1,2048,1024]{2,1,0:T(8,128)(2,1)}, u32[]{:S(2)}) copy-start(bf16[1,2048,1024]{2,1,0:T(8,128)(2,1)} %param.12) | copy-start | bytes 12582916
  34.4 13.4 %copy-start.10 = (bf16[1,512,1024]{2,1,0:T(8,128)(2,1)S(1)}, bf16[1,512,1024]{2,1,0:T(8,128)(2,1)}, u32[]{:S(2)}) copy-start(bf16[1,512,1024]{2,1,0:T(8,128)(2,1)} %param.15) | copy-start | bytes 3145732
  34.4 4.8 %collective-permute-start.6 = (bf16[128,512]{1,0:T(8,128)(2,1)S(1)}, bf16[128,512]{1,0:T(8,128)(2,1)S(1)}, u32[]{:S(2)}, u32[]{:S(2)}) collective-permute-start(bf16[128,512]{1,0:T(8,128)(2,1)S(1)} %get-tuple-element.26.refs_0_), channel_id=1, source_target_pairs={{0,2},{1,3},{2,0},{3,1},{4,6},{5,7},{6,4},{7,5},{8,10},{9,11},{10,... | collective-permute-start | bytes 393224 | tf_op jit(solution)/shard_map/ppermute | solution.py:30
  35.3 1.3 %collective-permute-start.13 = (bf16[64,512]{1,0:T(8,128)(2,1)S(1)}, bf16[64,512]{1,0:T(8,128)(2,1)S(1)}, u32[]{:S(2)}, u32[]{:S(2)}) collective-permute-start(bf16[64,512]{1,0:T(8,128)(2,1)S(1)} %copy-done.16), channel_id=1, source_target_pairs={{0,2},{1,3},{2,0},{3,1},{4,6},{5,7},{6,4},{7,5},{8,10},{9,11},{10,... | collective-permute-start | bytes 196616 | tf_op jit(solution)/shard_map/ppermute | solution.py:30
  36.5 5.6 %collective-permute-start.16 = (bf16[64,512]{1,0:T(8,128)(2,1)S(1)}, bf16[64,512]{1,0:T(8,128)(2,1)S(1)}, u32[]{:S(2)}, u32[]{:S(2)}) collective-permute-start(bf16[64,512]{1,0:T(8,128)(2,1)S(1)} %collective-permute-done.13), channel_id=1, source_target_pairs={{0,2},{1,3},{2,12},{3,13},{4,6},{5,7},{6,8},{7,9},{8,10},{9,11},{1... | collective-permute-start | bytes 196616 | tf_op jit(solution)/shard_map/ppermute | solution.py:30
  36.7 7.2 %collective-permute-start.15 = (bf16[64,512]{1,0:T(8,128)(2,1)S(1)}, bf16[64,512]{1,0:T(8,128)(2,1)S(1)}, u32[]{:S(2)}, u32[]{:S(2)}) collective-permute-start(bf16[64,512]{1,0:T(8,128)(2,1)S(1)} %collective-permute-done.13), channel_id=1, source_target_pairs={{0,2},{1,3},{2,8},{3,9},{4,6},{5,7},{6,12},{7,13},{8,10},{9,11},{1... | collective-permute-start | bytes 196616 | tf_op jit(solution)/shard_map/ppermute | solution.py:30
  39.1 4.8 %collective-permute-start.14 = (bf16[64,512]{1,0:T(8,128)(2,1)S(1)}, bf16[64,512]{1,0:T(8,128)(2,1)S(1)}, u32[]{:S(2)}, u32[]{:S(2)}) collective-permute-start(bf16[64,512]{1,0:T(8,128)(2,1)S(1)} %collective-permute-done.13), channel_id=1, source_target_pairs={{0,2},{1,3},{2,4},{3,5},{4,6},{5,7},{6,0},{7,1},{8,10},{9,11},{10,... | collective-permute-start | bytes 196616 | tf_op jit(solution)/shard_map/ppermute | solution.py:30
  39.1 9.7 %collective-permute-start.9 = (bf16[128,512]{1,0:T(8,128)(2,1)S(1)}, bf16[128,512]{1,0:T(8,128)(2,1)S(1)}, u32[]{:S(2)}, u32[]{:S(2)}) collective-permute-start(bf16[128,512]{1,0:T(8,128)(2,1)S(1)} %collective-permute-done.6), channel_id=1, source_target_pairs={{0,14},{1,15},{2,0},{3,1},{4,10},{5,11},{6,4},{7,5},{8,6},{9,7},{1... | collective-permute-start | bytes 393224 | tf_op jit(solution)/shard_map/ppermute | solution.py:30
  41.4 7.4 %collective-permute-start.8 = (bf16[128,512]{1,0:T(8,128)(2,1)S(1)}, bf16[128,512]{1,0:T(8,128)(2,1)S(1)}, u32[]{:S(2)}, u32[]{:S(2)}) collective-permute-start(bf16[128,512]{1,0:T(8,128)(2,1)S(1)} %collective-permute-done.6), channel_id=1, source_target_pairs={{0,10},{1,11},{2,0},{3,1},{4,14},{5,15},{6,4},{7,5},{8,2},{9,3},{1... | collective-permute-start | bytes 393224 | tf_op jit(solution)/shard_map/ppermute | solution.py:30
  42.1 6.7 %collective-permute-start.7 = (bf16[128,512]{1,0:T(8,128)(2,1)S(1)}, bf16[128,512]{1,0:T(8,128)(2,1)S(1)}, u32[]{:S(2)}, u32[]{:S(2)}) collective-permute-start(bf16[128,512]{1,0:T(8,128)(2,1)S(1)} %collective-permute-done.6), channel_id=1, source_target_pairs={{0,6},{1,7},{2,0},{3,1},{4,2},{5,3},{6,4},{7,5},{8,14},{9,15},{10,... | collective-permute-start | bytes 393224 | tf_op jit(solution)/shard_map/ppermute | solution.py:30
  47.2 5.5 %collective-permute-start.18 = (bf16[64,2048]{1,0:T(8,128)(2,1)S(1)}, bf16[64,2048]{1,0:T(8,128)(2,1)S(1)}, u32[]{:S(2)}, u32[]{:S(2)}) collective-permute-start(bf16[64,2048]{1,0:T(8,128)(2,1)S(1)} %shard_map.109), channel_id=1, source_target_pairs={{0,3},{1,2},{2,0},{3,1},{4,7},{5,6},{6,4},{7,5},{8,11},{9,10},{10,... | collective-permute-start | bytes 786440 | tf_op jit(solution)/shard_map/ppermute | solution.py:30
  47.3 5.5 %collective-permute-start.17 = (bf16[64,2048]{1,0:T(8,128)(2,1)S(1)}, bf16[64,2048]{1,0:T(8,128)(2,1)S(1)}, u32[]{:S(2)}, u32[]{:S(2)}) collective-permute-start(bf16[64,2048]{1,0:T(8,128)(2,1)S(1)} %shard_map.109), channel_id=1, source_target_pairs={{0,2},{1,3},{2,0},{3,1},{4,6},{5,7},{6,4},{7,5},{8,10},{9,11},{10,... | collective-permute-start | bytes 786440 | tf_op jit(solution)/shard_map/ppermute | solution.py:30
  52.0 16.7 %collective-permute-start.11 = (bf16[64,2048]{1,0:T(8,128)(2,1)S(1)}, bf16[64,2048]{1,0:T(8,128)(2,1)S(1)}, u32[]{:S(2)}, u32[]{:S(2)}) collective-permute-start(bf16[64,2048]{1,0:T(8,128)(2,1)S(1)} %get-tuple-element.30), channel_id=1, source_target_pairs={{0,2},{1,3},{2,1},{3,0},{4,6},{5,7},{6,5},{7,4},{8,10},{9,11},{10,... | collective-permute-start | bytes 786440 | tf_op jit(solution)/shard_map/ppermute | solution.py:30
  54.0 5.9 %collective-permute-start.19 = (bf16[64,512]{1,0:T(8,128)(2,1)S(1)}, bf16[64,512]{1,0:T(8,128)(2,1)S(1)}, u32[]{:S(2)}, u32[]{:S(2)}) collective-permute-start(bf16[64,512]{1,0:T(8,128)(2,1)S(1)} %get-tuple-element.35.refs_4_), channel_id=1, source_target_pairs={{0,2},{1,3},{2,0},{3,1},{4,6},{5,7},{6,4},{7,5},{8,10},{9,11},{10,... | collective-permute-start | bytes 196616 | tf_op jit(solution)/shard_map/ppermute | solution.py:30
  59.9 1.9 %collective-permute-start.22 = (bf16[64,512]{1,0:T(8,128)(2,1)S(1)}, bf16[64,512]{1,0:T(8,128)(2,1)S(1)}, u32[]{:S(2)}, u32[]{:S(2)}) collective-permute-start(bf16[64,512]{1,0:T(8,128)(2,1)S(1)} %collective-permute-done.19), channel_id=1, source_target_pairs={{0,14},{1,15},{2,0},{3,1},{4,10},{5,11},{6,4},{7,5},{8,6},{9,7},{1... | collective-permute-start | bytes 196616 | tf_op jit(solution)/shard_map/ppermute | solution.py:30
  59.9 2.5 %collective-permute-start.21 = (bf16[64,512]{1,0:T(8,128)(2,1)S(1)}, bf16[64,512]{1,0:T(8,128)(2,1)S(1)}, u32[]{:S(2)}, u32[]{:S(2)}) collective-permute-start(bf16[64,512]{1,0:T(8,128)(2,1)S(1)} %collective-permute-done.19), channel_id=1, source_target_pairs={{0,10},{1,11},{2,0},{3,1},{4,14},{5,15},{6,4},{7,5},{8,2},{9,3},{1... | collective-permute-start | bytes 196616 | tf_op jit(solution)/shard_map/ppermute | solution.py:30
  59.9 3.2 %collective-permute-start.20 = (bf16[64,512]{1,0:T(8,128)(2,1)S(1)}, bf16[64,512]{1,0:T(8,128)(2,1)S(1)}, u32[]{:S(2)}, u32[]{:S(2)}) collective-permute-start(bf16[64,512]{1,0:T(8,128)(2,1)S(1)} %collective-permute-done.19), channel_id=1, source_target_pairs={{0,6},{1,7},{2,0},{3,1},{4,2},{5,3},{6,4},{7,5},{8,14},{9,15},{10,... | collective-permute-start | bytes 196616 | tf_op jit(solution)/shard_map/ppermute | solution.py:30
  66.0 5.9 %collective-permute-start.24 = (bf16[32,2048]{1,0:T(8,128)(2,1)S(1)}, bf16[32,2048]{1,0:T(8,128)(2,1)S(1)}, u32[]{:S(2)}, u32[]{:S(2)}) collective-permute-start(bf16[32,2048]{1,0:T(8,128)(2,1)S(1)} %get-tuple-element.39), channel_id=1, source_target_pairs={{0,2},{1,3},{2,1},{3,0},{4,6},{5,7},{6,5},{7,4},{8,10},{9,11},{10,... | collective-permute-start | bytes 393224 | tf_op jit(solution)/shard_map/ppermute | solution.py:30
  68.7 4.7 %collective-permute-start.12 = (bf16[64,2048]{1,0:T(8,128)(2,1)S(1)}, bf16[64,2048]{1,0:T(8,128)(2,1)S(1)}, u32[]{:S(2)}, u32[]{:S(2)}) collective-permute-start(bf16[64,2048]{1,0:T(8,128)(2,1)S(1)} %collective-permute-done.11.refs_2_), channel_id=1, source_target_pairs={{0,2},{1,3},{2,0},{3,1},{4,6},{5,7},{6,4},{7,5},{8,10},{9,11},{10,... | collective-permute-start | bytes 786440 | tf_op jit(solution)/shard_map/ppermute | solution.py:30
  68.8 4.6 %collective-permute-start.10 = (bf16[64,1024]{1,0:T(8,128)(2,1)S(1)}, bf16[64,1024]{1,0:T(8,128)(2,1)S(1)}, u32[]{:S(2)}, u32[]{:S(2)}) collective-permute-start(bf16[64,1024]{1,0:T(8,128)(2,1)S(1)} %get-tuple-element.29), channel_id=1, source_target_pairs={{0,2},{1,3},{2,0},{3,1},{4,6},{5,7},{6,4},{7,5},{8,10},{9,11},{10,... | collective-permute-start | bytes 393224 | tf_op jit(solution)/shard_map/ppermute | solution.py:30
  72.0 1.4 %collective-permute-start.25 = (bf16[32,2048]{1,0:T(8,128)(2,1)S(1)}, bf16[32,2048]{1,0:T(8,128)(2,1)S(1)}, u32[]{:S(2)}, u32[]{:S(2)}) collective-permute-start(bf16[32,2048]{1,0:T(8,128)(2,1)S(1)} %collective-permute-done.24.refs_6_), channel_id=1, source_target_pairs={{0,2},{1,3},{2,0},{3,1},{4,6},{5,7},{6,4},{7,5},{8,10},{9,11},{10,... | collective-permute-start | bytes 393224 | tf_op jit(solution)/shard_map/ppermute | solution.py:30
  72.0 1.4 %collective-permute-start.23 = (bf16[32,1024]{1,0:T(8,128)(2,1)S(1)}, bf16[32,1024]{1,0:T(8,128)(2,1)S(1)}, u32[]{:S(2)}, u32[]{:S(2)}) collective-permute-start(bf16[32,1024]{1,0:T(8,128)(2,1)S(1)} %get-tuple-element.38), channel_id=1, source_target_pairs={{0,2},{1,3},{2,0},{3,1},{4,6},{5,7},{6,4},{7,5},{8,10},{9,11},{10,... | collective-permute-start | bytes 196616 | tf_op jit(solution)/shard_map/ppermute | solution.py:30

commit v3 on v2

--- a/solution.py
+++ b/solution.py
@@ -46,21 +46,52 @@
     return terms[0]
 
 
-def masked(values, first, length):
-    at = first + lax.broadcasted_iota(jnp.int32, values.shape, 0)
-    return jnp.where(at < length, values, 0.0)
-
-
-def first_latent_body(spans, rows, *refs):
+def place(axis):
+    return lax.axis_index(axis).astype(jnp.int32)
+
+
+def alive(at, length):
+    return jnp.where(at < length, 1.0, 0.0)
+
+
+def prepare_body(rows, n_pieces, lengths_ref, bias_ref, live_ref, final_ref):
+    groups = lengths_ref.shape[0]
+    block = n_pieces * rows
+    me = place("seq")
+    col = lax.broadcasted_iota(jnp.int32, (rows, block), 1)
+    row = lax.broadcasted_iota(jnp.int32, (rows, block), 0)
+    key_pos = jnp.bitwise_xor(me, col // rows) * rows + col % rows
+    for g in range(groups):
+        bias_ref[:, g * block : (g + 1) * block] = jnp.where(key_pos < lengths_ref[g], 0.0, -1e30)
+    bias_ref[:, groups * block :] = jnp.where(key_pos <= me * rows + row, 0.0, -1e30)
+    share = final_ref.shape[0] // groups
+    lanes = live_ref.shape[1]
+    at = me * rows + lax.broadcasted_iota(jnp.int32, (rows, lanes), 0)
+    shared_at = me * rows + place("head") * share
+    shared_at = shared_at + lax.broadcasted_iota(jnp.int32, (share, lanes), 0)
+    for g in range(groups):
+        live_ref[g * rows : (g + 1) * rows] = alive(at, lengths_ref[g])
+        final_ref[g * share : (g + 1) * share] = alive(shared_at, lengths_ref[g])
+
+
+def keep_live(values, live):
+    return jnp.where(live[:, :1] > 0.5, values, 0.0)
+
+
+def first_latent_body(spans, rows, cuts, *refs):
     x_hbm, gain_hbm, w_hbm, lgain_hbm, normed_ref, full_ref = refs[:6]
     latent_refs = refs[6 : 6 + len(spans)]
     x_ref, gain_ref, lgain_ref, w_ref, sems = refs[6 + len(spans) :]
     copies = [
         pltpu.make_async_copy(source, to, sems.at[i])
         for i, (source, to) in enumerate(
-            ((x_hbm, x_ref), (gain_hbm, gain_ref), (lgain_hbm, lgain_ref), (w_hbm, w_ref))
+            ((x_hbm, x_ref), (gain_hbm, gain_ref), (lgain_hbm, lgain_ref))
         )
     ]
+    depth = w_ref.shape[0] // cuts
+    tiles = [slice(i * depth, (i + 1) * depth) for i in range(cuts)]
+    for i, tile in enumerate(tiles):
+        copies.append(pltpu.make_async_copy(w_hbm.at[tile], w_ref.at[tile], sems.at[3 + i]))
     for copy in copies:
         copy.start()
     copies[0].wait()
@@ -68,131 +99,138 @@
     normed = rms(x_ref[...].astype(F32), gain_ref[...]).astype(BF16)
     normed_ref[...] = normed
     copies[2].wait()
-    copies[3].wait()
-    full = rms(dot(normed, w_ref[...]), lgain_ref[...])
+    raw = None
+    for i, tile in enumerate(tiles):
+        copies[3 + i].wait()
+        one = dot(normed[:, tile], w_ref[tile])
+        raw = one if raw is None else raw + one
+    full = rms(raw, lgain_ref[...])
     full_ref[...] = full
     latent = full.astype(BF16)
     for (low, high), latent_ref in zip(spans, latent_refs):
         latent_ref[...] = latent[low * rows : high * rows]
 
 
-def next_latent_body(span, rows, n_parts, where_ref, lengths_ref, *refs):
+def next_latent_body(span, rows, n_parts, *refs):
     x_ref = refs[0]
     parts = refs[1 : 1 + n_parts]
     refs = refs[1 + n_parts :]
-    gain_ref, w_ref, lgain_ref, before_ref, state_ref, normed_ref, live_ref, latent_ref = refs
-    low, high = span
-    span_rows = slice(low * rows, high * rows)
-    state = x_ref[span_rows].astype(F32) + tree_sum([p[...] for p in parts])
+    gain_ref, w_ref, lgain_ref, before_ref, live_ref = refs[:5]
+    state_ref, normed_ref, stored_ref, latent_ref = refs[5:]
+    at = slice(span[0] * rows, span[1] * rows)
+    state = x_ref[at].astype(F32) + tree_sum([p[...] for p in parts])
     state_ref[...] = state
     normed = rms(state, gain_ref[...]).astype(BF16)
     normed_ref[...] = normed
     full = rms(dot(normed, w_ref[...]), lgain_ref[...])
     latent_ref[...] = full.astype(BF16)
-    second = jnp.broadcast_to(where_ref[1], (rows, full.shape[1])) == 1
-    for g in range(low, high):
-        at = slice((g - low) * rows, (g - low + 1) * rows)
-        mine = jnp.where(second, full[at], before_ref[g * rows : (g + 1) * rows])
-        live_ref[at] = masked(mine, where_ref[0] * rows, lengths_ref[g])
+    second = jnp.broadcast_to(place("section"), full.shape) == 1
+    stored_ref[...] = keep_live(jnp.where(second, full, before_ref[at]), live_ref[at])
+
+
+def absorb(scale, query, wk, out_ref):
+    for h in range(out_ref.shape[0]):
+        cols = slice(h * HD, (h + 1) * HD)
+        one = dot(query[:, cols], wk[:, cols], ((1,), (1,)))
+        out_ref[h] = (one * scale).astype(BF16)
+
+
+def first_query_body(scale, cuts, normed_ref, wq_hbm, wk_hbm, out_ref, wq, wk, sems):
+    depth = wq.shape[0] // cuts
+    tiles = [slice(i * depth, (i + 1) * depth) for i in range(cuts)]
+    copies = [
+        pltpu.make_async_copy(wq_hbm.at[tile], wq.at[tile], sems.at[i])
+        for i, tile in enumerate(tiles)
+    ]
+    copies.append(pltpu.make_async_copy(wk_hbm, wk, sems.at[cuts]))
+    for copy in copies:
+        copy.start()
+    query = None
+    for i, tile in enumerate(tiles):
+        copies[i].wait()
+        one = dot(normed_ref[:, tile], wq[tile])
+        query = one if query is None else query + one
+    copies[cuts].wait()
+    absorb(scale, query.astype(BF16), wk, out_ref)
 
 
 def query_body(scale, normed_ref, wq_ref, wk_ref, out_ref):
-    heads = out_ref.shape[0]
-    query = dot(normed_ref[...], wq_ref[...]).astype(BF16)
-    for h in range(heads):
-        cols = slice(h * HD, (h + 1) * HD)
-        one = dot(query[:, cols], wk_ref[:, cols], ((1,), (1,)))
-        out_ref[h] = (one * scale).astype(BF16)
-
-
-def attention(spans, rows, n_pieces, offset, where_ref, lengths_ref, absorbed_ref, pieces, wv, kv, attn):
+    absorb(scale, dot(normed_ref[...], wq_ref[...]).astype(BF16), wk_ref, out_ref)
+
+
+def attention(spans, rows, n_pieces, offset, absorbed_ref, bias_ref, pieces, wv, kv, ctx, attn):
     heads = absorbed_ref.shape[0]
     rank = kv.shape[1]
     block = n_pieces * rows
-    me = where_ref[0]
     for i, (low, high) in enumerate(spans):
         for g in range(low, high):
             for k in range(n_pieces):
                 piece = pieces[i * n_pieces + k]
                 kv[pl.ds(g * block + k * rows, rows), :] = piece[pl.ds((g - low) * rows, rows), :]
-    col = lax.broadcasted_iota(jnp.int32, (rows, block), 1)
-    row = lax.broadcasted_iota(jnp.int32, (rows, block), 0)
-    key_pos = jnp.bitwise_xor(me, col // rows) * rows + col % rows
-    query_pos = me * rows + row
-    causal = key_pos <= query_pos
     low, high = spans[-1]
+    causal = bias_ref[:, bias_ref.shape[1] - block :]
     for g in range(low, high):
         keys = kv[: (g + 1) * block, :]
         at = g * rows - offset
         absorbed = absorbed_ref[:, at : at + rows, :].reshape(heads * rows, rank)
-        scores = dot(absorbed, keys, ((1,), (1,)))
-        mask = [key_pos < lengths_ref[b] for b in range(g)] + [causal]
-        mask = jnp.concatenate(mask, axis=1)[None]
-        scores = scores.reshape(heads, rows, (g + 1) * block)
-        scores = jnp.where(mask, scores, -1e30)
-        top = jnp.max(scores, axis=2, keepdims=True)
-        weights = jnp.where(mask, jnp.exp(scores - top), 0.0)
+        scores = dot(absorbed, keys, ((1,), (1,))).reshape(heads, rows, (g + 1) * block)
+        bias = jnp.concatenate([bias_ref[:, : g * block], causal], axis=1) if g else causal
+        scores = scores + bias[None]
+        weights = jnp.exp(scores - jnp.max(scores, axis=2, keepdims=True))
         total = jnp.sum(weights, axis=2, keepdims=True).reshape(heads * rows, 1)
         rounded = weights.astype(BF16).reshape(heads * rows, (g + 1) * block)
-        context = (dot(rounded, keys) / total).astype(BF16)
+        context = (dot(rounded, keys) * (1.0 / total)).astype(BF16)
         at = (g - low) * rows
-        for h in range(heads):
-            cols = slice(h * HD, (h + 1) * HD)
-            one = dot(context[h * rows : (h + 1) * rows], wv[:, cols])
-            attn[at : at + rows, cols] = one.astype(BF16)
-
-
-def attend_body(spans, rows, n_pieces, offset, where_ref, lengths_ref, absorbed_ref, *refs):
+        ctx[:, at : at + rows, :] = context.reshape(heads, rows, rank)
+    for h in range(heads):
+        cols = slice(h * HD, (h + 1) * HD)
+        attn[:, cols] = dot(ctx[h], wv[:, cols]).astype(BF16)
+
+
+def attend_body(spans, rows, n_pieces, offset, absorbed_ref, bias_ref, *refs):
     n_in = len(spans) * n_pieces
     pieces = refs[:n_in]
-    wv, wo, out_ref, kv, attn = refs[n_in:]
-    attention(
-        spans, rows, n_pieces, offset, where_ref, lengths_ref, absorbed_ref, pieces, wv, kv, attn
-    )
+    wv, wo, out_ref, kv, ctx, attn = refs[n_in:]
+    attention(spans, rows, n_pieces, offset, absorbed_ref, bias_ref, pieces, wv, kv, ctx, attn)
     out_ref[...] = dot(attn[...], wo[...]).astype(BF16)
 
 
-def attend_last_body(
-    spans, rows, n_pieces, offset, n_head, n_sec, where_ref, lengths_ref, absorbed_ref, *refs
-):
+def attend_last_body(spans, rows, n_pieces, offset, n_head, n_sec, absorbed_ref, bias_ref, *refs):
     n_in = len(spans) * n_pieces
     pieces = refs[:n_in]
     wv, wo, state_ref, keep_ref, give_ref = refs[n_in : n_in + 5]
     sends = refs[n_in + 5 : n_in + 4 + n_head]
-    kv, attn, total = refs[n_in + 4 + n_head :]
-    attention(
-        spans, rows, n_pieces, offset, where_ref, lengths_ref, absorbed_ref, pieces, wv, kv, attn
-    )
+    kv, ctx, attn, total = refs[n_in + 4 + n_head :]
+    attention(spans, rows, n_pieces, offset, absorbed_ref, bias_ref, pieces, wv, kv, ctx, attn)
     total[...] = dot(attn[...], wo[...])
     low, high = spans[-1]
     share = rows // n_head
     width = total.shape[1]
     part = width // n_sec
+    head = place("head")
     for g in range(high - low):
         to = slice(g * share, (g + 1) * share)
 
         def at(h):
             return pl.ds(pl.multiple_of(g * rows + h * share, share), share)
 
-        own = at(where_ref[2])
-        mine = state_ref[own, :] + total[own, :]
+        mine = state_ref[at(head), :] + total[at(head), :]
         give_ref[to] = mine[:, : width - part].astype(BF16)
         keep_ref[to] = mine[:, width - part :]
         for k in range(1, n_head):
-            sends[k - 1][to] = total[at(jnp.bitwise_xor(where_ref[2], k)), :].astype(BF16)
-
-
-def final_body(spans, rows, n_head, n_sec, where_ref, lengths_ref, *refs):
+            sends[k - 1][to] = total[at(jnp.bitwise_xor(head, k)), :].astype(BF16)
+
+
+def final_body(spans, rows, n_head, n_sec, final_ref, *refs):
     out_ref = refs[-1]
     per = 2 + 2 * (n_head - 1)
     share = rows // n_head
     part = out_ref.shape[2]
-    first = where_ref[0] * rows + where_ref[2] * share
+    last = jnp.broadcast_to(place("section"), (share, part)) == n_sec - 1
     for i, (low, high) in enumerate(spans):
         keep, given = refs[i * per : i * per + 2]
         came = refs[i * per + 2 : i * per + 1 + n_head]
         relay = refs[i * per + 1 + n_head : (i + 1) * per]
-        last = jnp.broadcast_to(where_ref[1], (share, part)) == n_sec - 1
         for g in range(low, high):
             at = slice((g - low) * share, (g - low + 1) * share)
             here = keep[at]
@@ -200,7 +238,8 @@
             for k in range(n_head - 1):
                 here = here + relay[k][at, (n_sec - 1) * part :].astype(F32)
                 there = there + came[k][at, :part].astype(F32)
-            out_ref[g] = masked(jnp.where(last, here, there), first, lengths_ref[g])
+            live = final_ref[g * share : (g + 1) * share]
+            out_ref[g] = keep_live(jnp.where(last, here, there), live)
 
 
 def in_hbm(value):
@@ -229,7 +268,6 @@
     n_head = lax.axis_size("head")
     assert n_sec == 2
     sizes = (n_seq, n_sec, n_head)
-    where = jnp.stack([lax.axis_index(axis) for axis in AXES]).astype(jnp.int32)
     groups, rows, width = hidden.shape
     rank = w_latent.shape[2]
     heads = w_key.shape[2] // HD
@@ -239,12 +277,27 @@
     x = hidden.reshape(total_rows, width)
     wl, wq, wk, wv, wo = w_latent[0], w_query[0], w_key[0], w_value[0], w_out[0]
     cut = max(1, groups - 1)
+    cuts = 4
     spans = [(0, cut), (cut, groups)] if cut < groups else [(0, groups)]
     span_size = [(high - low) * rows for low, high in spans]
 
+    def prepare():
+        return pl.pallas_call(
+            functools.partial(prepare_body, rows, n_seq),
+            out_shape=(
+                array(F32, rows, (groups + 1) * n_seq * rows),
+                array(F32, total_rows, HD),
+                array(F32, groups * share, HD),
+            ),
+            in_specs=[SMEM],
+            out_specs=(VMEM,) * 3,
+            compiler_params=params(8),
+            name="prepare",
+        )(lengths)
+
     def first_latent():
         out = pl.pallas_call(
-            functools.partial(first_latent_body, spans, rows),
+            functools.partial(first_latent_body, spans, rows, cuts),
             out_shape=(
                 array(BF16, total_rows, width),
                 array(F32, total_rows, rank),
@@ -257,7 +310,7 @@
                 pltpu.VMEM((1, width), F32),
                 pltpu.VMEM((1, rank), F32),
                 pltpu.VMEM((width, rank), BF16),
-                pltpu.SemaphoreType.DMA((4,)),
+                pltpu.SemaphoreType.DMA((3 + cuts,)),
             ],
             compiler_params=params(12),
             name="first_latent",
@@ -274,11 +327,11 @@
                 array(F32, size, rank),
                 array(BF16, size, rank),
             ),
-            in_specs=[SMEM] * 2 + [VMEM] * (5 + len(parts)),
+            in_specs=[VMEM] * (6 + len(parts)),
             out_specs=(VMEM,) * 4,
             compiler_params=params(8),
             cost_estimate=cost(2 * size * width * rank, 2 * width * (rank + 2 * size)),
-        )(where, lengths, x, *parts, attn_gain, wl, latent_gain, before)
+        )(x, *parts, attn_gain, wl, latent_gain, before, live)
 
     def project(normed):
         size = normed.shape[0]
@@ -293,6 +346,24 @@
             ),
         )(normed, wq, wk)
 
+    def first_project(normed):
+        size = normed.shape[0]
+        return pl.pallas_call(
+            functools.partial(first_query_body, 1.0 / HD**0.5, cuts),
+            out_shape=array(BF16, heads, size, rank),
+            in_specs=[VMEM, HBM, HBM],
+            out_specs=VMEM,
+            scratch_shapes=[
+                pltpu.VMEM((width, heads * HD), BF16),
+                pltpu.VMEM((rank, heads * HD), BF16),
+                pltpu.SemaphoreType.DMA((cuts + 1,)),
+            ],
+            compiler_params=params(14),
+            cost_estimate=cost(
+                2 * size * heads * HD * (width + rank), 2 * heads * HD * (width + rank + size)
+            ),
+        )(normed, in_hbm(wq), in_hbm(wk))
+
     def attend(i, absorbed, offset, pieces, state=None):
         which = spans[: i + 1]
         high = spans[i][1]
@@ -300,6 +371,7 @@
         flat = [piece for of_span in pieces[: i + 1] for piece in of_span]
         scratch = [
             pltpu.VMEM((high * n_seq * rows, rank), BF16),
+            pltpu.VMEM((heads, size, rank), BF16),
             pltpu.VMEM((size, heads * HD), BF16),
         ]
         common = dict(
@@ -314,11 +386,11 @@
             return pl.pallas_call(
                 functools.partial(attend_body, which, rows, n_seq, offset),
                 out_shape=array(BF16, size, width),
-                in_specs=[SMEM, SMEM] + [VMEM] * (3 + len(flat)),
+                in_specs=[VMEM] * (4 + len(flat)),
                 out_specs=VMEM,
                 scratch_shapes=scratch,
                 **common,
-            )(where, lengths, absorbed, *flat, wv, wo)
+            )(absorbed, bias, *flat, wv, wo)
         small = size // n_head
         return pl.pallas_call(
             functools.partial(attend_last_body, which, rows, n_seq, offset, n_head, n_sec),
@@ -327,11 +399,11 @@
                 array(BF16, small, width - part_width),
                 *(array(BF16, small, width) for _ in range(n_head - 1)),
             ),
-            in_specs=[SMEM, SMEM] + [VMEM] * (4 + len(flat)),
+            in_specs=[VMEM] * (5 + len(flat)),
             out_specs=(VMEM,) * (1 + n_head),
             scratch_shapes=scratch + [pltpu.VMEM((size, width), F32)],
             **common,
-        )(where, lengths, absorbed, *flat, wv, wo, state)
+        )(absorbed, bias, *flat, wv, wo, state)
 
     def swap(value):
         return permute(value, sizes, lambda s, c, h: (s, 1 - c, h))
@@ -355,7 +427,8 @@
 
     normed, full, latents = first_latent()
     pieces = [gather(latent, 0) for latent in latents]
-    absorbed = project(normed)
+    bias, live, final_live = prepare()
+    absorbed = first_project(normed)
     parts = [hand_on(attend(i, absorbed, 0, pieces)) for i in range(len(spans))]
     pieces, queries, states, lives = [], [], [], []
     for i in range(len(spans)):
@@ -377,11 +450,11 @@
     final = pl.pallas_call(
         functools.partial(final_body, spans, rows, n_head, n_sec),
         out_shape=array(F32, groups, share, part_width),
-        in_specs=[SMEM] * 2 + [VMEM] * len(ends),
+        in_specs=[VMEM] * (1 + len(ends)),
         out_specs=VMEM,
         compiler_params=params(12),
         name="final",
-    )(where, lengths, *ends)
+    )(final_live, *ends)
     stored = jnp.concatenate(lives, 0).reshape(1, groups, rows, rank)
     return (final, stored)
 

time: 75.1 us -> 60.5 us (0.81)
  local copies, waits for them, and re-layouts: 10.4 us -> 0.71 us
  Pallas kernels: 23.5 us -> 20.3 us
  starting transfers between devices: 22.5 us -> 20 us
  waiting for transfers between devices: 16.7 us -> 17.7 us
    unnamed x38 -> x18, local copies, waits for them, and re-layouts: 10.4 us -> 0.71 us
    pallas_call x1 -> x3, Pallas kernels: 2.66 us -> 6.23 us  [the longest x1 3.3 us: first_project(): pl.pallas_call(functools.partial(first_query_body, 1.0 / HD ** 0.5, cuts)...]
    pallas_call x2, Pallas kernels: 7.11 us -> 4.57 us  [attend(): pl.pallas_call(functools.partial(attend_body, which, rows, n_seq, offset)...]
    ppermute x26, starting transfers between devices: 22.5 us -> 20 us  [permute(): return lax.ppermute(value, AXES, pairs)]
    pallas_call x3 -> x2, Pallas kernels: 3.63 us -> 2.21 us  [project(): pl.pallas_call(functools.partial(query_body, 1.0 / HD ** 0.5), out_shape=...]
    pallas_call x2, Pallas kernels: 6.05 us -> 4.79 us  [attend(): pl.pallas_call(functools.partial(attend_last_body, which, rows, n_seq, of...]
    pallas_call x2, Pallas kernels: 2.7 us -> 1.6 us  [next_latent(): pl.pallas_call(functools.partial(next_latent_body, spans[i], rows, len(pa...]
    ppermute x26, waiting for transfers between devices: 16.7 us -> 17.7 us  [permute(): return lax.ppermute(value, AXES, pairs)]
  transfers between devices with their start and end apart: 26 -> 26, of which waited for: 12 -> 12; matrix products, arithmetic and copies ran while one was open for 1% -> 1% of each run, Pallas kernels for 19% -> 23%
where the time goes in v3:
time: 60.5 us; the launch traced here: 60.3 us
  Pallas kernels  20.3 us (34%)
  starting transfers between devices  20 us (33%)
  waiting for transfers between devices  17.7 us (29%)
  between operations  0.86 us (1%)
  other arithmetic  0.77 us (1%)
  local copies, waits for them, and re-layouts  0.71 us (1%)
    ppermute x26, starting transfers between devices, permute(): return lax.ppermute(value, AXES, pairs)  20 us
    ppermute x26, waiting for transfers between devices, permute(): return lax.ppermute(value, AXES, pairs)  17.7 us
    pallas_call x2, Pallas kernels, attend(): pl.pallas_call(functools.partial(attend_last_body, which, rows, n_seq, of...  4.79 us
    pallas_call x2, Pallas kernels, attend(): pl.pallas_call(functools.partial(attend_body, which, rows, n_seq, offset)...  4.57 us
    pallas_call x1, Pallas kernels, first_project(): pl.pallas_call(functools.partial(first_query_body, 1.0 / HD ** 0.5, cuts)...  3.3 us
    pallas_call x1, Pallas kernels, first_latent(): pl.pallas_call(functools.partial(first_latent_body, spans, rows, cuts), o...  2.35 us
    pallas_call x2, Pallas kernels, project(): pl.pallas_call(functools.partial(query_body, 1.0 / HD ** 0.5), out_shape=...  2.21 us
    pallas_call x2, Pallas kernels, next_latent(): pl.pallas_call(functools.partial(next_latent_body, spans[i], rows, len(pa...  1.6 us
  transfers between devices with their start and end apart: 26, of which 12 were waited for; matrix products, arithmetic and copies ran while one was open for 1% of the time, Pallas kernels for 23%

profile of v3, /device:TPU:0, one launch (start us, length us, event | category | flops | bytes accessed | tf_op | source)
XLA Modules:
  0.0 60.3 jit_solution(5390196926331103128)
XLA Ops:
  0.6 2.4 %first_latent.1 = (bf16[192,2048]{1,0:T(8,128)(2,1)S(1)}, f32[192,512]{1,0:T(8,128)S(1)}, bf16[128,512]{1,0:T(8,128)(2,1)S(1)}, bf16[64,512]{1,0:T(8,128)(2,1)S(1)}) custom-call(bf16[192,2048]{1,0:T(8,128)(2,1)} %bitcast.24, f32[1,2048]{1,0:T(1,128)} %refs_3_.5, bf16[2048,512]{1,0:T(8,128)(2,1)} %bitcast.14, f32[1,512]{1,0:T(1,128)} %refs_5_.3), custom_call_target="tpu_custom_call" | custom-call | tf_op jit(solution)/shard_map/first_latent/pallas_call | solution.py:299
  3.0 0.0 copy-start
  3.0 0.0 copy-start.3
  3.0 0.6 collective-permute-start
  3.6 1.0 %collective-permute-done = bf16[128,512]{1,0:T(8,128)(2,1)S(1)} collective-permute-done((bf16[128,512]{1,0:T(8,128)(2,1)S(1)}, bf16[128,512]{1,0:T(8,128)(2,1)S(1)}, u32[]{:S(2)}, u32[]{:S(2)}) %collective-permute-start) | collective-permute-done | bytes 131104 | tf_op jit(solution)/shard_map/ppermute | solution.py:30
  4.6 0.4 collective-permute-start.3
  4.9 4.7 %collective-permute-start.2 = (bf16[128,512]{1,0:T(8,128)(2,1)S(1)}, bf16[128,512]{1,0:T(8,128)(2,1)S(1)}, u32[]{:S(2)}, u32[]{:S(2)}) collective-permute-start(bf16[128,512]{1,0:T(8,128)(2,1)S(1)} %collective-permute-done), channel_id=1, source_target_pairs={{0,2},{1,3},{2,8},{3,9},{4,6},{5,7},{6,12},{7,13},{8,10},{9,11},{1... | collective-permute-start | bytes 393224 | tf_op jit(solution)/shard_map/ppermute | solution.py:30
  9.6 0.7 %copy-done.8 = s32[3]{0:T(128)S(1)} copy-done((s32[3]{0:T(128)S(1)}, s32[3]{0:T(128)}, u32[]{:S(2)}) %copy-start.8) | copy-done | bytes 36
  10.3 0.6 prepare.1
  10.9 3.3 %shard_map.104.absorbed_ref = bf16[8,192,512]{2,1,0:T(8,128)(2,1)S(1)} custom-call(bf16[192,2048]{1,0:T(8,128)(2,1)S(1)} %get-tuple-element.26.normed_ref, bf16[2048,1024]{1,0:T(8,128)(2,1)} %bitcast.11, bf16[512,1024]{1,0:T(8,128)(2,1)} %bitcast.21), custom_call_target="tpu_custom_call" | custom-call | flops 1006632960 | bytes 5636096 | tf_op jit(solution)/shard_map/pallas_call | solution.py:351
  14.2 1.3 %collective-permute-done.2.refs_2_ = bf16[128,512]{1,0:T(8,128)(2,1)S(1)} collective-permute-done((bf16[128,512]{1,0:T(8,128)(2,1)S(1)}, bf16[128,512]{1,0:T(8,128)(2,1)S(1)}, u32[]{:S(2)}, u32[]{:S(2)}) %collective-permute-start.2) | collective-permute-done | bytes 131104 | tf_op jit(solution)/shard_map/ppermute | solution.py:30
  15.5 2.4 %shard_map.105 = bf16[128,2048]{1,0:T(8,128)(2,1)S(1)} custom-call(bf16[8,192,512]{2,1,0:T(8,128)(2,1)S(1)} %shard_map.104.absorbed_ref, f32[64,1024]{1,0:T(8,128)S(1)} %get-tuple-element.27.bias_ref, bf16[128,512]{1,0:T(8,128)(2,1)S(1)} %get-tuple-element.28.refs_0_, bf16[128,512]{1,0:T(8,128)(2,1)S(1)} %collective-permute-done.1.refs_1_, ...), custom_call_target="tpu_custom_call" | custom-call | flops 1073741824 | bytes 5242880 | tf_op jit(solution)/shard_map/pallas_call | solution.py:386
  17.9 0.1 collective-permute-start.5
  18.0 0.5 collective-permute-start.4
  18.5 6.2 %collective-permute-done.5.refs_2_ = bf16[128,2048]{1,0:T(8,128)(2,1)S(1)} collective-permute-done((bf16[128,2048]{1,0:T(8,128)(2,1)S(1)}, bf16[128,2048]{1,0:T(8,128)(2,1)S(1)}, u32[]{:S(2)}, u32[]{:S(2)}) %collective-permute-start.5) | collective-permute-done | bytes 524320 | tf_op jit(solution)/shard_map/ppermute | solution.py:30
  24.7 0.9 %shard_map.106 = (f32[128,2048]{1,0:T(8,128)S(1)}, bf16[128,2048]{1,0:T(8,128)(2,1)S(1)}, f32[128,512]{1,0:T(8,128)S(1)}, bf16[128,512]{1,0:T(8,128)(2,1)S(1)}) custom-call(bf16[192,2048]{1,0:T(8,128)(2,1)S(1)} %bitcast.25, bf16[128,2048]{1,0:T(8,128)(2,1)S(1)} %collective-permute-done.4.refs_1_, bf16[128,2048]{1,0:T(8,128)(2,1)S(1)} %collective-permute-done.5.refs_2_, ...), custom_call_target="tpu_custom_call" | custom-call | flops 268435456 | bytes 3145728 | tf_op jit(solution)/shard_map/pallas_call | solution.py:322
  25.6 1.8 %collective-permute-start.6 = (bf16[128,512]{1,0:T(8,128)(2,1)S(1)}, bf16[128,512]{1,0:T(8,128)(2,1)S(1)}, u32[]{:S(2)}, u32[]{:S(2)}) collective-permute-start(bf16[128,512]{1,0:T(8,128)(2,1)S(1)} %get-tuple-element.32.refs_0_), channel_id=1, source_target_pairs={{0,2},{1,3},{2,0},{3,1},{4,6},{5,7},{6,4},{7,5},{8,10},{9,11},{10,... | collective-permute-start | bytes 393224 | tf_op jit(solution)/shard_map/ppermute | solution.py:30
  27.4 0.1 collective-permute-start.13
  27.5 1.2 %collective-permute-done.13 = bf16[64,512]{1,0:T(8,128)(2,1)S(1)} collective-permute-done((bf16[64,512]{1,0:T(8,128)(2,1)S(1)}, bf16[64,512]{1,0:T(8,128)(2,1)S(1)}, u32[]{:S(2)}, u32[]{:S(2)}) %collective-permute-start.13) | collective-permute-done | bytes 65568 | tf_op jit(solution)/shard_map/ppermute | solution.py:30
  28.7 0.2 collective-permute-start.16
  28.9 2.4 %collective-permute-start.15 = (bf16[64,512]{1,0:T(8,128)(2,1)S(1)}, bf16[64,512]{1,0:T(8,128)(2,1)S(1)}, u32[]{:S(2)}, u32[]{:S(2)}) collective-permute-start(bf16[64,512]{1,0:T(8,128)(2,1)S(1)} %collective-permute-done.13), channel_id=1, source_target_pairs={{0,2},{1,3},{2,8},{3,9},{4,6},{5,7},{6,12},{7,13},{8,10},{9,11},{1... | collective-permute-start | bytes 196616 | tf_op jit(solution)/shard_map/ppermute | solution.py:30
  31.3 1.4 %collective-permute-start.9 = (bf16[128,512]{1,0:T(8,128)(2,1)S(1)}, bf16[128,512]{1,0:T(8,128)(2,1)S(1)}, u32[]{:S(2)}, u32[]{:S(2)}) collective-permute-start(bf16[128,512]{1,0:T(8,128)(2,1)S(1)} %collective-permute-done.6), channel_id=1, source_target_pairs={{0,14},{1,15},{2,0},{3,1},{4,10},{5,11},{6,4},{7,5},{8,6},{9,7},{1... | collective-permute-start | bytes 393224 | tf_op jit(solution)/shard_map/ppermute | solution.py:30
  32.7 0.2 collective-permute-start.8
  32.9 1.4 %collective-permute-done.16.refs_7_ = bf16[64,512]{1,0:T(8,128)(2,1)S(1)} collective-permute-done((bf16[64,512]{1,0:T(8,128)(2,1)S(1)}, bf16[64,512]{1,0:T(8,128)(2,1)S(1)}, u32[]{:S(2)}, u32[]{:S(2)}) %collective-permute-start.16) | collective-permute-done | bytes 65568 | tf_op jit(solution)/shard_map/ppermute | solution.py:30
  34.3 0.9 %collective-permute-done.15.refs_6_ = bf16[64,512]{1,0:T(8,128)(2,1)S(1)} collective-permute-done((bf16[64,512]{1,0:T(8,128)(2,1)S(1)}, bf16[64,512]{1,0:T(8,128)(2,1)S(1)}, u32[]{:S(2)}, u32[]{:S(2)}) %collective-permute-start.15) | collective-permute-done | bytes 65568 | tf_op jit(solution)/shard_map/ppermute | solution.py:30
  35.2 2.2 %shard_map.109 = bf16[64,2048]{1,0:T(8,128)(2,1)S(1)} custom-call(bf16[8,192,512]{2,1,0:T(8,128)(2,1)S(1)} %shard_map.104.absorbed_ref, f32[64,1024]{1,0:T(8,128)S(1)} %get-tuple-element.27.bias_ref, bf16[128,512]{1,0:T(8,128)(2,1)S(1)} %get-tuple-element.28.refs_0_, bf16[128,512]{1,0:T(8,128)(2,1)S(1)} %collective-permute-done.1.refs_1_, ...), custom_call_target="tpu_custom_call" | custom-call | flops 805306368 | bytes 5242880 | tf_op jit(solution)/shard_map/pallas_call | solution.py:386
  37.4 0.1 collective-permute-start.18
  37.5 0.5 collective-permute-start.17
  38.0 1.0 %shard_map.107.absorbed_ref = bf16[8,128,512]{2,1,0:T(8,128)(2,1)S(1)} custom-call(bf16[128,2048]{1,0:T(8,128)(2,1)S(1)} %get-tuple-element.31.normed_ref, bf16[2048,1024]{1,0:T(8,128)(2,1)S(1)} %bitcast.12, bf16[512,1024]{1,0:T(8,128)(2,1)S(1)} %bitcast.22), custom_call_target="tpu_custom_call" | custom-call | flops 671088640 | bytes 5505024 | tf_op jit(solution)/shard_map/pallas_call | solution.py:338
  39.0 2.5 %shard_map.108 = (f32[64,1024]{1,0:T(8,128)S(1)}, bf16[64,1024]{1,0:T(8,128)(2,1)S(1)}, bf16[64,2048]{1,0:T(8,128)(2,1)S(1)}) custom-call(bf16[8,128,512]{2,1,0:T(8,128)(2,1)S(1)} %shard_map.107.absorbed_ref, f32[64,1024]{1,0:T(8,128)S(1)} %get-tuple-element.27.bias_ref, bf16[128,512]{1,0:T(8,128)(2,1)S(1)} %get-tuple-element.32.refs_0_, ...), custom_call_target="tpu_custom_call" | custom-call | flops 1073741824 | bytes 5242880 | tf_op jit(solution)/shard_map/pallas_call | solution.py:395
  41.6 2.7 %collective-permute-start.11 = (bf16[64,2048]{1,0:T(8,128)(2,1)S(1)}, bf16[64,2048]{1,0:T(8,128)(2,1)S(1)}, u32[]{:S(2)}, u32[]{:S(2)}) collective-permute-start(bf16[64,2048]{1,0:T(8,128)(2,1)S(1)} %get-tuple-element.36), channel_id=1, source_target_pairs={{0,2},{1,3},{2,1},{3,0},{4,6},{5,7},{6,5},{7,4},{8,10},{9,11},{10,... | collective-permute-start | bytes 786440 | tf_op jit(solution)/shard_map/ppermute | solution.py:30
  44.3 0.8 %shard_map.110 = (f32[64,2048]{1,0:T(8,128)S(1)}, bf16[64,2048]{1,0:T(8,128)(2,1)S(1)}, f32[64,512]{1,0:T(8,128)S(1)}, bf16[64,512]{1,0:T(8,128)(2,1)S(1)}) custom-call(bf16[192,2048]{1,0:T(8,128)(2,1)S(1)} %bitcast.26, bf16[64,2048]{1,0:T(8,128)(2,1)S(1)} %collective-permute-done.17.refs_1_, bf16[64,2048]{1,0:T(8,128)(2,1)S(1)} %collective-permute-done.18.refs_2_, ...), custom_call_target="tpu_custom_call" | custom-call | flops 134217728 | bytes 2621440 | tf_op jit(solution)/shard_map/pallas_call | solution.py:322
  45.1 0.1 collective-permute-start.19
  45.1 1.2 %collective-permute-done.19 = bf16[64,512]{1,0:T(8,128)(2,1)S(1)} collective-permute-done((bf16[64,512]{1,0:T(8,128)(2,1)S(1)}, bf16[64,512]{1,0:T(8,128)(2,1)S(1)}, u32[]{:S(2)}, u32[]{:S(2)}) %collective-permute-start.19) | collective-permute-done | bytes 65568 | tf_op jit(solution)/shard_map/ppermute | solution.py:30
  46.4 1.1 %collective-permute-start.22 = (bf16[64,512]{1,0:T(8,128)(2,1)S(1)}, bf16[64,512]{1,0:T(8,128)(2,1)S(1)}, u32[]{:S(2)}, u32[]{:S(2)}) collective-permute-start(bf16[64,512]{1,0:T(8,128)(2,1)S(1)} %collective-permute-done.19), channel_id=1, source_target_pairs={{0,14},{1,15},{2,0},{3,1},{4,10},{5,11},{6,4},{7,5},{8,6},{9,7},{1... | collective-permute-start | bytes 196616 | tf_op jit(solution)/shard_map/ppermute | solution.py:30
  47.5 1.2 %shard_map.111.absorbed_ref = bf16[8,64,512]{2,1,0:T(8,128)(2,1)S(1)} custom-call(bf16[64,2048]{1,0:T(8,128)(2,1)S(1)} %get-tuple-element.40.normed_ref, bf16[2048,1024]{1,0:T(8,128)(2,1)S(1)} %bitcast.13, bf16[512,1024]{1,0:T(8,128)(2,1)S(1)} %bitcast.23), custom_call_target="tpu_custom_call" | custom-call | flops 335544320 | bytes 5373952 | tf_op jit(solution)/shard_map/pallas_call | solution.py:338
  48.7 0.7 %collective-permute-done.22.refs_7_ = bf16[64,512]{1,0:T(8,128)(2,1)S(1)} collective-permute-done((bf16[64,512]{1,0:T(8,128)(2,1)S(1)}, bf16[64,512]{1,0:T(8,128)(2,1)S(1)}, u32[]{:S(2)}, u32[]{:S(2)}) %collective-permute-start.22) | collective-permute-done | bytes 65568 | tf_op jit(solution)/shard_map/ppermute | solution.py:30
  49.4 0.6 %collective-permute-done.21.refs_6_ = bf16[64,512]{1,0:T(8,128)(2,1)S(1)} collective-permute-done((bf16[64,512]{1,0:T(8,128)(2,1)S(1)}, bf16[64,512]{1,0:T(8,128)(2,1)S(1)}, u32[]{:S(2)}, u32[]{:S(2)}) %collective-permute-start.21) | collective-permute-done | bytes 65568 | tf_op jit(solution)/shard_map/ppermute | solution.py:30
  50.0 0.7 %collective-permute-done.20.refs_5_ = bf16[64,512]{1,0:T(8,128)(2,1)S(1)} collective-permute-done((bf16[64,512]{1,0:T(8,128)(2,1)S(1)}, bf16[64,512]{1,0:T(8,128)(2,1)S(1)}, u32[]{:S(2)}, u32[]{:S(2)}) %collective-permute-start.20) | collective-permute-done | bytes 65568 | tf_op jit(solution)/shard_map/ppermute | solution.py:30
  50.7 2.2 %shard_map.112 = (f32[32,1024]{1,0:T(8,128)S(1)}, bf16[32,1024]{1,0:T(8,128)(2,1)S(1)}, bf16[32,2048]{1,0:T(8,128)(2,1)S(1)}) custom-call(bf16[8,64,512]{2,1,0:T(8,128)(2,1)S(1)} %shard_map.111.absorbed_ref, f32[64,1024]{1,0:T(8,128)S(1)} %get-tuple-element.27.bias_ref, bf16[128,512]{1,0:T(8,128)(2,1)S(1)} %get-tuple-element.32.refs_0_, ...), custom_call_target="tpu_custom_call" | custom-call | flops 805306368 | bytes 5242880 | tf_op jit(solution)/shard_map/pallas_call | solution.py:395
  52.9 2.2 %collective-permute-start.24 = (bf16[32,2048]{1,0:T(8,128)(2,1)S(1)}, bf16[32,2048]{1,0:T(8,128)(2,1)S(1)}, u32[]{:S(2)}, u32[]{:S(2)}) collective-permute-start(bf16[32,2048]{1,0:T(8,128)(2,1)S(1)} %get-tuple-element.45), channel_id=1, source_target_pairs={{0,2},{1,3},{2,1},{3,0},{4,6},{5,7},{6,5},{7,4},{8,10},{9,11},{10,... | collective-permute-start | bytes 393224 | tf_op jit(solution)/shard_map/ppermute | solution.py:30
  55.2 0.1 collective-permute-start.12
  55.3 0.4 collective-permute-start.10
  55.7 2.3 %collective-permute-done.24.refs_6_ = bf16[32,2048]{1,0:T(8,128)(2,1)S(1)} collective-permute-done((bf16[32,2048]{1,0:T(8,128)(2,1)S(1)}, bf16[32,2048]{1,0:T(8,128)(2,1)S(1)}, u32[]{:S(2)}, u32[]{:S(2)}) %collective-permute-start.24) | collective-permute-done | bytes 131104 | tf_op jit(solution)/shard_map/ppermute | solution.py:30
  58.0 0.5 collective-permute-start.23
  58.5 0.8 %pad_maximum_fusion = f32[192,512]{1,0:T(8,128)} fusion(f32[64,512]{1,0:T(8,128)S(1)} %get-tuple-element.47, f32[128,512]{1,0:T(8,128)S(1)} %get-tuple-element.46), kind=kLoop, calls=%fused_computation | loop fusion | flops 98304 | bytes 786432 | tf_op jit(solution)/shard_map/concatenate | solution.py:458
  59.3 0.2 collective-permute-done.23.refs_5_
  59.5 0.9 %final.1 = f32[3,32,1024]{2,1,0:T(8,128)} custom-call(f32[96,128]{1,0:T(8,128)S(1)} %get-tuple-element.25.final_ref, f32[64,1024]{1,0:T(8,128)S(1)} %get-tuple-element.34.refs_0_, bf16[64,1024]{1,0:T(8,128)(2,1)S(1)} %collective-permute-done.10.refs_1_, bf16[64,2048]{1,0:T(8,128)(2,1)S(1)} %collective-permute-done.11.refs_2_, ...), custom_call_target="tpu_custom_call" | custom-call | tf_op jit(solution)/shard_map/final/pallas_call | solution.py:450
  (35 shorter events, 0.1 us)
Async XLA Ops:
  3.0 12.5 %copy-start = (bf16[1,1024,2048]{2,1,0:T(8,128)(2,1)S(1)}, bf16[1,1024,2048]{2,1,0:T(8,128)(2,1)}, u32[]{:S(2)}) copy-start(bf16[1,1024,2048]{2,1,0:T(8,128)(2,1)} %param.17) | copy-start | bytes 12582916
  3.0 12.5 %copy-start.3 = (bf16[1,512,1024]{2,1,0:T(8,128)(2,1)S(1)}, bf16[1,512,1024]{2,1,0:T(8,128)(2,1)}, u32[]{:S(2)}) copy-start(bf16[1,512,1024]{2,1,0:T(8,128)(2,1)} %param.16) | copy-start | bytes 3145732
  3.0 1.5 %collective-permute-start = (bf16[128,512]{1,0:T(8,128)(2,1)S(1)}, bf16[128,512]{1,0:T(8,128)(2,1)S(1)}, u32[]{:S(2)}, u32[]{:S(2)}) collective-permute-start(bf16[128,512]{1,0:T(8,128)(2,1)S(1)} %get-tuple-element.28.refs_0_), channel_id=1, source_target_pairs={{0,2},{1,3},{2,0},{3,1},{4,6},{5,7},{6,4},{7,5},{8,10},{9,11},{10,... | collective-permute-start | bytes 393224 | tf_op jit(solution)/shard_map/ppermute | solution.py:30
  4.6 9.7 %collective-permute-start.3 = (bf16[128,512]{1,0:T(8,128)(2,1)S(1)}, bf16[128,512]{1,0:T(8,128)(2,1)S(1)}, u32[]{:S(2)}, u32[]{:S(2)}) collective-permute-start(bf16[128,512]{1,0:T(8,128)(2,1)S(1)} %collective-permute-done), channel_id=1, source_target_pairs={{0,2},{1,3},{2,12},{3,13},{4,6},{5,7},{6,8},{7,9},{8,10},{9,11},{1... | collective-permute-start | bytes 393224 | tf_op jit(solution)/shard_map/ppermute | solution.py:30
  4.9 10.6 %collective-permute-start.2 = (bf16[128,512]{1,0:T(8,128)(2,1)S(1)}, bf16[128,512]{1,0:T(8,128)(2,1)S(1)}, u32[]{:S(2)}, u32[]{:S(2)}) collective-permute-start(bf16[128,512]{1,0:T(8,128)(2,1)S(1)} %collective-permute-done), channel_id=1, source_target_pairs={{0,2},{1,3},{2,8},{3,9},{4,6},{5,7},{6,12},{7,13},{8,10},{9,11},{1... | collective-permute-start | bytes 393224 | tf_op jit(solution)/shard_map/ppermute | solution.py:30
  9.6 5.9 %collective-permute-start.1 = (bf16[128,512]{1,0:T(8,128)(2,1)S(1)}, bf16[128,512]{1,0:T(8,128)(2,1)S(1)}, u32[]{:S(2)}, u32[]{:S(2)}) collective-permute-start(bf16[128,512]{1,0:T(8,128)(2,1)S(1)} %collective-permute-done), channel_id=1, source_target_pairs={{0,2},{1,3},{2,4},{3,5},{4,6},{5,7},{6,0},{7,1},{8,10},{9,11},{10,... | collective-permute-start | bytes 393224 | tf_op jit(solution)/shard_map/ppermute | solution.py:30
  9.6 0.7 %copy-start.8 = (s32[3]{0:T(128)S(1)}, s32[3]{0:T(128)}, u32[]{:S(2)}) copy-start(s32[3]{0:T(128)} %lengths_ref.1) | copy-start | bytes 40
  14.2 10.5 %copy-start.2 = (bf16[1,2048,512]{2,1,0:T(8,128)(2,1)S(1)}, bf16[1,2048,512]{2,1,0:T(8,128)(2,1)}, u32[]{:S(2)}) copy-start(bf16[1,2048,512]{2,1,0:T(8,128)(2,1)} %param.13) | copy-start | bytes 6291460
  14.2 10.5 %copy-start.5 = (bf16[3,64,2048]{2,1,0:T(8,128)(2,1)S(1)}, bf16[3,64,2048]{2,1,0:T(8,128)(2,1)}, u32[]{:S(2)}) copy-start(bf16[3,64,2048]{2,1,0:T(8,128)(2,1)} %param.9) | copy-start | bytes 2359300
  14.2 10.5 %copy-start.6 = (f32[1,2048]{1,0:T(1,128)S(1)}, f32[1,2048]{1,0:T(1,128)}, u32[]{:S(2)}) copy-start(f32[1,2048]{1,0:T(1,128)} %refs_3_.5) | copy-start | bytes 24580
  14.2 10.5 %copy-start.7 = (f32[1,512]{1,0:T(1,128)S(1)}, f32[1,512]{1,0:T(1,128)}, u32[]{:S(2)}) copy-start(f32[1,512]{1,0:T(1,128)} %refs_5_.3) | copy-start | bytes 6148
  17.9 6.8 %collective-permute-start.5 = (bf16[128,2048]{1,0:T(8,128)(2,1)S(1)}, bf16[128,2048]{1,0:T(8,128)(2,1)S(1)}, u32[]{:S(2)}, u32[]{:S(2)}) collective-permute-start(bf16[128,2048]{1,0:T(8,128)(2,1)S(1)} %shard_map.105), channel_id=1, source_target_pairs={{0,3},{1,2},{2,0},{3,1},{4,7},{5,6},{6,4},{7,5},{8,11},{9,10},{10,... | collective-permute-start | bytes 1572872 | tf_op jit(solution)/shard_map/ppermute | solution.py:30
  18.0 6.7 %collective-permute-start.4 = (bf16[128,2048]{1,0:T(8,128)(2,1)S(1)}, bf16[128,2048]{1,0:T(8,128)(2,1)S(1)}, u32[]{:S(2)}, u32[]{:S(2)}) collective-permute-start(bf16[128,2048]{1,0:T(8,128)(2,1)S(1)} %shard_map.105), channel_id=1, source_target_pairs={{0,2},{1,3},{2,0},{3,1},{4,6},{5,7},{6,4},{7,5},{8,10},{9,11},{10,... | collective-permute-start | bytes 1572872 | tf_op jit(solution)/shard_map/ppermute | solution.py:30
  25.6 12.4 %copy-start.1 = (bf16[1,2048,1024]{2,1,0:T(8,128)(2,1)S(1)}, bf16[1,2048,1024]{2,1,0:T(8,128)(2,1)}, u32[]{:S(2)}) copy-start(bf16[1,2048,1024]{2,1,0:T(8,128)(2,1)} %param.12) | copy-start | bytes 12582916
  25.6 12.4 %copy-start.4 = (bf16[1,512,1024]{2,1,0:T(8,128)(2,1)S(1)}, bf16[1,512,1024]{2,1,0:T(8,128)(2,1)}, u32[]{:S(2)}) copy-start(bf16[1,512,1024]{2,1,0:T(8,128)(2,1)} %param.15) | copy-start | bytes 3145732
  25.6 5.7 %collective-permute-start.6 = (bf16[128,512]{1,0:T(8,128)(2,1)S(1)}, bf16[128,512]{1,0:T(8,128)(2,1)S(1)}, u32[]{:S(2)}, u32[]{:S(2)}) collective-permute-start(bf16[128,512]{1,0:T(8,128)(2,1)S(1)} %get-tuple-element.32.refs_0_), channel_id=1, source_target_pairs={{0,2},{1,3},{2,0},{3,1},{4,6},{5,7},{6,4},{7,5},{8,10},{9,11},{10,... | collective-permute-start | bytes 393224 | tf_op jit(solution)/shard_map/ppermute | solution.py:30
  27.4 1.3 %collective-permute-start.13 = (bf16[64,512]{1,0:T(8,128)(2,1)S(1)}, bf16[64,512]{1,0:T(8,128)(2,1)S(1)}, u32[]{:S(2)}, u32[]{:S(2)}) collective-permute-start(bf16[64,512]{1,0:T(8,128)(2,1)S(1)} %get-tuple-element.37.refs_4_), channel_id=1, source_target_pairs={{0,2},{1,3},{2,0},{3,1},{4,6},{5,7},{6,4},{7,5},{8,10},{9,11},{10,... | collective-permute-start | bytes 196616 | tf_op jit(solution)/shard_map/ppermute | solution.py:30
  28.7 5.6 %collective-permute-start.16 = (bf16[64,512]{1,0:T(8,128)(2,1)S(1)}, bf16[64,512]{1,0:T(8,128)(2,1)S(1)}, u32[]{:S(2)}, u32[]{:S(2)}) collective-permute-start(bf16[64,512]{1,0:T(8,128)(2,1)S(1)} %collective-permute-done.13), channel_id=1, source_target_pairs={{0,2},{1,3},{2,12},{3,13},{4,6},{5,7},{6,8},{7,9},{8,10},{9,11},{1... | collective-permute-start | bytes 196616 | tf_op jit(solution)/shard_map/ppermute | solution.py:30
  28.9 6.3 %collective-permute-start.15 = (bf16[64,512]{1,0:T(8,128)(2,1)S(1)}, bf16[64,512]{1,0:T(8,128)(2,1)S(1)}, u32[]{:S(2)}, u32[]{:S(2)}) collective-permute-start(bf16[64,512]{1,0:T(8,128)(2,1)S(1)} %collective-permute-done.13), channel_id=1, source_target_pairs={{0,2},{1,3},{2,8},{3,9},{4,6},{5,7},{6,12},{7,13},{8,10},{9,11},{1... | collective-permute-start | bytes 196616 | tf_op jit(solution)/shard_map/ppermute | solution.py:30
  31.3 3.9 %collective-permute-start.14 = (bf16[64,512]{1,0:T(8,128)(2,1)S(1)}, bf16[64,512]{1,0:T(8,128)(2,1)S(1)}, u32[]{:S(2)}, u32[]{:S(2)}) collective-permute-start(bf16[64,512]{1,0:T(8,128)(2,1)S(1)} %collective-permute-done.13), channel_id=1, source_target_pairs={{0,2},{1,3},{2,4},{3,5},{4,6},{5,7},{6,0},{7,1},{8,10},{9,11},{10,... | collective-permute-start | bytes 196616 | tf_op jit(solution)/shard_map/ppermute | solution.py:30
  31.3 7.7 %collective-permute-start.9 = (bf16[128,512]{1,0:T(8,128)(2,1)S(1)}, bf16[128,512]{1,0:T(8,128)(2,1)S(1)}, u32[]{:S(2)}, u32[]{:S(2)}) collective-permute-start(bf16[128,512]{1,0:T(8,128)(2,1)S(1)} %collective-permute-done.6), channel_id=1, source_target_pairs={{0,14},{1,15},{2,0},{3,1},{4,10},{5,11},{6,4},{7,5},{8,6},{9,7},{1... | collective-permute-start | bytes 393224 | tf_op jit(solution)/shard_map/ppermute | solution.py:30
  32.7 6.3 %collective-permute-start.8 = (bf16[128,512]{1,0:T(8,128)(2,1)S(1)}, bf16[128,512]{1,0:T(8,128)(2,1)S(1)}, u32[]{:S(2)}, u32[]{:S(2)}) collective-permute-start(bf16[128,512]{1,0:T(8,128)(2,1)S(1)} %collective-permute-done.6), channel_id=1, source_target_pairs={{0,10},{1,11},{2,0},{3,1},{4,14},{5,15},{6,4},{7,5},{8,2},{9,3},{1... | collective-permute-start | bytes 393224 | tf_op jit(solution)/shard_map/ppermute | solution.py:30
  34.3 4.7 %collective-permute-start.7 = (bf16[128,512]{1,0:T(8,128)(2,1)S(1)}, bf16[128,512]{1,0:T(8,128)(2,1)S(1)}, u32[]{:S(2)}, u32[]{:S(2)}) collective-permute-start(bf16[128,512]{1,0:T(8,128)(2,1)S(1)} %collective-permute-done.6), channel_id=1, source_target_pairs={{0,6},{1,7},{2,0},{3,1},{4,2},{5,3},{6,4},{7,5},{8,14},{9,15},{10,... | collective-permute-start | bytes 393224 | tf_op jit(solution)/shard_map/ppermute | solution.py:30
  37.4 6.9 %collective-permute-start.18 = (bf16[64,2048]{1,0:T(8,128)(2,1)S(1)}, bf16[64,2048]{1,0:T(8,128)(2,1)S(1)}, u32[]{:S(2)}, u32[]{:S(2)}) collective-permute-start(bf16[64,2048]{1,0:T(8,128)(2,1)S(1)} %shard_map.109), channel_id=1, source_target_pairs={{0,3},{1,2},{2,0},{3,1},{4,7},{5,6},{6,4},{7,5},{8,11},{9,10},{10,... | collective-permute-start | bytes 786440 | tf_op jit(solution)/shard_map/ppermute | solution.py:30
  37.5 6.8 %collective-permute-start.17 = (bf16[64,2048]{1,0:T(8,128)(2,1)S(1)}, bf16[64,2048]{1,0:T(8,128)(2,1)S(1)}, u32[]{:S(2)}, u32[]{:S(2)}) collective-permute-start(bf16[64,2048]{1,0:T(8,128)(2,1)S(1)} %shard_map.109), channel_id=1, source_target_pairs={{0,2},{1,3},{2,0},{3,1},{4,6},{5,7},{6,4},{7,5},{8,10},{9,11},{10,... | collective-permute-start | bytes 786440 | tf_op jit(solution)/shard_map/ppermute | solution.py:30
  41.6 13.6 %collective-permute-start.11 = (bf16[64,2048]{1,0:T(8,128)(2,1)S(1)}, bf16[64,2048]{1,0:T(8,128)(2,1)S(1)}, u32[]{:S(2)}, u32[]{:S(2)}) collective-permute-start(bf16[64,2048]{1,0:T(8,128)(2,1)S(1)} %get-tuple-element.36), channel_id=1, source_target_pairs={{0,2},{1,3},{2,1},{3,0},{4,6},{5,7},{6,5},{7,4},{8,10},{9,11},{10,... | collective-permute-start | bytes 786440 | tf_op jit(solution)/shard_map/ppermute | solution.py:30
  45.1 1.3 %collective-permute-start.19 = (bf16[64,512]{1,0:T(8,128)(2,1)S(1)}, bf16[64,512]{1,0:T(8,128)(2,1)S(1)}, u32[]{:S(2)}, u32[]{:S(2)}) collective-permute-start(bf16[64,512]{1,0:T(8,128)(2,1)S(1)} %get-tuple-element.41.refs_4_), channel_id=1, source_target_pairs={{0,2},{1,3},{2,0},{3,1},{4,6},{5,7},{6,4},{7,5},{8,10},{9,11},{10,... | collective-permute-start | bytes 196616 | tf_op jit(solution)/shard_map/ppermute | solution.py:30
  46.4 3.0 %collective-permute-start.22 = (bf16[64,512]{1,0:T(8,128)(2,1)S(1)}, bf16[64,512]{1,0:T(8,128)(2,1)S(1)}, u32[]{:S(2)}, u32[]{:S(2)}) collective-permute-start(bf16[64,512]{1,0:T(8,128)(2,1)S(1)} %collective-permute-done.19), channel_id=1, source_target_pairs={{0,14},{1,15},{2,0},{3,1},{4,10},{5,11},{6,4},{7,5},{8,6},{9,7},{1... | collective-permute-start | bytes 196616 | tf_op jit(solution)/shard_map/ppermute | solution.py:30
  47.5 2.5 %collective-permute-start.21 = (bf16[64,512]{1,0:T(8,128)(2,1)S(1)}, bf16[64,512]{1,0:T(8,128)(2,1)S(1)}, u32[]{:S(2)}, u32[]{:S(2)}) collective-permute-start(bf16[64,512]{1,0:T(8,128)(2,1)S(1)} %collective-permute-done.19), channel_id=1, source_target_pairs={{0,10},{1,11},{2,0},{3,1},{4,14},{5,15},{6,4},{7,5},{8,2},{9,3},{1... | collective-permute-start | bytes 196616 | tf_op jit(solution)/shard_map/ppermute | solution.py:30
  47.5 3.2 %collective-permute-start.20 = (bf16[64,512]{1,0:T(8,128)(2,1)S(1)}, bf16[64,512]{1,0:T(8,128)(2,1)S(1)}, u32[]{:S(2)}, u32[]{:S(2)}) collective-permute-start(bf16[64,512]{1,0:T(8,128)(2,1)S(1)} %collective-permute-done.19), channel_id=1, source_target_pairs={{0,6},{1,7},{2,0},{3,1},{4,2},{5,3},{6,4},{7,5},{8,14},{9,15},{10,... | collective-permute-start | bytes 196616 | tf_op jit(solution)/shard_map/ppermute | solution.py:30
  52.9 5.1 %collective-permute-start.24 = (bf16[32,2048]{1,0:T(8,128)(2,1)S(1)}, bf16[32,2048]{1,0:T(8,128)(2,1)S(1)}, u32[]{:S(2)}, u32[]{:S(2)}) collective-permute-start(bf16[32,2048]{1,0:T(8,128)(2,1)S(1)} %get-tuple-element.45), channel_id=1, source_target_pairs={{0,2},{1,3},{2,1},{3,0},{4,6},{5,7},{6,5},{7,4},{8,10},{9,11},{10,... | collective-permute-start | bytes 393224 | tf_op jit(solution)/shard_map/ppermute | solution.py:30
  55.2 4.3 %collective-permute-start.12 = (bf16[64,2048]{1,0:T(8,128)(2,1)S(1)}, bf16[64,2048]{1,0:T(8,128)(2,1)S(1)}, u32[]{:S(2)}, u32[]{:S(2)}) collective-permute-start(bf16[64,2048]{1,0:T(8,128)(2,1)S(1)} %collective-permute-done.11.refs_2_), channel_id=1, source_target_pairs={{0,2},{1,3},{2,0},{3,1},{4,6},{5,7},{6,4},{7,5},{8,10},{9,11},{10,... | collective-permute-start | bytes 786440 | tf_op jit(solution)/shard_map/ppermute | solution.py:30
  55.3 4.2 %collective-permute-start.10 = (bf16[64,1024]{1,0:T(8,128)(2,1)S(1)}, bf16[64,1024]{1,0:T(8,128)(2,1)S(1)}, u32[]{:S(2)}, u32[]{:S(2)}) collective-permute-start(bf16[64,1024]{1,0:T(8,128)(2,1)S(1)} %get-tuple-element.35), channel_id=1, source_target_pairs={{0,2},{1,3},{2,0},{3,1},{4,6},{5,7},{6,4},{7,5},{8,10},{9,11},{10,... | collective-permute-start | bytes 393224 | tf_op jit(solution)/shard_map/ppermute | solution.py:30
  58.0 1.4 %collective-permute-start.25 = (bf16[32,2048]{1,0:T(8,128)(2,1)S(1)}, bf16[32,2048]{1,0:T(8,128)(2,1)S(1)}, u32[]{:S(2)}, u32[]{:S(2)}) collective-permute-start(bf16[32,2048]{1,0:T(8,128)(2,1)S(1)} %collective-permute-done.24.refs_6_), channel_id=1, source_target_pairs={{0,2},{1,3},{2,0},{3,1},{4,6},{5,7},{6,4},{7,5},{8,10},{9,11},{10,... | collective-permute-start | bytes 393224 | tf_op jit(solution)/shard_map/ppermute | solution.py:30
  58.0 1.4 %collective-permute-start.23 = (bf16[32,1024]{1,0:T(8,128)(2,1)S(1)}, bf16[32,1024]{1,0:T(8,128)(2,1)S(1)}, u32[]{:S(2)}, u32[]{:S(2)}) collective-permute-start(bf16[32,1024]{1,0:T(8,128)(2,1)S(1)} %get-tuple-element.44), channel_id=1, source_target_pairs={{0,2},{1,3},{2,0},{3,1},{4,6},{5,7},{6,4},{7,5},{8,10},{9,11},{10,... | collective-permute-start | bytes 196616 | tf_op jit(solution)/shard_map/ppermute | solution.py:30

commit v4 on v3

--- a/solution.py
+++ b/solution.py
@@ -48,6 +48,15 @@
 
 def place(axis):
     return lax.axis_index(axis).astype(jnp.int32)
+
+
+def in_turn(section, work, *outs):
+    pl.when(place("section") == section)(work)
+
+    @pl.when(place("section") != section)
+    def _():
+        for out in outs:
+            out[...] = jnp.zeros_like(out)
 
 
 def alive(at, length):
@@ -82,50 +91,73 @@
     x_hbm, gain_hbm, w_hbm, lgain_hbm, normed_ref, full_ref = refs[:6]
     latent_refs = refs[6 : 6 + len(spans)]
     x_ref, gain_ref, lgain_ref, w_ref, sems = refs[6 + len(spans) :]
-    copies = [
-        pltpu.make_async_copy(source, to, sems.at[i])
-        for i, (source, to) in enumerate(
-            ((x_hbm, x_ref), (gain_hbm, gain_ref), (lgain_hbm, lgain_ref))
-        )
-    ]
-    depth = w_ref.shape[0] // cuts
-    tiles = [slice(i * depth, (i + 1) * depth) for i in range(cuts)]
-    for i, tile in enumerate(tiles):
-        copies.append(pltpu.make_async_copy(w_hbm.at[tile], w_ref.at[tile], sems.at[3 + i]))
-    for copy in copies:
-        copy.start()
-    copies[0].wait()
-    copies[1].wait()
-    normed = rms(x_ref[...].astype(F32), gain_ref[...]).astype(BF16)
-    normed_ref[...] = normed
-    copies[2].wait()
-    raw = None
-    for i, tile in enumerate(tiles):
-        copies[3 + i].wait()
-        one = dot(normed[:, tile], w_ref[tile])
-        raw = one if raw is None else raw + one
-    full = rms(raw, lgain_ref[...])
-    full_ref[...] = full
-    latent = full.astype(BF16)
-    for (low, high), latent_ref in zip(spans, latent_refs):
-        latent_ref[...] = latent[low * rows : high * rows]
-
-
-def next_latent_body(span, rows, n_parts, *refs):
+
+    def work():
+        copies = [
+            pltpu.make_async_copy(source, to, sems.at[i])
+            for i, (source, to) in enumerate(
+                ((x_hbm, x_ref), (gain_hbm, gain_ref), (lgain_hbm, lgain_ref))
+            )
+        ]
+        depth = w_ref.shape[0] // cuts
+        tiles = [slice(i * depth, (i + 1) * depth) for i in range(cuts)]
+        for i, tile in enumerate(tiles):
+            copies.append(pltpu.make_async_copy(w_hbm.at[tile], w_ref.at[tile], sems.at[3 + i]))
+        for copy in copies:
+            copy.start()
+        copies[0].wait()
+        copies[1].wait()
+        normed = rms(x_ref[...].astype(F32), gain_ref[...]).astype(BF16)
+        normed_ref[...] = normed
+        copies[2].wait()
+        raw = None
+        for i, tile in enumerate(tiles):
+            copies[3 + i].wait()
+            one = dot(normed[:, tile], w_ref[tile])
+            raw = one if raw is None else raw + one
+        full = rms(raw, lgain_ref[...])
+        full_ref[...] = full
+        latent = full.astype(BF16)
+        for (low, high), latent_ref in zip(spans, latent_refs):
+            latent_ref[...] = latent[low * rows : high * rows]
+
+    in_turn(0, work, normed_ref, full_ref, *latent_refs)
+
+
+def next_latent_body(span, hands, rows, n_head, *refs):
     x_ref = refs[0]
-    parts = refs[1 : 1 + n_parts]
-    refs = refs[1 + n_parts :]
+    parts = refs[1 : 1 + n_head * len(hands)]
+    refs = refs[1 + n_head * len(hands) :]
     gain_ref, w_ref, lgain_ref, before_ref, live_ref = refs[:5]
     state_ref, normed_ref, stored_ref, latent_ref = refs[5:]
     at = slice(span[0] * rows, span[1] * rows)
-    state = x_ref[at].astype(F32) + tree_sum([p[...] for p in parts])
-    state_ref[...] = state
-    normed = rms(state, gain_ref[...]).astype(BF16)
-    normed_ref[...] = normed
-    full = rms(dot(normed, w_ref[...]), lgain_ref[...])
-    latent_ref[...] = full.astype(BF16)
-    second = jnp.broadcast_to(place("section"), full.shape) == 1
-    stored_ref[...] = keep_live(jnp.where(second, full, before_ref[at]), live_ref[at])
+
+    def work():
+        states = []
+        for i, (low, high) in enumerate(hands):
+            terms = [p[...] for p in parts[i * n_head : (i + 1) * n_head]]
+            states.append(x_ref[low * rows : high * rows].astype(F32) + tree_sum(terms))
+        state = jnp.concatenate(states, axis=0)
+        state_ref[...] = state
+        normed = rms(state, gain_ref[...]).astype(BF16)
+        normed_ref[...] = normed
+        full = rms(dot(normed, w_ref[...]), lgain_ref[...])
+        latent_ref[...] = full.astype(BF16)
+        stored_ref[...] = keep_live(full, live_ref[at])
+
+    in_turn(1, work, state_ref, normed_ref, latent_ref)
+
+    @pl.when(place("section") == 0)
+    def _():
+        stored_ref[...] = keep_live(before_ref[at], live_ref[at])
+
+
+def wide_dot(a, b):
+    extra = 128 - a.shape[0]
+    if extra <= 0:
+        return dot(a, b)
+    padded = jnp.concatenate([a, jnp.zeros((extra, a.shape[1]), a.dtype)], axis=0)
+    return dot(padded, b)[: a.shape[0]]
 
 
 def absorb(scale, query, wk, out_ref):
@@ -135,39 +167,24 @@
         out_ref[h] = (one * scale).astype(BF16)
 
 
-def first_query_body(scale, cuts, normed_ref, wq_hbm, wk_hbm, out_ref, wq, wk, sems):
-    depth = wq.shape[0] // cuts
-    tiles = [slice(i * depth, (i + 1) * depth) for i in range(cuts)]
-    copies = [
-        pltpu.make_async_copy(wq_hbm.at[tile], wq.at[tile], sems.at[i])
-        for i, tile in enumerate(tiles)
-    ]
-    copies.append(pltpu.make_async_copy(wk_hbm, wk, sems.at[cuts]))
-    for copy in copies:
-        copy.start()
-    query = None
-    for i, tile in enumerate(tiles):
-        copies[i].wait()
-        one = dot(normed_ref[:, tile], wq[tile])
-        query = one if query is None else query + one
-    copies[cuts].wait()
-    absorb(scale, query.astype(BF16), wk, out_ref)
-
-
-def query_body(scale, normed_ref, wq_ref, wk_ref, out_ref):
-    absorb(scale, dot(normed_ref[...], wq_ref[...]).astype(BF16), wk_ref, out_ref)
-
-
-def attention(spans, rows, n_pieces, offset, absorbed_ref, bias_ref, pieces, wv, kv, ctx, attn):
+def query_body(scale, section, normed_ref, wq_ref, wk_ref, out_ref):
+    def work():
+        query = wide_dot(normed_ref[...], wq_ref[...]).astype(BF16)
+        absorb(scale, query, wk_ref, out_ref)
+
+    in_turn(section, work, out_ref)
+
+
+def attention(spans, own, rows, n_pieces, offset, absorbed_ref, bias_ref, pieces, wv, kv, ctx, attn):
     heads = absorbed_ref.shape[0]
     rank = kv.shape[1]
     block = n_pieces * rows
     for i, (low, high) in enumerate(spans):
-        for g in range(low, high):
+        for g in range(low, min(high, own[1])):
             for k in range(n_pieces):
                 piece = pieces[i * n_pieces + k]
                 kv[pl.ds(g * block + k * rows, rows), :] = piece[pl.ds((g - low) * rows, rows), :]
-    low, high = spans[-1]
+    low, high = own
     causal = bias_ref[:, bias_ref.shape[1] - block :]
     for g in range(low, high):
         keys = kv[: (g + 1) * block, :]
@@ -187,38 +204,50 @@
         attn[:, cols] = dot(ctx[h], wv[:, cols]).astype(BF16)
 
 
-def attend_body(spans, rows, n_pieces, offset, absorbed_ref, bias_ref, *refs):
+def attend_body(spans, own, rows, n_pieces, offset, absorbed_ref, bias_ref, *refs):
     n_in = len(spans) * n_pieces
     pieces = refs[:n_in]
     wv, wo, out_ref, kv, ctx, attn = refs[n_in:]
-    attention(spans, rows, n_pieces, offset, absorbed_ref, bias_ref, pieces, wv, kv, ctx, attn)
-    out_ref[...] = dot(attn[...], wo[...]).astype(BF16)
-
-
-def attend_last_body(spans, rows, n_pieces, offset, n_head, n_sec, absorbed_ref, bias_ref, *refs):
+
+    def work():
+        attention(
+            spans, own, rows, n_pieces, offset, absorbed_ref, bias_ref, pieces, wv, kv, ctx, attn
+        )
+        out_ref[...] = dot(attn[...], wo[...]).astype(BF16)
+
+    in_turn(0, work, out_ref)
+
+
+def attend_last_body(spans, own, rows, n_pieces, offset, n_head, n_sec, absorbed_ref, bias_ref, *refs):
     n_in = len(spans) * n_pieces
     pieces = refs[:n_in]
     wv, wo, state_ref, keep_ref, give_ref = refs[n_in : n_in + 5]
     sends = refs[n_in + 5 : n_in + 4 + n_head]
     kv, ctx, attn, total = refs[n_in + 4 + n_head :]
-    attention(spans, rows, n_pieces, offset, absorbed_ref, bias_ref, pieces, wv, kv, ctx, attn)
-    total[...] = dot(attn[...], wo[...])
-    low, high = spans[-1]
-    share = rows // n_head
-    width = total.shape[1]
-    part = width // n_sec
-    head = place("head")
-    for g in range(high - low):
-        to = slice(g * share, (g + 1) * share)
-
-        def at(h):
-            return pl.ds(pl.multiple_of(g * rows + h * share, share), share)
-
-        mine = state_ref[at(head), :] + total[at(head), :]
-        give_ref[to] = mine[:, : width - part].astype(BF16)
-        keep_ref[to] = mine[:, width - part :]
-        for k in range(1, n_head):
-            sends[k - 1][to] = total[at(jnp.bitwise_xor(head, k)), :].astype(BF16)
+
+    def work():
+        attention(
+            spans, own, rows, n_pieces, offset, absorbed_ref, bias_ref, pieces, wv, kv, ctx, attn
+        )
+        total[...] = dot(attn[...], wo[...])
+        low, high = own
+        share = rows // n_head
+        width = total.shape[1]
+        part = width // n_sec
+        head = place("head")
+        for g in range(high - low):
+            to = slice(g * share, (g + 1) * share)
+
+            def at(h):
+                return pl.ds(pl.multiple_of(g * rows + h * share, share), share)
+
+            mine = state_ref[at(head), :] + total[at(head), :]
+            give_ref[to] = mine[:, : width - part].astype(BF16)
+            keep_ref[to] = mine[:, width - part :]
+            for k in range(1, n_head):
+                sends[k - 1][to] = total[at(jnp.bitwise_xor(head, k)), :].astype(BF16)
+
+    in_turn(n_sec - 1, work, keep_ref, give_ref, *sends)
 
 
 def final_body(spans, rows, n_head, n_sec, final_ref, *refs):
@@ -250,6 +279,13 @@
     return pltpu.CompilerParams(vmem_limit_bytes=limit * MIB)
 
 
+def plan(groups):
+    cut = max(1, groups - 1)
+    two = [(0, cut), (cut, groups)] if cut < groups else [(0, groups)]
+    each = [(g, g + 1) for g in range(groups)]
+    return two, each, two
+
+
 def array(dtype, *shape):
     return jax.ShapeDtypeStruct(shape, dtype)
 
@@ -276,10 +312,11 @@
     part_width = width // n_sec
     x = hidden.reshape(total_rows, width)
     wl, wq, wk, wv, wo = w_latent[0], w_query[0], w_key[0], w_value[0], w_out[0]
-    cut = max(1, groups - 1)
     cuts = 4
-    spans = [(0, cut), (cut, groups)] if cut < groups else [(0, groups)]
-    span_size = [(high - low) * rows for low, high in spans]
+    firsts, hands, nexts = plan(groups)
+
+    def count(span):
+        return (span[1] - span[0]) * rows
 
     def prepare():
         return pl.pallas_call(
@@ -292,19 +329,20 @@
             in_specs=[SMEM],
             out_specs=(VMEM,) * 3,
             compiler_params=params(8),
+            cost_estimate=cost(6 * 10**9, 1 << 20),
             name="prepare",
-        )(lengths)
+        )(in_hbm(lengths))
 
     def first_latent():
         out = pl.pallas_call(
-            functools.partial(first_latent_body, spans, rows, cuts),
+            functools.partial(first_latent_body, firsts, rows, cuts),
             out_shape=(
                 array(BF16, total_rows, width),
                 array(F32, total_rows, rank),
-                *(array(BF16, size, rank) for size in span_size),
+                *(array(BF16, count(span), rank) for span in firsts),
             ),
             in_specs=[HBM] * 4,
-            out_specs=(VMEM,) * (2 + len(spans)),
+            out_specs=(VMEM,) * (2 + len(firsts)),
             scratch_shapes=[
                 pltpu.VMEM((total_rows, width), BF16),
                 pltpu.VMEM((1, width), F32),
@@ -318,9 +356,11 @@
         return out[0], out[1], list(out[2:])
 
     def next_latent(i, parts, before):
-        size = span_size[i]
+        span = nexts[i]
+        size = count(span)
+        inside = [hand for hand in hands if span[0] <= hand[0] < span[1]]
         return pl.pallas_call(
-            functools.partial(next_latent_body, spans[i], rows, len(parts)),
+            functools.partial(next_latent_body, span, inside, rows, n_head),
             out_shape=(
                 array(F32, size, width),
                 array(BF16, size, width),
@@ -333,10 +373,10 @@
             cost_estimate=cost(2 * size * width * rank, 2 * width * (rank + 2 * size)),
         )(x, *parts, attn_gain, wl, latent_gain, before, live)
 
-    def project(normed):
+    def project(section, normed):
         size = normed.shape[0]
         return pl.pallas_call(
-            functools.partial(query_body, 1.0 / HD**0.5),
+            functools.partial(query_body, 1.0 / HD**0.5, section),
             out_shape=array(BF16, heads, size, rank),
             in_specs=[VMEM] * 3,
             out_specs=VMEM,
@@ -346,29 +386,11 @@
             ),
         )(normed, wq, wk)
 
-    def first_project(normed):
-        size = normed.shape[0]
-        return pl.pallas_call(
-            functools.partial(first_query_body, 1.0 / HD**0.5, cuts),
-            out_shape=array(BF16, heads, size, rank),
-            in_specs=[VMEM, HBM, HBM],
-            out_specs=VMEM,
-            scratch_shapes=[
-                pltpu.VMEM((width, heads * HD), BF16),
-                pltpu.VMEM((rank, heads * HD), BF16),
-                pltpu.SemaphoreType.DMA((cuts + 1,)),
-            ],
-            compiler_params=params(14),
-            cost_estimate=cost(
-                2 * size * heads * HD * (width + rank), 2 * heads * HD * (width + rank + size)
-            ),
-        )(normed, in_hbm(wq), in_hbm(wk))
-
-    def attend(i, absorbed, offset, pieces, state=None):
-        which = spans[: i + 1]
-        high = spans[i][1]
-        size = span_size[i]
-        flat = [piece for of_span in pieces[: i + 1] for piece in of_span]
+    def attend(name, own, absorbed, offset, spans, pieces, state=None):
+        high = own[1]
+        size = count(own)
+        which = [span for span in spans if span[0] < high]
+        flat = [piece for of_span in pieces[: len(which)] for piece in of_span]
         scratch = [
             pltpu.VMEM((high * n_seq * rows, rank), BF16),
             pltpu.VMEM((heads, size, rank), BF16),
@@ -381,10 +403,11 @@
                 2 * heads * HD * (width + rank),
                 heads * size * high * n_seq * rows,
             ),
+            name=name,
         )
         if state is None:
             return pl.pallas_call(
-                functools.partial(attend_body, which, rows, n_seq, offset),
+                functools.partial(attend_body, which, own, rows, n_seq, offset),
                 out_shape=array(BF16, size, width),
                 in_specs=[VMEM] * (4 + len(flat)),
                 out_specs=VMEM,
@@ -393,7 +416,7 @@
             )(absorbed, bias, *flat, wv, wo)
         small = size // n_head
         return pl.pallas_call(
-            functools.partial(attend_last_body, which, rows, n_seq, offset, n_head, n_sec),
+            functools.partial(attend_last_body, which, own, rows, n_seq, offset, n_head, n_sec),
             out_shape=(
                 array(F32, small, part_width),
                 array(BF16, small, width - part_width),
@@ -428,27 +451,33 @@
     normed, full, latents = first_latent()
     pieces = [gather(latent, 0) for latent in latents]
     bias, live, final_live = prepare()
-    absorbed = first_project(normed)
-    parts = [hand_on(attend(i, absorbed, 0, pieces)) for i in range(len(spans))]
+    absorbed = project(0, normed)
+    parts = [
+        hand_on(attend(f"attend_0_{i}", own, absorbed, 0, firsts, pieces))
+        for i, own in enumerate(hands)
+    ]
     pieces, queries, states, lives = [], [], [], []
-    for i in range(len(spans)):
-        part = parts[i]
-        if i:
-            part = [after(p, queries[-1]) for p in part]
+    for i, span in enumerate(nexts):
+        part = []
+        for hand, one in zip(hands, parts):
+            if span[0] <= hand[0] < span[1]:
+                part += [after(p, queries[-1]) for p in one] if i else one
         state, normed, stored, latent = next_latent(i, part, full)
         states.append(state)
         lives.append(stored)
         pieces.append(gather(latent, 1))
-        queries.append(project(normed))
+        queries.append(project(1, normed))
     ends = []
-    for i in range(len(spans)):
-        keep, give, *sends = attend(i, queries[i], spans[i][0] * rows, pieces, states[i])
+    for i, own in enumerate(nexts):
+        keep, give, *sends = attend(
+            f"attend_1_{i}", own, queries[i], own[0] * rows, nexts, pieces, states[i]
+        )
         given = swap(give)
         came = [cross(sends[k - 1], 1, k) for k in range(1, n_head)]
         relay = [swap(one) for one in came]
         ends += [keep, given, *came, *relay]
     final = pl.pallas_call(
-        functools.partial(final_body, spans, rows, n_head, n_sec),
+        functools.partial(final_body, nexts, rows, n_head, n_sec),
         out_shape=array(F32, groups, share, part_width),
         in_specs=[VMEM] * (1 + len(ends)),
         out_specs=VMEM,

time: 60.5 us -> 59.2 us (0.979)
  Pallas kernels: 20.3 us -> 11.6 us
  starting transfers between devices: 20 us -> 26.8 us
  waiting for transfers between devices: 17.7 us -> 18.9 us
  local copies, waits for them, and re-layouts: 0.71 us -> 0.05 us
    pallas_call x11 -> x12, Pallas kernels: 19.7 us -> 10.9 us  [the longest x3 5.56 us: attend(): pl.pallas_call(functools.partial(attend_body, which, own, rows, n_seq, of...]
    ppermute x26 -> x28, starting transfers between devices: 20 us -> 26.8 us  [permute(): return lax.ppermute(value, AXES, pairs)]
    ppermute x26 -> x28, waiting for transfers between devices: 17.7 us -> 18.9 us  [permute(): return lax.ppermute(value, AXES, pairs)]
    unnamed x18 -> x16, local copies, waits for them, and re-layouts: 0.71 us -> 0.05 us
  transfers between devices with their start and end apart: 26 -> 28, of which waited for: 12 -> 14; matrix products, arithmetic and copies ran while one was open for 1% -> 1% of each run, Pallas kernels for 23% -> 11%
where the time goes in v4:
time: 59.2 us; the launch traced here: 59.1 us
  starting transfers between devices  26.8 us (45%)
  waiting for transfers between devices  18.9 us (32%)
  Pallas kernels  11.6 us (20%)
  between operations  0.89 us (2%)
  other arithmetic  0.77 us (1%)
    ppermute x28, starting transfers between devices, permute(): return lax.ppermute(value, AXES, pairs)  26.8 us
    ppermute x28, waiting for transfers between devices, permute(): return lax.ppermute(value, AXES, pairs)  18.9 us
    pallas_call x3, Pallas kernels, attend(): pl.pallas_call(functools.partial(attend_body, which, own, rows, n_seq, of...  5.56 us
    pallas_call x1, Pallas kernels, first_latent(): pl.pallas_call(functools.partial(first_latent_body, firsts, rows, cuts),...  2.36 us
    pallas_call x3, Pallas kernels, project(): pl.pallas_call(functools.partial(query_body, 1.0 / HD ** 0.5, section), o...  1.52 us
  transfers between devices with their start and end apart: 28, of which 14 were waited for; matrix products, arithmetic and copies ran while one was open for 1% of the time, Pallas kernels for 11%

profile of v4, /device:TPU:0, one launch (start us, length us, event | category | flops | bytes accessed | tf_op | source)
XLA Modules:
  0.0 59.1 jit_solution(8909335188366148988)
XLA Ops:
  0.6 2.4 %first_latent.1 = (bf16[192,2048]{1,0:T(8,128)(2,1)S(1)}, f32[192,512]{1,0:T(8,128)S(1)}, bf16[128,512]{1,0:T(8,128)(2,1)S(1)}, bf16[64,512]{1,0:T(8,128)(2,1)S(1)}) custom-call(bf16[192,2048]{1,0:T(8,128)(2,1)} %bitcast.26, f32[1,2048]{1,0:T(1,128)} %refs_3_.3, bf16[2048,512]{1,0:T(8,128)(2,1)} %bitcast.20, f32[1,512]{1,0:T(1,128)} %refs_5_.3), custom_call_target="tpu_custom_call" | custom-call | tf_op jit(solution)/shard_map/first_latent/pallas_call | solution.py:337
  3.0 0.1 collective-permute-start
  3.1 1.3 %collective-permute-done = bf16[128,512]{1,0:T(8,128)(2,1)S(1)} collective-permute-done((bf16[128,512]{1,0:T(8,128)(2,1)S(1)}, bf16[128,512]{1,0:T(8,128)(2,1)S(1)}, u32[]{:S(2)}, u32[]{:S(2)}) %collective-permute-start) | collective-permute-done | bytes 131104 | tf_op jit(solution)/shard_map/ppermute | solution.py:30
  4.4 0.1 collective-permute-start.3
  4.6 5.0 %collective-permute-start.2 = (bf16[128,512]{1,0:T(8,128)(2,1)S(1)}, bf16[128,512]{1,0:T(8,128)(2,1)S(1)}, u32[]{:S(2)}, u32[]{:S(2)}) collective-permute-start(bf16[128,512]{1,0:T(8,128)(2,1)S(1)} %collective-permute-done), channel_id=1, source_target_pairs={{0,2},{1,3},{2,8},{3,9},{4,6},{5,7},{6,12},{7,13},{8,10},{9,11},{1... | collective-permute-start | bytes 393224 | tf_op jit(solution)/shard_map/ppermute | solution.py:30
  9.6 0.7 %prepare.1 = (f32[64,1024]{1,0:T(8,128)S(1)}, f32[192,128]{1,0:T(8,128)S(1)}, f32[96,128]{1,0:T(8,128)S(1)}) custom-call(s32[3]{0:T(128)} %lengths_ref.1), custom_call_target="tpu_custom_call" | custom-call | flops 6000000000 | bytes 1048576 | tf_op jit(solution)/shard_map/prepare/pallas_call | solution.py:322
  10.4 1.4 %shard_map.104.absorbed_ref = bf16[8,192,512]{2,1,0:T(8,128)(2,1)S(1)} custom-call(bf16[192,2048]{1,0:T(8,128)(2,1)S(1)} %get-tuple-element.26.normed_ref, bf16[2048,1024]{1,0:T(8,128)(2,1)S(1)} %bitcast.12, bf16[512,1024]{1,0:T(8,128)(2,1)S(1)} %bitcast.23), custom_call_target="tpu_custom_call" | custom-call | flops 1006632960 | bytes 5636096 | tf_op jit(solution)/shard_map/pallas_call | solution.py:378
  11.8 0.2 collective-permute-done.3.refs_3_
  12.0 3.5 %collective-permute-done.2.refs_2_ = bf16[128,512]{1,0:T(8,128)(2,1)S(1)} collective-permute-done((bf16[128,512]{1,0:T(8,128)(2,1)S(1)}, bf16[128,512]{1,0:T(8,128)(2,1)S(1)}, u32[]{:S(2)}, u32[]{:S(2)}) %collective-permute-start.2) | collective-permute-done | bytes 131104 | tf_op jit(solution)/shard_map/ppermute | solution.py:30
  15.5 1.5 %attend_0_0.1 = bf16[64,2048]{1,0:T(8,128)(2,1)S(1)} custom-call(bf16[8,192,512]{2,1,0:T(8,128)(2,1)S(1)} %shard_map.104.absorbed_ref, f32[64,1024]{1,0:T(8,128)S(1)} %get-tuple-element.27.bias_ref, bf16[128,512]{1,0:T(8,128)(2,1)S(1)} %get-tuple-element.28.refs_0_, bf16[128,512]{1,0:T(8,128)(2,1)S(1)} %collective-permute-done.1.refs_1_, ...), custom_call_target="tpu_custom_call" | custom-call | flops 268435456 | bytes 5242880 | tf_op jit(solution)/shard_map/attend_0_0/pallas_call | solution.py:409
  17.1 0.1 collective-permute-start.5
  17.2 0.5 collective-permute-start.4
  17.7 1.8 %attend_0_1.1 = bf16[64,2048]{1,0:T(8,128)(2,1)S(1)} custom-call(bf16[8,192,512]{2,1,0:T(8,128)(2,1)S(1)} %shard_map.104.absorbed_ref, f32[64,1024]{1,0:T(8,128)S(1)} %get-tuple-element.27.bias_ref, bf16[128,512]{1,0:T(8,128)(2,1)S(1)} %get-tuple-element.28.refs_0_, bf16[128,512]{1,0:T(8,128)(2,1)S(1)} %collective-permute-done.1.refs_1_, ...), custom_call_target="tpu_custom_call" | custom-call | flops 536870912 | bytes 5242880 | tf_op jit(solution)/shard_map/attend_0_1/pallas_call | solution.py:409
  19.5 0.1 collective-permute-start.7
  19.6 0.5 collective-permute-start.6
  20.1 1.0 %collective-permute-done.5.refs_2_ = bf16[64,2048]{1,0:T(8,128)(2,1)S(1)} collective-permute-done((bf16[64,2048]{1,0:T(8,128)(2,1)S(1)}, bf16[64,2048]{1,0:T(8,128)(2,1)S(1)}, u32[]{:S(2)}, u32[]{:S(2)}) %collective-permute-start.5) | collective-permute-done | bytes 262176 | tf_op jit(solution)/shard_map/ppermute | solution.py:30
  21.1 2.8 %collective-permute-done.7.refs_4_ = bf16[64,2048]{1,0:T(8,128)(2,1)S(1)} collective-permute-done((bf16[64,2048]{1,0:T(8,128)(2,1)S(1)}, bf16[64,2048]{1,0:T(8,128)(2,1)S(1)}, u32[]{:S(2)}, u32[]{:S(2)}) %collective-permute-start.7) | collective-permute-done | bytes 262176 | tf_op jit(solution)/shard_map/ppermute | solution.py:30
  23.9 0.2 shard_map.105
  24.2 2.5 %collective-permute-start.8 = (bf16[128,512]{1,0:T(8,128)(2,1)S(1)}, bf16[128,512]{1,0:T(8,128)(2,1)S(1)}, u32[]{:S(2)}, u32[]{:S(2)}) collective-permute-start(bf16[128,512]{1,0:T(8,128)(2,1)S(1)} %get-tuple-element.32.refs_0_), channel_id=1, source_target_pairs={{0,2},{1,3},{2,0},{3,1},{4,6},{5,7},{6,4},{7,5},{8,10},{9,11},{10,... | collective-permute-start | bytes 393224 | tf_op jit(solution)/shard_map/ppermute | solution.py:30
  26.6 0.1 collective-permute-start.15
  26.7 1.2 %collective-permute-done.15 = bf16[64,512]{1,0:T(8,128)(2,1)S(1)} collective-permute-done((bf16[64,512]{1,0:T(8,128)(2,1)S(1)}, bf16[64,512]{1,0:T(8,128)(2,1)S(1)}, u32[]{:S(2)}, u32[]{:S(2)}) %collective-permute-start.15) | collective-permute-done | bytes 65568 | tf_op jit(solution)/shard_map/ppermute | solution.py:30
  27.9 0.2 collective-permute-start.18
  28.1 2.5 %collective-permute-start.17 = (bf16[64,512]{1,0:T(8,128)(2,1)S(1)}, bf16[64,512]{1,0:T(8,128)(2,1)S(1)}, u32[]{:S(2)}, u32[]{:S(2)}) collective-permute-start(bf16[64,512]{1,0:T(8,128)(2,1)S(1)} %collective-permute-done.15), channel_id=1, source_target_pairs={{0,2},{1,3},{2,8},{3,9},{4,6},{5,7},{6,12},{7,13},{8,10},{9,11},{1... | collective-permute-start | bytes 196616 | tf_op jit(solution)/shard_map/ppermute | solution.py:30
  30.5 1.4 %collective-permute-start.11 = (bf16[128,512]{1,0:T(8,128)(2,1)S(1)}, bf16[128,512]{1,0:T(8,128)(2,1)S(1)}, u32[]{:S(2)}, u32[]{:S(2)}) collective-permute-start(bf16[128,512]{1,0:T(8,128)(2,1)S(1)} %collective-permute-done.8), channel_id=1, source_target_pairs={{0,14},{1,15},{2,0},{3,1},{4,10},{5,11},{6,4},{7,5},{8,6},{9,7},{1... | collective-permute-start | bytes 393224 | tf_op jit(solution)/shard_map/ppermute | solution.py:30
  31.9 0.2 collective-permute-start.10
  32.1 1.4 %collective-permute-done.18.refs_7_ = bf16[64,512]{1,0:T(8,128)(2,1)S(1)} collective-permute-done((bf16[64,512]{1,0:T(8,128)(2,1)S(1)}, bf16[64,512]{1,0:T(8,128)(2,1)S(1)}, u32[]{:S(2)}, u32[]{:S(2)}) %collective-permute-start.18) | collective-permute-done | bytes 65568 | tf_op jit(solution)/shard_map/ppermute | solution.py:30
  33.5 0.9 %collective-permute-done.17.refs_6_ = bf16[64,512]{1,0:T(8,128)(2,1)S(1)} collective-permute-done((bf16[64,512]{1,0:T(8,128)(2,1)S(1)}, bf16[64,512]{1,0:T(8,128)(2,1)S(1)}, u32[]{:S(2)}, u32[]{:S(2)}) %collective-permute-start.17) | collective-permute-done | bytes 65568 | tf_op jit(solution)/shard_map/ppermute | solution.py:30
  34.4 2.2 %attend_0_2.1 = bf16[64,2048]{1,0:T(8,128)(2,1)S(1)} custom-call(bf16[8,192,512]{2,1,0:T(8,128)(2,1)S(1)} %shard_map.104.absorbed_ref, f32[64,1024]{1,0:T(8,128)S(1)} %get-tuple-element.27.bias_ref, bf16[128,512]{1,0:T(8,128)(2,1)S(1)} %get-tuple-element.28.refs_0_, bf16[128,512]{1,0:T(8,128)(2,1)S(1)} %collective-permute-done.1.refs_1_, ...), custom_call_target="tpu_custom_call" | custom-call | flops 805306368 | bytes 5242880 | tf_op jit(solution)/shard_map/attend_0_2/pallas_call | solution.py:409
  36.6 0.1 collective-permute-start.20
  36.7 0.5 collective-permute-start.19
  37.2 0.1 shard_map.106.absorbed_ref
  37.3 0.2 attend_1_0.1
  37.6 5.8 %collective-permute-start.13 = (bf16[64,2048]{1,0:T(8,128)(2,1)S(1)}, bf16[64,2048]{1,0:T(8,128)(2,1)S(1)}, u32[]{:S(2)}, u32[]{:S(2)}) collective-permute-start(bf16[64,2048]{1,0:T(8,128)(2,1)S(1)} %get-tuple-element.36), channel_id=1, source_target_pairs={{0,2},{1,3},{2,1},{3,0},{4,6},{5,7},{6,5},{7,4},{8,10},{9,11},{10,... | collective-permute-start | bytes 786440 | tf_op jit(solution)/shard_map/ppermute | solution.py:30
  43.3 0.1 shard_map.107
  43.5 0.7 %collective-permute-start.21 = (bf16[64,512]{1,0:T(8,128)(2,1)S(1)}, bf16[64,512]{1,0:T(8,128)(2,1)S(1)}, u32[]{:S(2)}, u32[]{:S(2)}) collective-permute-start(bf16[64,512]{1,0:T(8,128)(2,1)S(1)} %get-tuple-element.41.refs_4_), channel_id=1, source_target_pairs={{0,2},{1,3},{2,0},{3,1},{4,6},{5,7},{6,4},{7,5},{8,10},{9,11},{10,... | collective-permute-start | bytes 196616 | tf_op jit(solution)/shard_map/ppermute | solution.py:30
  44.2 0.9 %collective-permute-done.21 = bf16[64,512]{1,0:T(8,128)(2,1)S(1)} collective-permute-done((bf16[64,512]{1,0:T(8,128)(2,1)S(1)}, bf16[64,512]{1,0:T(8,128)(2,1)S(1)}, u32[]{:S(2)}, u32[]{:S(2)}) %collective-permute-start.21) | collective-permute-done | bytes 65568 | tf_op jit(solution)/shard_map/ppermute | solution.py:30
  45.1 1.3 %collective-permute-start.24 = (bf16[64,512]{1,0:T(8,128)(2,1)S(1)}, bf16[64,512]{1,0:T(8,128)(2,1)S(1)}, u32[]{:S(2)}, u32[]{:S(2)}) collective-permute-start(bf16[64,512]{1,0:T(8,128)(2,1)S(1)} %collective-permute-done.21), channel_id=1, source_target_pairs={{0,14},{1,15},{2,0},{3,1},{4,10},{5,11},{6,4},{7,5},{8,6},{9,7},{1... | collective-permute-start | bytes 196616 | tf_op jit(solution)/shard_map/ppermute | solution.py:30
  46.4 1.9 %collective-permute-done.24.refs_7_ = bf16[64,512]{1,0:T(8,128)(2,1)S(1)} collective-permute-done((bf16[64,512]{1,0:T(8,128)(2,1)S(1)}, bf16[64,512]{1,0:T(8,128)(2,1)S(1)}, u32[]{:S(2)}, u32[]{:S(2)}) %collective-permute-start.24) | collective-permute-done | bytes 65568 | tf_op jit(solution)/shard_map/ppermute | solution.py:30
  48.3 0.6 %collective-permute-done.23.refs_6_ = bf16[64,512]{1,0:T(8,128)(2,1)S(1)} collective-permute-done((bf16[64,512]{1,0:T(8,128)(2,1)S(1)}, bf16[64,512]{1,0:T(8,128)(2,1)S(1)}, u32[]{:S(2)}, u32[]{:S(2)}) %collective-permute-start.23) | collective-permute-done | bytes 65568 | tf_op jit(solution)/shard_map/ppermute | solution.py:30
  48.9 0.7 %collective-permute-done.22.refs_5_ = bf16[64,512]{1,0:T(8,128)(2,1)S(1)} collective-permute-done((bf16[64,512]{1,0:T(8,128)(2,1)S(1)}, bf16[64,512]{1,0:T(8,128)(2,1)S(1)}, u32[]{:S(2)}, u32[]{:S(2)}) %collective-permute-start.22) | collective-permute-done | bytes 65568 | tf_op jit(solution)/shard_map/ppermute | solution.py:30
  49.6 4.3 %collective-permute-start.26 = (bf16[32,2048]{1,0:T(8,128)(2,1)S(1)}, bf16[32,2048]{1,0:T(8,128)(2,1)S(1)}, u32[]{:S(2)}, u32[]{:S(2)}) collective-permute-start(bf16[32,2048]{1,0:T(8,128)(2,1)S(1)} %get-tuple-element.45), channel_id=1, source_target_pairs={{0,2},{1,3},{2,1},{3,0},{4,6},{5,7},{6,5},{7,4},{8,10},{9,11},{10,... | collective-permute-start | bytes 393224 | tf_op jit(solution)/shard_map/ppermute | solution.py:30
  53.9 0.1 collective-permute-start.14
  54.0 0.4 collective-permute-start.12
  54.4 2.3 %collective-permute-done.26.refs_6_ = bf16[32,2048]{1,0:T(8,128)(2,1)S(1)} collective-permute-done((bf16[32,2048]{1,0:T(8,128)(2,1)S(1)}, bf16[32,2048]{1,0:T(8,128)(2,1)S(1)}, u32[]{:S(2)}, u32[]{:S(2)}) %collective-permute-start.26) | collective-permute-done | bytes 131104 | tf_op jit(solution)/shard_map/ppermute | solution.py:30
  56.7 0.5 collective-permute-start.25
  57.3 0.8 %pad_maximum_fusion = f32[192,512]{1,0:T(8,128)} fusion(f32[64,512]{1,0:T(8,128)S(1)} %get-tuple-element.47, f32[128,512]{1,0:T(8,128)S(1)} %get-tuple-element.46), kind=kLoop, calls=%fused_computation | loop fusion | flops 98304 | bytes 786432 | tf_op jit(solution)/shard_map/concatenate | solution.py:487
  58.0 0.2 collective-permute-done.25.refs_5_
  58.2 0.9 %final.1 = f32[3,32,1024]{2,1,0:T(8,128)} custom-call(f32[96,128]{1,0:T(8,128)S(1)} %get-tuple-element.25.final_ref, f32[64,1024]{1,0:T(8,128)S(1)} %get-tuple-element.34.refs_0_, bf16[64,1024]{1,0:T(8,128)(2,1)S(1)} %collective-permute-done.12.refs_1_, bf16[64,2048]{1,0:T(8,128)(2,1)S(1)} %collective-permute-done.13.refs_2_, ...), custom_call_target="tpu_custom_call" | custom-call | tf_op jit(solution)/shard_map/final/pallas_call | solution.py:479
  (38 shorter events, 0.2 us)
Async XLA Ops:
  3.0 7.4 %copy-start.1 = (bf16[1,2048,1024]{2,1,0:T(8,128)(2,1)S(1)}, bf16[1,2048,1024]{2,1,0:T(8,128)(2,1)}, u32[]{:S(2)}) copy-start(bf16[1,2048,1024]{2,1,0:T(8,128)(2,1)} %param.12) | copy-start | bytes 12582916
  3.0 7.4 %copy-start.4 = (bf16[1,512,1024]{2,1,0:T(8,128)(2,1)S(1)}, bf16[1,512,1024]{2,1,0:T(8,128)(2,1)}, u32[]{:S(2)}) copy-start(bf16[1,512,1024]{2,1,0:T(8,128)(2,1)} %param.15) | copy-start | bytes 3145732
  3.0 1.4 %collective-permute-start = (bf16[128,512]{1,0:T(8,128)(2,1)S(1)}, bf16[128,512]{1,0:T(8,128)(2,1)S(1)}, u32[]{:S(2)}, u32[]{:S(2)}) collective-permute-start(bf16[128,512]{1,0:T(8,128)(2,1)S(1)} %get-tuple-element.28.refs_0_), channel_id=1, source_target_pairs={{0,2},{1,3},{2,0},{3,1},{4,6},{5,7},{6,4},{7,5},{8,10},{9,11},{10,... | collective-permute-start | bytes 393224 | tf_op jit(solution)/shard_map/ppermute | solution.py:30
  4.4 7.6 %collective-permute-start.3 = (bf16[128,512]{1,0:T(8,128)(2,1)S(1)}, bf16[128,512]{1,0:T(8,128)(2,1)S(1)}, u32[]{:S(2)}, u32[]{:S(2)}) collective-permute-start(bf16[128,512]{1,0:T(8,128)(2,1)S(1)} %collective-permute-done), channel_id=1, source_target_pairs={{0,2},{1,3},{2,12},{3,13},{4,6},{5,7},{6,8},{7,9},{8,10},{9,11},{1... | collective-permute-start | bytes 393224 | tf_op jit(solution)/shard_map/ppermute | solution.py:30
  4.6 10.9 %collective-permute-start.2 = (bf16[128,512]{1,0:T(8,128)(2,1)S(1)}, bf16[128,512]{1,0:T(8,128)(2,1)S(1)}, u32[]{:S(2)}, u32[]{:S(2)}) collective-permute-start(bf16[128,512]{1,0:T(8,128)(2,1)S(1)} %collective-permute-done), channel_id=1, source_target_pairs={{0,2},{1,3},{2,8},{3,9},{4,6},{5,7},{6,12},{7,13},{8,10},{9,11},{1... | collective-permute-start | bytes 393224 | tf_op jit(solution)/shard_map/ppermute | solution.py:30
  9.6 5.9 %collective-permute-start.1 = (bf16[128,512]{1,0:T(8,128)(2,1)S(1)}, bf16[128,512]{1,0:T(8,128)(2,1)S(1)}, u32[]{:S(2)}, u32[]{:S(2)}) collective-permute-start(bf16[128,512]{1,0:T(8,128)(2,1)S(1)} %collective-permute-done), channel_id=1, source_target_pairs={{0,2},{1,3},{2,4},{3,5},{4,6},{5,7},{6,0},{7,1},{8,10},{9,11},{10,... | collective-permute-start | bytes 393224 | tf_op jit(solution)/shard_map/ppermute | solution.py:30
  10.3 5.2 %copy-start = (bf16[1,1024,2048]{2,1,0:T(8,128)(2,1)S(1)}, bf16[1,1024,2048]{2,1,0:T(8,128)(2,1)}, u32[]{:S(2)}) copy-start(bf16[1,1024,2048]{2,1,0:T(8,128)(2,1)} %param.17) | copy-start | bytes 12582916
  10.4 5.2 %copy-start.2 = (bf16[1,512,1024]{2,1,0:T(8,128)(2,1)S(1)}, bf16[1,512,1024]{2,1,0:T(8,128)(2,1)}, u32[]{:S(2)}) copy-start(bf16[1,512,1024]{2,1,0:T(8,128)(2,1)} %param.16) | copy-start | bytes 3145732
  17.1 6.8 %copy-start.3 = (bf16[1,2048,512]{2,1,0:T(8,128)(2,1)S(1)}, bf16[1,2048,512]{2,1,0:T(8,128)(2,1)}, u32[]{:S(2)}) copy-start(bf16[1,2048,512]{2,1,0:T(8,128)(2,1)} %param.13) | copy-start | bytes 6291460
  17.1 6.8 %copy-start.5 = (bf16[3,64,2048]{2,1,0:T(8,128)(2,1)S(1)}, bf16[3,64,2048]{2,1,0:T(8,128)(2,1)}, u32[]{:S(2)}) copy-start(bf16[3,64,2048]{2,1,0:T(8,128)(2,1)} %param.9) | copy-start | bytes 2359300
  17.1 6.8 %copy-start.6 = (f32[1,2048]{1,0:T(1,128)S(1)}, f32[1,2048]{1,0:T(1,128)}, u32[]{:S(2)}) copy-start(f32[1,2048]{1,0:T(1,128)} %refs_3_.3) | copy-start | bytes 24580
  17.1 6.8 %copy-start.7 = (f32[1,512]{1,0:T(1,128)S(1)}, f32[1,512]{1,0:T(1,128)}, u32[]{:S(2)}) copy-start(f32[1,512]{1,0:T(1,128)} %refs_5_.3) | copy-start | bytes 6148
  17.1 3.9 %collective-permute-start.5 = (bf16[64,2048]{1,0:T(8,128)(2,1)S(1)}, bf16[64,2048]{1,0:T(8,128)(2,1)S(1)}, u32[]{:S(2)}, u32[]{:S(2)}) collective-permute-start(bf16[64,2048]{1,0:T(8,128)(2,1)S(1)} %attend_0_0.1), channel_id=1, source_target_pairs={{0,3},{1,2},{2,0},{3,1},{4,7},{5,6},{6,4},{7,5},{8,11},{9,10},{10,... | collective-permute-start | bytes 786440 | tf_op jit(solution)/shard_map/ppermute | solution.py:30
  17.2 3.9 %collective-permute-start.4 = (bf16[64,2048]{1,0:T(8,128)(2,1)S(1)}, bf16[64,2048]{1,0:T(8,128)(2,1)S(1)}, u32[]{:S(2)}, u32[]{:S(2)}) collective-permute-start(bf16[64,2048]{1,0:T(8,128)(2,1)S(1)} %attend_0_0.1), channel_id=1, source_target_pairs={{0,2},{1,3},{2,0},{3,1},{4,6},{5,7},{6,4},{7,5},{8,10},{9,11},{10,... | collective-permute-start | bytes 786440 | tf_op jit(solution)/shard_map/ppermute | solution.py:30
  19.5 4.4 %collective-permute-start.7 = (bf16[64,2048]{1,0:T(8,128)(2,1)S(1)}, bf16[64,2048]{1,0:T(8,128)(2,1)S(1)}, u32[]{:S(2)}, u32[]{:S(2)}) collective-permute-start(bf16[64,2048]{1,0:T(8,128)(2,1)S(1)} %attend_0_1.1), channel_id=1, source_target_pairs={{0,3},{1,2},{2,0},{3,1},{4,7},{5,6},{6,4},{7,5},{8,11},{9,10},{10,... | collective-permute-start | bytes 786440 | tf_op jit(solution)/shard_map/ppermute | solution.py:30
  19.6 4.3 %collective-permute-start.6 = (bf16[64,2048]{1,0:T(8,128)(2,1)S(1)}, bf16[64,2048]{1,0:T(8,128)(2,1)S(1)}, u32[]{:S(2)}, u32[]{:S(2)}) collective-permute-start(bf16[64,2048]{1,0:T(8,128)(2,1)S(1)} %attend_0_1.1), channel_id=1, source_target_pairs={{0,2},{1,3},{2,0},{3,1},{4,6},{5,7},{6,4},{7,5},{8,10},{9,11},{10,... | collective-permute-start | bytes 786440 | tf_op jit(solution)/shard_map/ppermute | solution.py:30
  24.2 6.4 %collective-permute-start.8 = (bf16[128,512]{1,0:T(8,128)(2,1)S(1)}, bf16[128,512]{1,0:T(8,128)(2,1)S(1)}, u32[]{:S(2)}, u32[]{:S(2)}) collective-permute-start(bf16[128,512]{1,0:T(8,128)(2,1)S(1)} %get-tuple-element.32.refs_0_), channel_id=1, source_target_pairs={{0,2},{1,3},{2,0},{3,1},{4,6},{5,7},{6,4},{7,5},{8,10},{9,11},{10,... | collective-permute-start | bytes 393224 | tf_op jit(solution)/shard_map/ppermute | solution.py:30
  26.6 1.3 %collective-permute-start.15 = (bf16[64,512]{1,0:T(8,128)(2,1)S(1)}, bf16[64,512]{1,0:T(8,128)(2,1)S(1)}, u32[]{:S(2)}, u32[]{:S(2)}) collective-permute-start(bf16[64,512]{1,0:T(8,128)(2,1)S(1)} %get-tuple-element.37.refs_4_), channel_id=1, source_target_pairs={{0,2},{1,3},{2,0},{3,1},{4,6},{5,7},{6,4},{7,5},{8,10},{9,11},{10,... | collective-permute-start | bytes 196616 | tf_op jit(solution)/shard_map/ppermute | solution.py:30
  27.9 5.6 %collective-permute-start.18 = (bf16[64,512]{1,0:T(8,128)(2,1)S(1)}, bf16[64,512]{1,0:T(8,128)(2,1)S(1)}, u32[]{:S(2)}, u32[]{:S(2)}) collective-permute-start(bf16[64,512]{1,0:T(8,128)(2,1)S(1)} %collective-permute-done.15), channel_id=1, source_target_pairs={{0,2},{1,3},{2,12},{3,13},{4,6},{5,7},{6,8},{7,9},{8,10},{9,11},{1... | collective-permute-start | bytes 196616 | tf_op jit(solution)/shard_map/ppermute | solution.py:30
  28.1 6.3 %collective-permute-start.17 = (bf16[64,512]{1,0:T(8,128)(2,1)S(1)}, bf16[64,512]{1,0:T(8,128)(2,1)S(1)}, u32[]{:S(2)}, u32[]{:S(2)}) collective-permute-start(bf16[64,512]{1,0:T(8,128)(2,1)S(1)} %collective-permute-done.15), channel_id=1, source_target_pairs={{0,2},{1,3},{2,8},{3,9},{4,6},{5,7},{6,12},{7,13},{8,10},{9,11},{1... | collective-permute-start | bytes 196616 | tf_op jit(solution)/shard_map/ppermute | solution.py:30
  30.5 3.9 %collective-permute-start.16 = (bf16[64,512]{1,0:T(8,128)(2,1)S(1)}, bf16[64,512]{1,0:T(8,128)(2,1)S(1)}, u32[]{:S(2)}, u32[]{:S(2)}) collective-permute-start(bf16[64,512]{1,0:T(8,128)(2,1)S(1)} %collective-permute-done.15), channel_id=1, source_target_pairs={{0,2},{1,3},{2,4},{3,5},{4,6},{5,7},{6,0},{7,1},{8,10},{9,11},{10,... | collective-permute-start | bytes 196616 | tf_op jit(solution)/shard_map/ppermute | solution.py:30
  30.5 6.7 %collective-permute-start.11 = (bf16[128,512]{1,0:T(8,128)(2,1)S(1)}, bf16[128,512]{1,0:T(8,128)(2,1)S(1)}, u32[]{:S(2)}, u32[]{:S(2)}) collective-permute-start(bf16[128,512]{1,0:T(8,128)(2,1)S(1)} %collective-permute-done.8), channel_id=1, source_target_pairs={{0,14},{1,15},{2,0},{3,1},{4,10},{5,11},{6,4},{7,5},{8,6},{9,7},{1... | collective-permute-start | bytes 393224 | tf_op jit(solution)/shard_map/ppermute | solution.py:30
  31.9 5.4 %collective-permute-start.10 = (bf16[128,512]{1,0:T(8,128)(2,1)S(1)}, bf16[128,512]{1,0:T(8,128)(2,1)S(1)}, u32[]{:S(2)}, u32[]{:S(2)}) collective-permute-start(bf16[128,512]{1,0:T(8,128)(2,1)S(1)} %collective-permute-done.8), channel_id=1, source_target_pairs={{0,10},{1,11},{2,0},{3,1},{4,14},{5,15},{6,4},{7,5},{8,2},{9,3},{1... | collective-permute-start | bytes 393224 | tf_op jit(solution)/shard_map/ppermute | solution.py:30
  33.5 3.8 %collective-permute-start.9 = (bf16[128,512]{1,0:T(8,128)(2,1)S(1)}, bf16[128,512]{1,0:T(8,128)(2,1)S(1)}, u32[]{:S(2)}, u32[]{:S(2)}) collective-permute-start(bf16[128,512]{1,0:T(8,128)(2,1)S(1)} %collective-permute-done.8), channel_id=1, source_target_pairs={{0,6},{1,7},{2,0},{3,1},{4,2},{5,3},{6,4},{7,5},{8,14},{9,15},{10,... | collective-permute-start | bytes 393224 | tf_op jit(solution)/shard_map/ppermute | solution.py:30
  36.6 6.7 %collective-permute-start.20 = (bf16[64,2048]{1,0:T(8,128)(2,1)S(1)}, bf16[64,2048]{1,0:T(8,128)(2,1)S(1)}, u32[]{:S(2)}, u32[]{:S(2)}) collective-permute-start(bf16[64,2048]{1,0:T(8,128)(2,1)S(1)} %attend_0_2.1), channel_id=1, source_target_pairs={{0,3},{1,2},{2,0},{3,1},{4,7},{5,6},{6,4},{7,5},{8,11},{9,10},{10,... | collective-permute-start | bytes 786440 | tf_op jit(solution)/shard_map/ppermute | solution.py:30
  36.7 6.6 %collective-permute-start.19 = (bf16[64,2048]{1,0:T(8,128)(2,1)S(1)}, bf16[64,2048]{1,0:T(8,128)(2,1)S(1)}, u32[]{:S(2)}, u32[]{:S(2)}) collective-permute-start(bf16[64,2048]{1,0:T(8,128)(2,1)S(1)} %attend_0_2.1), channel_id=1, source_target_pairs={{0,2},{1,3},{2,0},{3,1},{4,6},{5,7},{6,4},{7,5},{8,10},{9,11},{10,... | collective-permute-start | bytes 786440 | tf_op jit(solution)/shard_map/ppermute | solution.py:30
  37.6 16.4 %collective-permute-start.13 = (bf16[64,2048]{1,0:T(8,128)(2,1)S(1)}, bf16[64,2048]{1,0:T(8,128)(2,1)S(1)}, u32[]{:S(2)}, u32[]{:S(2)}) collective-permute-start(bf16[64,2048]{1,0:T(8,128)(2,1)S(1)} %get-tuple-element.36), channel_id=1, source_target_pairs={{0,2},{1,3},{2,1},{3,0},{4,6},{5,7},{6,5},{7,4},{8,10},{9,11},{10,... | collective-permute-start | bytes 786440 | tf_op jit(solution)/shard_map/ppermute | solution.py:30
  43.5 1.6 %collective-permute-start.21 = (bf16[64,512]{1,0:T(8,128)(2,1)S(1)}, bf16[64,512]{1,0:T(8,128)(2,1)S(1)}, u32[]{:S(2)}, u32[]{:S(2)}) collective-permute-start(bf16[64,512]{1,0:T(8,128)(2,1)S(1)} %get-tuple-element.41.refs_4_), channel_id=1, source_target_pairs={{0,2},{1,3},{2,0},{3,1},{4,6},{5,7},{6,4},{7,5},{8,10},{9,11},{10,... | collective-permute-start | bytes 196616 | tf_op jit(solution)/shard_map/ppermute | solution.py:30
  45.1 3.2 %collective-permute-start.24 = (bf16[64,512]{1,0:T(8,128)(2,1)S(1)}, bf16[64,512]{1,0:T(8,128)(2,1)S(1)}, u32[]{:S(2)}, u32[]{:S(2)}) collective-permute-start(bf16[64,512]{1,0:T(8,128)(2,1)S(1)} %collective-permute-done.21), channel_id=1, source_target_pairs={{0,14},{1,15},{2,0},{3,1},{4,10},{5,11},{6,4},{7,5},{8,6},{9,7},{1... | collective-permute-start | bytes 196616 | tf_op jit(solution)/shard_map/ppermute | solution.py:30
  46.4 2.5 %collective-permute-start.23 = (bf16[64,512]{1,0:T(8,128)(2,1)S(1)}, bf16[64,512]{1,0:T(8,128)(2,1)S(1)}, u32[]{:S(2)}, u32[]{:S(2)}) collective-permute-start(bf16[64,512]{1,0:T(8,128)(2,1)S(1)} %collective-permute-done.21), channel_id=1, source_target_pairs={{0,10},{1,11},{2,0},{3,1},{4,14},{5,15},{6,4},{7,5},{8,2},{9,3},{1... | collective-permute-start | bytes 196616 | tf_op jit(solution)/shard_map/ppermute | solution.py:30
  46.4 3.2 %collective-permute-start.22 = (bf16[64,512]{1,0:T(8,128)(2,1)S(1)}, bf16[64,512]{1,0:T(8,128)(2,1)S(1)}, u32[]{:S(2)}, u32[]{:S(2)}) collective-permute-start(bf16[64,512]{1,0:T(8,128)(2,1)S(1)} %collective-permute-done.21), channel_id=1, source_target_pairs={{0,6},{1,7},{2,0},{3,1},{4,2},{5,3},{6,4},{7,5},{8,14},{9,15},{10,... | collective-permute-start | bytes 196616 | tf_op jit(solution)/shard_map/ppermute | solution.py:30
  49.6 7.1 %collective-permute-start.26 = (bf16[32,2048]{1,0:T(8,128)(2,1)S(1)}, bf16[32,2048]{1,0:T(8,128)(2,1)S(1)}, u32[]{:S(2)}, u32[]{:S(2)}) collective-permute-start(bf16[32,2048]{1,0:T(8,128)(2,1)S(1)} %get-tuple-element.45), channel_id=1, source_target_pairs={{0,2},{1,3},{2,1},{3,0},{4,6},{5,7},{6,5},{7,4},{8,10},{9,11},{10,... | collective-permute-start | bytes 393224 | tf_op jit(solution)/shard_map/ppermute | solution.py:30
  53.9 4.3 %collective-permute-start.14 = (bf16[64,2048]{1,0:T(8,128)(2,1)S(1)}, bf16[64,2048]{1,0:T(8,128)(2,1)S(1)}, u32[]{:S(2)}, u32[]{:S(2)}) collective-permute-start(bf16[64,2048]{1,0:T(8,128)(2,1)S(1)} %collective-permute-done.13.refs_2_), channel_id=1, source_target_pairs={{0,2},{1,3},{2,0},{3,1},{4,6},{5,7},{6,4},{7,5},{8,10},{9,11},{10,... | collective-permute-start | bytes 786440 | tf_op jit(solution)/shard_map/ppermute | solution.py:30
  54.0 4.2 %collective-permute-start.12 = (bf16[64,1024]{1,0:T(8,128)(2,1)S(1)}, bf16[64,1024]{1,0:T(8,128)(2,1)S(1)}, u32[]{:S(2)}, u32[]{:S(2)}) collective-permute-start(bf16[64,1024]{1,0:T(8,128)(2,1)S(1)} %get-tuple-element.35), channel_id=1, source_target_pairs={{0,2},{1,3},{2,0},{3,1},{4,6},{5,7},{6,4},{7,5},{8,10},{9,11},{10,... | collective-permute-start | bytes 393224 | tf_op jit(solution)/shard_map/ppermute | solution.py:30
  56.7 1.4 %collective-permute-start.27 = (bf16[32,2048]{1,0:T(8,128)(2,1)S(1)}, bf16[32,2048]{1,0:T(8,128)(2,1)S(1)}, u32[]{:S(2)}, u32[]{:S(2)}) collective-permute-start(bf16[32,2048]{1,0:T(8,128)(2,1)S(1)} %collective-permute-done.26.refs_6_), channel_id=1, source_target_pairs={{0,2},{1,3},{2,0},{3,1},{4,6},{5,7},{6,4},{7,5},{8,10},{9,11},{10,... | collective-permute-start | bytes 393224 | tf_op jit(solution)/shard_map/ppermute | solution.py:30
  56.7 1.4 %collective-permute-start.25 = (bf16[32,1024]{1,0:T(8,128)(2,1)S(1)}, bf16[32,1024]{1,0:T(8,128)(2,1)S(1)}, u32[]{:S(2)}, u32[]{:S(2)}) collective-permute-start(bf16[32,1024]{1,0:T(8,128)(2,1)S(1)} %get-tuple-element.44), channel_id=1, source_target_pairs={{0,2},{1,3},{2,0},{3,1},{4,6},{5,7},{6,4},{7,5},{8,10},{9,11},{10,... | collective-permute-start | bytes 196616 | tf_op jit(solution)/shard_map/ppermute | solution.py:30

commit v5 on v4

--- a/solution.py
+++ b/solution.py
@@ -436,14 +436,19 @@
             value, sizes, lambda s, c, h: (s, 1 - c, h ^ k) if c == source else (s, 1 - c, h)
         )
 
+    def flip(value, source, k):
+        return permute(
+            value, sizes, lambda s, c, h: (s ^ k, 1 - c, h) if c == source else (s, 1 - c, h)
+        )
+
     def gather(latent, tick):
-        there = swap(latent)
-        return [latent] + [
-            permute(
-                there, sizes, lambda s, c, h, k=k: (s, 1 - c, h) if c == tick else (s ^ k, tick, h)
-            )
-            for k in range(1, n_seq)
-        ]
+        if n_seq != 4:
+            there = swap(latent)
+            return [latent] + [flip(there, 1 - tick, k) for k in range(1, n_seq)]
+        far = flip(latent, tick, 2)
+        side = flip(latent, tick, 1)
+        turned = flip(far, 1 - tick, 1)
+        return [latent, swap(side), swap(far), turned]
 
     def hand_on(partial):
         return [swap(partial)] + [cross(partial, 0, k) for k in range(1, n_head)]

time: 59.2 us -> 57.6 us (0.973)
  waiting for transfers between devices: 18.9 us -> 12.9 us
  starting transfers between devices: 26.8 us -> 30.3 us
  local copies, waits for them, and re-layouts: 0.05 us -> 1.04 us
    ppermute x28 -> x32, waiting for transfers between devices: 18.9 us -> 12.9 us  [permute(): return lax.ppermute(value, AXES, pairs)]
    ppermute x28 -> x32, starting transfers between devices: 26.8 us -> 30.3 us  [permute(): return lax.ppermute(value, AXES, pairs)]
    unnamed x16, local copies, waits for them, and re-layouts: 0.05 us -> 1.04 us
  transfers between devices with their start and end apart: 28 -> 32, of which waited for: 14 -> 9; matrix products, arithmetic and copies ran while one was open for 1% -> 1% of each run, Pallas kernels for 11% -> 12%
where the time goes in v5:
time: 57.6 us; the launch traced here: 57.5 us
  starting transfers between devices  30.3 us (53%)
  waiting for transfers between devices  12.9 us (22%)
  Pallas kernels  11.6 us (20%)
  local copies, waits for them, and re-layouts  1.04 us (2%)
  between operations  0.91 us (2%)
  other arithmetic  0.77 us (1%)
    ppermute x32, starting transfers between devices, permute(): return lax.ppermute(value, AXES, pairs)  30.3 us
    ppermute x32, waiting for transfers between devices, permute(): return lax.ppermute(value, AXES, pairs)  12.9 us
    pallas_call x3, Pallas kernels, attend(): pl.pallas_call(functools.partial(attend_body, which, own, rows, n_seq, of...  5.55 us
    pallas_call x1, Pallas kernels, first_latent(): pl.pallas_call(functools.partial(first_latent_body, firsts, rows, cuts),...  2.36 us
    pallas_call x3, Pallas kernels, project(): pl.pallas_call(functools.partial(query_body, 1.0 / HD ** 0.5, section), o...  1.52 us
  transfers between devices with their start and end apart: 32, of which 9 were waited for; matrix products, arithmetic and copies ran while one was open for 1% of the time, Pallas kernels for 12%

profile of v5, /device:TPU:0, one launch (start us, length us, event | category | flops | bytes accessed | tf_op | source)
XLA Modules:
  0.0 57.5 jit_solution(12073260483372970698)
XLA Ops:
  0.6 2.4 %first_latent.1 = (bf16[192,2048]{1,0:T(8,128)(2,1)S(1)}, f32[192,512]{1,0:T(8,128)S(1)}, bf16[128,512]{1,0:T(8,128)(2,1)S(1)}, bf16[64,512]{1,0:T(8,128)(2,1)S(1)}) custom-call(bf16[192,2048]{1,0:T(8,128)(2,1)} %bitcast.26, f32[1,2048]{1,0:T(1,128)} %refs_3_.3, bf16[2048,512]{1,0:T(8,128)(2,1)} %bitcast.20, f32[1,512]{1,0:T(1,128)} %refs_5_.3), custom_call_target="tpu_custom_call" | custom-call | tf_op jit(solution)/shard_map/first_latent/pallas_call | solution.py:337
  3.0 1.4 %collective-permute-start.2 = (bf16[128,512]{1,0:T(8,128)(2,1)S(1)}, bf16[128,512]{1,0:T(8,128)(2,1)S(1)}, u32[]{:S(2)}, u32[]{:S(2)}) collective-permute-start(bf16[128,512]{1,0:T(8,128)(2,1)S(1)} %get-tuple-element.28.refs_0_), channel_id=1, source_target_pairs={{0,10},{1,11},{2,0},{3,1},{4,14},{5,15},{6,4},{7,5},{8,2},{9,3},{1... | collective-permute-start | bytes 393224 | tf_op jit(solution)/shard_map/ppermute | solution.py:30
  4.4 1.9 %collective-permute-start = (bf16[128,512]{1,0:T(8,128)(2,1)S(1)}, bf16[128,512]{1,0:T(8,128)(2,1)S(1)}, u32[]{:S(2)}, u32[]{:S(2)}) collective-permute-start(bf16[128,512]{1,0:T(8,128)(2,1)S(1)} %get-tuple-element.28.refs_0_), channel_id=1, source_target_pairs={{0,6},{1,7},{2,0},{3,1},{4,2},{5,3},{6,4},{7,5},{8,14},{9,15},{10,... | collective-permute-start | bytes 393224 | tf_op jit(solution)/shard_map/ppermute | solution.py:30
  6.2 0.7 %collective-permute-done.2 = bf16[128,512]{1,0:T(8,128)(2,1)S(1)} collective-permute-done((bf16[128,512]{1,0:T(8,128)(2,1)S(1)}, bf16[128,512]{1,0:T(8,128)(2,1)S(1)}, u32[]{:S(2)}, u32[]{:S(2)}) %collective-permute-start.2) | collective-permute-done | bytes 131104 | tf_op jit(solution)/shard_map/ppermute | solution.py:30
  6.9 4.5 %collective-permute-start.4 = (bf16[128,512]{1,0:T(8,128)(2,1)S(1)}, bf16[128,512]{1,0:T(8,128)(2,1)S(1)}, u32[]{:S(2)}, u32[]{:S(2)}) collective-permute-start(bf16[128,512]{1,0:T(8,128)(2,1)S(1)} %collective-permute-done.2), channel_id=1, source_target_pairs={{0,2},{1,3},{2,4},{3,5},{4,6},{5,7},{6,0},{7,1},{8,10},{9,11},{10,... | collective-permute-start | bytes 393224 | tf_op jit(solution)/shard_map/ppermute | solution.py:30
  11.4 0.5 collective-permute-start.1
  11.9 0.7 %prepare.1 = (f32[64,1024]{1,0:T(8,128)S(1)}, f32[192,128]{1,0:T(8,128)S(1)}, f32[96,128]{1,0:T(8,128)S(1)}) custom-call(s32[3]{0:T(128)} %lengths_ref.1), custom_call_target="tpu_custom_call" | custom-call | flops 6000000000 | bytes 1048576 | tf_op jit(solution)/shard_map/prepare/pallas_call | solution.py:322
  12.6 1.4 %shard_map.104.absorbed_ref = bf16[8,192,512]{2,1,0:T(8,128)(2,1)S(1)} custom-call(bf16[192,2048]{1,0:T(8,128)(2,1)S(1)} %get-tuple-element.26.normed_ref, bf16[2048,1024]{1,0:T(8,128)(2,1)S(1)} %bitcast.12, bf16[512,1024]{1,0:T(8,128)(2,1)S(1)} %bitcast.23), custom_call_target="tpu_custom_call" | custom-call | flops 1006632960 | bytes 5636096 | tf_op jit(solution)/shard_map/pallas_call | solution.py:378
  14.1 0.7 %copy-done = bf16[1,1024,2048]{2,1,0:T(8,128)(2,1)S(1)} copy-done((bf16[1,1024,2048]{2,1,0:T(8,128)(2,1)S(1)}, bf16[1,1024,2048]{2,1,0:T(8,128)(2,1)}, u32[]{:S(2)}) %copy-start) | copy-done | bytes 4194328
  14.8 0.3 copy-done.2
  15.1 1.5 %attend_0_0.1 = bf16[64,2048]{1,0:T(8,128)(2,1)S(1)} custom-call(bf16[8,192,512]{2,1,0:T(8,128)(2,1)S(1)} %shard_map.104.absorbed_ref, f32[64,1024]{1,0:T(8,128)S(1)} %get-tuple-element.27.bias_ref, bf16[128,512]{1,0:T(8,128)(2,1)S(1)} %get-tuple-element.28.refs_0_, bf16[128,512]{1,0:T(8,128)(2,1)S(1)} %collective-permute-done.1.refs_1_, ...), custom_call_target="tpu_custom_call" | custom-call | flops 268435456 | bytes 5242880 | tf_op jit(solution)/shard_map/attend_0_0/pallas_call | solution.py:409
  16.7 0.1 collective-permute-start.6
  16.7 0.5 collective-permute-start.5
  17.2 1.8 %attend_0_1.1 = bf16[64,2048]{1,0:T(8,128)(2,1)S(1)} custom-call(bf16[8,192,512]{2,1,0:T(8,128)(2,1)S(1)} %shard_map.104.absorbed_ref, f32[64,1024]{1,0:T(8,128)S(1)} %get-tuple-element.27.bias_ref, bf16[128,512]{1,0:T(8,128)(2,1)S(1)} %get-tuple-element.28.refs_0_, bf16[128,512]{1,0:T(8,128)(2,1)S(1)} %collective-permute-done.1.refs_1_, ...), custom_call_target="tpu_custom_call" | custom-call | flops 536870912 | bytes 5242880 | tf_op jit(solution)/shard_map/attend_0_1/pallas_call | solution.py:409
  19.0 0.1 collective-permute-start.8
  19.1 0.5 collective-permute-start.7
  19.6 1.0 %collective-permute-done.6.refs_2_ = bf16[64,2048]{1,0:T(8,128)(2,1)S(1)} collective-permute-done((bf16[64,2048]{1,0:T(8,128)(2,1)S(1)}, bf16[64,2048]{1,0:T(8,128)(2,1)S(1)}, u32[]{:S(2)}, u32[]{:S(2)}) %collective-permute-start.6) | collective-permute-done | bytes 262176 | tf_op jit(solution)/shard_map/ppermute | solution.py:30
  20.6 2.8 %collective-permute-done.8.refs_4_ = bf16[64,2048]{1,0:T(8,128)(2,1)S(1)} collective-permute-done((bf16[64,2048]{1,0:T(8,128)(2,1)S(1)}, bf16[64,2048]{1,0:T(8,128)(2,1)S(1)}, u32[]{:S(2)}, u32[]{:S(2)}) %collective-permute-start.8) | collective-permute-done | bytes 262176 | tf_op jit(solution)/shard_map/ppermute | solution.py:30
  23.4 0.2 shard_map.105
  23.7 2.5 %collective-permute-start.11 = (bf16[128,512]{1,0:T(8,128)(2,1)S(1)}, bf16[128,512]{1,0:T(8,128)(2,1)S(1)}, u32[]{:S(2)}, u32[]{:S(2)}) collective-permute-start(bf16[128,512]{1,0:T(8,128)(2,1)S(1)} %get-tuple-element.32.refs_0_), channel_id=1, source_target_pairs={{0,2},{1,3},{2,8},{3,9},{4,6},{5,7},{6,12},{7,13},{8,10},{9,11},{1... | collective-permute-start | bytes 393224 | tf_op jit(solution)/shard_map/ppermute | solution.py:30
  26.1 0.7 %collective-permute-start.19 = (bf16[64,512]{1,0:T(8,128)(2,1)S(1)}, bf16[64,512]{1,0:T(8,128)(2,1)S(1)}, u32[]{:S(2)}, u32[]{:S(2)}) collective-permute-start(bf16[64,512]{1,0:T(8,128)(2,1)S(1)} %get-tuple-element.37.refs_4_), channel_id=1, source_target_pairs={{0,10},{1,11},{2,0},{3,1},{4,14},{5,15},{6,4},{7,5},{8,2},{9,3},{1... | collective-permute-start | bytes 196616 | tf_op jit(solution)/shard_map/ppermute | solution.py:30
  26.9 1.7 %collective-permute-start.17 = (bf16[64,512]{1,0:T(8,128)(2,1)S(1)}, bf16[64,512]{1,0:T(8,128)(2,1)S(1)}, u32[]{:S(2)}, u32[]{:S(2)}) collective-permute-start(bf16[64,512]{1,0:T(8,128)(2,1)S(1)} %get-tuple-element.37.refs_4_), channel_id=1, source_target_pairs={{0,6},{1,7},{2,0},{3,1},{4,2},{5,3},{6,4},{7,5},{8,14},{9,15},{10,... | collective-permute-start | bytes 196616 | tf_op jit(solution)/shard_map/ppermute | solution.py:30
  28.6 0.2 collective-permute-done.19
  28.8 3.7 %collective-permute-start.21 = (bf16[64,512]{1,0:T(8,128)(2,1)S(1)}, bf16[64,512]{1,0:T(8,128)(2,1)S(1)}, u32[]{:S(2)}, u32[]{:S(2)}) collective-permute-start(bf16[64,512]{1,0:T(8,128)(2,1)S(1)} %collective-permute-done.19), channel_id=1, source_target_pairs={{0,2},{1,3},{2,4},{3,5},{4,6},{5,7},{6,0},{7,1},{8,10},{9,11},{10,... | collective-permute-start | bytes 196616 | tf_op jit(solution)/shard_map/ppermute | solution.py:30
  32.5 0.7 %collective-permute-start.18 = (bf16[64,512]{1,0:T(8,128)(2,1)S(1)}, bf16[64,512]{1,0:T(8,128)(2,1)S(1)}, u32[]{:S(2)}, u32[]{:S(2)}) collective-permute-start(bf16[64,512]{1,0:T(8,128)(2,1)S(1)} %collective-permute-done.17), channel_id=1, source_target_pairs={{0,2},{1,3},{2,0},{3,1},{4,6},{5,7},{6,4},{7,5},{8,10},{9,11},{10,... | collective-permute-start | bytes 196616 | tf_op jit(solution)/shard_map/ppermute | solution.py:30
  33.2 0.2 collective-permute-start.13
  33.3 0.9 %collective-permute-done.21.refs_7_ = bf16[64,512]{1,0:T(8,128)(2,1)S(1)} collective-permute-done((bf16[64,512]{1,0:T(8,128)(2,1)S(1)}, bf16[64,512]{1,0:T(8,128)(2,1)S(1)}, u32[]{:S(2)}, u32[]{:S(2)}) %collective-permute-start.21) | collective-permute-done | bytes 65568 | tf_op jit(solution)/shard_map/ppermute | solution.py:30
  34.2 0.5 collective-permute-start.10
  34.7 2.2 %attend_0_2.1 = bf16[64,2048]{1,0:T(8,128)(2,1)S(1)} custom-call(bf16[8,192,512]{2,1,0:T(8,128)(2,1)S(1)} %shard_map.104.absorbed_ref, f32[64,1024]{1,0:T(8,128)S(1)} %get-tuple-element.27.bias_ref, bf16[128,512]{1,0:T(8,128)(2,1)S(1)} %get-tuple-element.28.refs_0_, bf16[128,512]{1,0:T(8,128)(2,1)S(1)} %collective-permute-done.1.refs_1_, ...), custom_call_target="tpu_custom_call" | custom-call | flops 805306368 | bytes 5242880 | tf_op jit(solution)/shard_map/attend_0_2/pallas_call | solution.py:409
  36.9 0.1 collective-permute-start.23
  37.0 0.5 collective-permute-start.22
  37.5 0.1 shard_map.106.absorbed_ref
  37.6 0.2 attend_1_0.1
  37.8 3.6 %collective-permute-start.15 = (bf16[64,2048]{1,0:T(8,128)(2,1)S(1)}, bf16[64,2048]{1,0:T(8,128)(2,1)S(1)}, u32[]{:S(2)}, u32[]{:S(2)}) collective-permute-start(bf16[64,2048]{1,0:T(8,128)(2,1)S(1)} %get-tuple-element.36), channel_id=1, source_target_pairs={{0,2},{1,3},{2,1},{3,0},{4,6},{5,7},{6,5},{7,4},{8,10},{9,11},{10,... | collective-permute-start | bytes 786440 | tf_op jit(solution)/shard_map/ppermute | solution.py:30
  41.4 0.1 shard_map.107
  41.5 1.8 %collective-permute-start.26 = (bf16[64,512]{1,0:T(8,128)(2,1)S(1)}, bf16[64,512]{1,0:T(8,128)(2,1)S(1)}, u32[]{:S(2)}, u32[]{:S(2)}) collective-permute-start(bf16[64,512]{1,0:T(8,128)(2,1)S(1)} %get-tuple-element.41.refs_4_), channel_id=1, source_target_pairs={{0,2},{1,3},{2,8},{3,9},{4,6},{5,7},{6,12},{7,13},{8,10},{9,11},{1... | collective-permute-start | bytes 196616 | tf_op jit(solution)/shard_map/ppermute | solution.py:30
  43.3 0.6 %collective-permute-start.24 = (bf16[64,512]{1,0:T(8,128)(2,1)S(1)}, bf16[64,512]{1,0:T(8,128)(2,1)S(1)}, u32[]{:S(2)}, u32[]{:S(2)}) collective-permute-start(bf16[64,512]{1,0:T(8,128)(2,1)S(1)} %get-tuple-element.41.refs_4_), channel_id=1, source_target_pairs={{0,2},{1,3},{2,4},{3,5},{4,6},{5,7},{6,0},{7,1},{8,10},{9,11},{10,... | collective-permute-start | bytes 196616 | tf_op jit(solution)/shard_map/ppermute | solution.py:30
  43.9 3.7 %collective-permute-done.26 = bf16[64,512]{1,0:T(8,128)(2,1)S(1)} collective-permute-done((bf16[64,512]{1,0:T(8,128)(2,1)S(1)}, bf16[64,512]{1,0:T(8,128)(2,1)S(1)}, u32[]{:S(2)}, u32[]{:S(2)}) %collective-permute-start.26) | collective-permute-done | bytes 65568 | tf_op jit(solution)/shard_map/ppermute | solution.py:30
  47.6 0.5 collective-permute-start.27
  48.2 1.4 %collective-permute-done.28.refs_7_ = bf16[64,512]{1,0:T(8,128)(2,1)S(1)} collective-permute-done((bf16[64,512]{1,0:T(8,128)(2,1)S(1)}, bf16[64,512]{1,0:T(8,128)(2,1)S(1)}, u32[]{:S(2)}, u32[]{:S(2)}) %collective-permute-start.28) | collective-permute-done | bytes 65568 | tf_op jit(solution)/shard_map/ppermute | solution.py:30
  49.6 3.0 %collective-permute-start.30 = (bf16[32,2048]{1,0:T(8,128)(2,1)S(1)}, bf16[32,2048]{1,0:T(8,128)(2,1)S(1)}, u32[]{:S(2)}, u32[]{:S(2)}) collective-permute-start(bf16[32,2048]{1,0:T(8,128)(2,1)S(1)} %get-tuple-element.45), channel_id=1, source_target_pairs={{0,2},{1,3},{2,1},{3,0},{4,6},{5,7},{6,5},{7,4},{8,10},{9,11},{10,... | collective-permute-start | bytes 393224 | tf_op jit(solution)/shard_map/ppermute | solution.py:30
  52.5 0.1 collective-permute-start.16
  52.6 0.4 collective-permute-start.14
  53.0 2.1 %collective-permute-done.30.refs_6_ = bf16[32,2048]{1,0:T(8,128)(2,1)S(1)} collective-permute-done((bf16[32,2048]{1,0:T(8,128)(2,1)S(1)}, bf16[32,2048]{1,0:T(8,128)(2,1)S(1)}, u32[]{:S(2)}, u32[]{:S(2)}) %collective-permute-start.30) | collective-permute-done | bytes 131104 | tf_op jit(solution)/shard_map/ppermute | solution.py:30
  55.2 0.5 collective-permute-start.29
  55.7 0.8 %pad_maximum_fusion = f32[192,512]{1,0:T(8,128)} fusion(f32[64,512]{1,0:T(8,128)S(1)} %get-tuple-element.47, f32[128,512]{1,0:T(8,128)S(1)} %get-tuple-element.46), kind=kLoop, calls=%fused_computation | loop fusion | flops 98304 | bytes 786432 | tf_op jit(solution)/shard_map/concatenate | solution.py:492
  56.5 0.2 collective-permute-done.29.refs_5_
  56.6 0.9 %final.1 = f32[3,32,1024]{2,1,0:T(8,128)} custom-call(f32[96,128]{1,0:T(8,128)S(1)} %get-tuple-element.25.final_ref, f32[64,1024]{1,0:T(8,128)S(1)} %get-tuple-element.34.refs_0_, bf16[64,1024]{1,0:T(8,128)(2,1)S(1)} %collective-permute-done.14.refs_1_, bf16[64,2048]{1,0:T(8,128)(2,1)S(1)} %collective-permute-done.15.refs_2_, ...), custom_call_target="tpu_custom_call" | custom-call | tf_op jit(solution)/shard_map/final/pallas_call | solution.py:484
  (46 shorter events, 0.2 us)
Async XLA Ops:
  3.0 9.6 %copy-start.1 = (bf16[1,2048,1024]{2,1,0:T(8,128)(2,1)S(1)}, bf16[1,2048,1024]{2,1,0:T(8,128)(2,1)}, u32[]{:S(2)}) copy-start(bf16[1,2048,1024]{2,1,0:T(8,128)(2,1)} %param.12) | copy-start | bytes 12582916
  3.0 9.6 %copy-start.4 = (bf16[1,512,1024]{2,1,0:T(8,128)(2,1)S(1)}, bf16[1,512,1024]{2,1,0:T(8,128)(2,1)}, u32[]{:S(2)}) copy-start(bf16[1,512,1024]{2,1,0:T(8,128)(2,1)} %param.15) | copy-start | bytes 3145732
  3.0 3.9 %collective-permute-start.2 = (bf16[128,512]{1,0:T(8,128)(2,1)S(1)}, bf16[128,512]{1,0:T(8,128)(2,1)S(1)}, u32[]{:S(2)}, u32[]{:S(2)}) collective-permute-start(bf16[128,512]{1,0:T(8,128)(2,1)S(1)} %get-tuple-element.28.refs_0_), channel_id=1, source_target_pairs={{0,10},{1,11},{2,0},{3,1},{4,14},{5,15},{6,4},{7,5},{8,2},{9,3},{1... | collective-permute-start | bytes 393224 | tf_op jit(solution)/shard_map/ppermute | solution.py:30
  4.4 7.0 %collective-permute-start = (bf16[128,512]{1,0:T(8,128)(2,1)S(1)}, bf16[128,512]{1,0:T(8,128)(2,1)S(1)}, u32[]{:S(2)}, u32[]{:S(2)}) collective-permute-start(bf16[128,512]{1,0:T(8,128)(2,1)S(1)} %get-tuple-element.28.refs_0_), channel_id=1, source_target_pairs={{0,6},{1,7},{2,0},{3,1},{4,2},{5,3},{6,4},{7,5},{8,14},{9,15},{10,... | collective-permute-start | bytes 393224 | tf_op jit(solution)/shard_map/ppermute | solution.py:30
  6.9 7.1 %collective-permute-start.4 = (bf16[128,512]{1,0:T(8,128)(2,1)S(1)}, bf16[128,512]{1,0:T(8,128)(2,1)S(1)}, u32[]{:S(2)}, u32[]{:S(2)}) collective-permute-start(bf16[128,512]{1,0:T(8,128)(2,1)S(1)} %collective-permute-done.2), channel_id=1, source_target_pairs={{0,2},{1,3},{2,4},{3,5},{4,6},{5,7},{6,0},{7,1},{8,10},{9,11},{10,... | collective-permute-start | bytes 393224 | tf_op jit(solution)/shard_map/ppermute | solution.py:30
  11.4 2.7 %collective-permute-start.3 = (bf16[128,512]{1,0:T(8,128)(2,1)S(1)}, bf16[128,512]{1,0:T(8,128)(2,1)S(1)}, u32[]{:S(2)}, u32[]{:S(2)}) collective-permute-start(bf16[128,512]{1,0:T(8,128)(2,1)S(1)} %collective-permute-done.2), channel_id=1, source_target_pairs={{0,2},{1,3},{2,0},{3,1},{4,6},{5,7},{6,4},{7,5},{8,10},{9,11},{10,... | collective-permute-start | bytes 393224 | tf_op jit(solution)/shard_map/ppermute | solution.py:30
  11.4 2.7 %collective-permute-start.1 = (bf16[128,512]{1,0:T(8,128)(2,1)S(1)}, bf16[128,512]{1,0:T(8,128)(2,1)S(1)}, u32[]{:S(2)}, u32[]{:S(2)}) collective-permute-start(bf16[128,512]{1,0:T(8,128)(2,1)S(1)} %collective-permute-done), channel_id=1, source_target_pairs={{0,2},{1,3},{2,0},{3,1},{4,6},{5,7},{6,4},{7,5},{8,10},{9,11},{10,... | collective-permute-start | bytes 393224 | tf_op jit(solution)/shard_map/ppermute | solution.py:30
  12.6 2.2 %copy-start = (bf16[1,1024,2048]{2,1,0:T(8,128)(2,1)S(1)}, bf16[1,1024,2048]{2,1,0:T(8,128)(2,1)}, u32[]{:S(2)}) copy-start(bf16[1,1024,2048]{2,1,0:T(8,128)(2,1)} %param.17) | copy-start | bytes 12582916
  12.6 2.5 %copy-start.2 = (bf16[1,512,1024]{2,1,0:T(8,128)(2,1)S(1)}, bf16[1,512,1024]{2,1,0:T(8,128)(2,1)}, u32[]{:S(2)}) copy-start(bf16[1,512,1024]{2,1,0:T(8,128)(2,1)} %param.16) | copy-start | bytes 3145732
  16.6 6.8 %copy-start.3 = (bf16[1,2048,512]{2,1,0:T(8,128)(2,1)S(1)}, bf16[1,2048,512]{2,1,0:T(8,128)(2,1)}, u32[]{:S(2)}) copy-start(bf16[1,2048,512]{2,1,0:T(8,128)(2,1)} %param.13) | copy-start | bytes 6291460
  16.6 6.8 %copy-start.5 = (bf16[3,64,2048]{2,1,0:T(8,128)(2,1)S(1)}, bf16[3,64,2048]{2,1,0:T(8,128)(2,1)}, u32[]{:S(2)}) copy-start(bf16[3,64,2048]{2,1,0:T(8,128)(2,1)} %param.9) | copy-start | bytes 2359300
  16.6 6.8 %copy-start.6 = (f32[1,2048]{1,0:T(1,128)S(1)}, f32[1,2048]{1,0:T(1,128)}, u32[]{:S(2)}) copy-start(f32[1,2048]{1,0:T(1,128)} %refs_3_.3) | copy-start | bytes 24580
  16.7 6.8 %copy-start.7 = (f32[1,512]{1,0:T(1,128)S(1)}, f32[1,512]{1,0:T(1,128)}, u32[]{:S(2)}) copy-start(f32[1,512]{1,0:T(1,128)} %refs_5_.3) | copy-start | bytes 6148
  16.7 3.9 %collective-permute-start.6 = (bf16[64,2048]{1,0:T(8,128)(2,1)S(1)}, bf16[64,2048]{1,0:T(8,128)(2,1)S(1)}, u32[]{:S(2)}, u32[]{:S(2)}) collective-permute-start(bf16[64,2048]{1,0:T(8,128)(2,1)S(1)} %attend_0_0.1), channel_id=1, source_target_pairs={{0,3},{1,2},{2,0},{3,1},{4,7},{5,6},{6,4},{7,5},{8,11},{9,10},{10,... | collective-permute-start | bytes 786440 | tf_op jit(solution)/shard_map/ppermute | solution.py:30
  16.7 3.9 %collective-permute-start.5 = (bf16[64,2048]{1,0:T(8,128)(2,1)S(1)}, bf16[64,2048]{1,0:T(8,128)(2,1)S(1)}, u32[]{:S(2)}, u32[]{:S(2)}) collective-permute-start(bf16[64,2048]{1,0:T(8,128)(2,1)S(1)} %attend_0_0.1), channel_id=1, source_target_pairs={{0,2},{1,3},{2,0},{3,1},{4,6},{5,7},{6,4},{7,5},{8,10},{9,11},{10,... | collective-permute-start | bytes 786440 | tf_op jit(solution)/shard_map/ppermute | solution.py:30
  19.0 4.4 %collective-permute-start.8 = (bf16[64,2048]{1,0:T(8,128)(2,1)S(1)}, bf16[64,2048]{1,0:T(8,128)(2,1)S(1)}, u32[]{:S(2)}, u32[]{:S(2)}) collective-permute-start(bf16[64,2048]{1,0:T(8,128)(2,1)S(1)} %attend_0_1.1), channel_id=1, source_target_pairs={{0,3},{1,2},{2,0},{3,1},{4,7},{5,6},{6,4},{7,5},{8,11},{9,10},{10,... | collective-permute-start | bytes 786440 | tf_op jit(solution)/shard_map/ppermute | solution.py:30
  19.1 4.3 %collective-permute-start.7 = (bf16[64,2048]{1,0:T(8,128)(2,1)S(1)}, bf16[64,2048]{1,0:T(8,128)(2,1)S(1)}, u32[]{:S(2)}, u32[]{:S(2)}) collective-permute-start(bf16[64,2048]{1,0:T(8,128)(2,1)S(1)} %attend_0_1.1), channel_id=1, source_target_pairs={{0,2},{1,3},{2,0},{3,1},{4,6},{5,7},{6,4},{7,5},{8,10},{9,11},{10,... | collective-permute-start | bytes 786440 | tf_op jit(solution)/shard_map/ppermute | solution.py:30
  23.7 9.5 %collective-permute-start.11 = (bf16[128,512]{1,0:T(8,128)(2,1)S(1)}, bf16[128,512]{1,0:T(8,128)(2,1)S(1)}, u32[]{:S(2)}, u32[]{:S(2)}) collective-permute-start(bf16[128,512]{1,0:T(8,128)(2,1)S(1)} %get-tuple-element.32.refs_0_), channel_id=1, source_target_pairs={{0,2},{1,3},{2,8},{3,9},{4,6},{5,7},{6,12},{7,13},{8,10},{9,11},{1... | collective-permute-start | bytes 393224 | tf_op jit(solution)/shard_map/ppermute | solution.py:30
  26.1 2.6 %collective-permute-start.19 = (bf16[64,512]{1,0:T(8,128)(2,1)S(1)}, bf16[64,512]{1,0:T(8,128)(2,1)S(1)}, u32[]{:S(2)}, u32[]{:S(2)}) collective-permute-start(bf16[64,512]{1,0:T(8,128)(2,1)S(1)} %get-tuple-element.37.refs_4_), channel_id=1, source_target_pairs={{0,10},{1,11},{2,0},{3,1},{4,14},{5,15},{6,4},{7,5},{8,2},{9,3},{1... | collective-permute-start | bytes 196616 | tf_op jit(solution)/shard_map/ppermute | solution.py:30
  26.9 7.3 %collective-permute-start.9 = (bf16[128,512]{1,0:T(8,128)(2,1)S(1)}, bf16[128,512]{1,0:T(8,128)(2,1)S(1)}, u32[]{:S(2)}, u32[]{:S(2)}) collective-permute-start(bf16[128,512]{1,0:T(8,128)(2,1)S(1)} %get-tuple-element.32.refs_0_), channel_id=1, source_target_pairs={{0,2},{1,3},{2,4},{3,5},{4,6},{5,7},{6,0},{7,1},{8,10},{9,11},{10,... | collective-permute-start | bytes 393224 | tf_op jit(solution)/shard_map/ppermute | solution.py:30
  26.9 5.6 %collective-permute-start.17 = (bf16[64,512]{1,0:T(8,128)(2,1)S(1)}, bf16[64,512]{1,0:T(8,128)(2,1)S(1)}, u32[]{:S(2)}, u32[]{:S(2)}) collective-permute-start(bf16[64,512]{1,0:T(8,128)(2,1)S(1)} %get-tuple-element.37.refs_4_), channel_id=1, source_target_pairs={{0,6},{1,7},{2,0},{3,1},{4,2},{5,3},{6,4},{7,5},{8,14},{9,15},{10,... | collective-permute-start | bytes 196616 | tf_op jit(solution)/shard_map/ppermute | solution.py:30
  28.8 5.4 %collective-permute-start.21 = (bf16[64,512]{1,0:T(8,128)(2,1)S(1)}, bf16[64,512]{1,0:T(8,128)(2,1)S(1)}, u32[]{:S(2)}, u32[]{:S(2)}) collective-permute-start(bf16[64,512]{1,0:T(8,128)(2,1)S(1)} %collective-permute-done.19), channel_id=1, source_target_pairs={{0,2},{1,3},{2,4},{3,5},{4,6},{5,7},{6,0},{7,1},{8,10},{9,11},{10,... | collective-permute-start | bytes 196616 | tf_op jit(solution)/shard_map/ppermute | solution.py:30
  32.5 2.2 %collective-permute-start.20 = (bf16[64,512]{1,0:T(8,128)(2,1)S(1)}, bf16[64,512]{1,0:T(8,128)(2,1)S(1)}, u32[]{:S(2)}, u32[]{:S(2)}) collective-permute-start(bf16[64,512]{1,0:T(8,128)(2,1)S(1)} %collective-permute-done.19), channel_id=1, source_target_pairs={{0,2},{1,3},{2,0},{3,1},{4,6},{5,7},{6,4},{7,5},{8,10},{9,11},{10,... | collective-permute-start | bytes 196616 | tf_op jit(solution)/shard_map/ppermute | solution.py:30
  32.5 2.2 %collective-permute-start.18 = (bf16[64,512]{1,0:T(8,128)(2,1)S(1)}, bf16[64,512]{1,0:T(8,128)(2,1)S(1)}, u32[]{:S(2)}, u32[]{:S(2)}) collective-permute-start(bf16[64,512]{1,0:T(8,128)(2,1)S(1)} %collective-permute-done.17), channel_id=1, source_target_pairs={{0,2},{1,3},{2,0},{3,1},{4,6},{5,7},{6,4},{7,5},{8,10},{9,11},{10,... | collective-permute-start | bytes 196616 | tf_op jit(solution)/shard_map/ppermute | solution.py:30
  33.2 4.4 %collective-permute-start.13 = (bf16[128,512]{1,0:T(8,128)(2,1)S(1)}, bf16[128,512]{1,0:T(8,128)(2,1)S(1)}, u32[]{:S(2)}, u32[]{:S(2)}) collective-permute-start(bf16[128,512]{1,0:T(8,128)(2,1)S(1)} %collective-permute-done.11), channel_id=1, source_target_pairs={{0,6},{1,7},{2,0},{3,1},{4,2},{5,3},{6,4},{7,5},{8,14},{9,15},{10,... | collective-permute-start | bytes 393224 | tf_op jit(solution)/shard_map/ppermute | solution.py:30
  34.2 3.4 %collective-permute-start.12 = (bf16[128,512]{1,0:T(8,128)(2,1)S(1)}, bf16[128,512]{1,0:T(8,128)(2,1)S(1)}, u32[]{:S(2)}, u32[]{:S(2)}) collective-permute-start(bf16[128,512]{1,0:T(8,128)(2,1)S(1)} %collective-permute-done.11), channel_id=1, source_target_pairs={{0,2},{1,3},{2,0},{3,1},{4,6},{5,7},{6,4},{7,5},{8,10},{9,11},{10,... | collective-permute-start | bytes 393224 | tf_op jit(solution)/shard_map/ppermute | solution.py:30
  34.2 3.4 %collective-permute-start.10 = (bf16[128,512]{1,0:T(8,128)(2,1)S(1)}, bf16[128,512]{1,0:T(8,128)(2,1)S(1)}, u32[]{:S(2)}, u32[]{:S(2)}) collective-permute-start(bf16[128,512]{1,0:T(8,128)(2,1)S(1)} %collective-permute-done.9), channel_id=1, source_target_pairs={{0,2},{1,3},{2,0},{3,1},{4,6},{5,7},{6,4},{7,5},{8,10},{9,11},{10,... | collective-permute-start | bytes 393224 | tf_op jit(solution)/shard_map/ppermute | solution.py:30
  36.9 4.5 %collective-permute-start.23 = (bf16[64,2048]{1,0:T(8,128)(2,1)S(1)}, bf16[64,2048]{1,0:T(8,128)(2,1)S(1)}, u32[]{:S(2)}, u32[]{:S(2)}) collective-permute-start(bf16[64,2048]{1,0:T(8,128)(2,1)S(1)} %attend_0_2.1), channel_id=1, source_target_pairs={{0,3},{1,2},{2,0},{3,1},{4,7},{5,6},{6,4},{7,5},{8,11},{9,10},{10,... | collective-permute-start | bytes 786440 | tf_op jit(solution)/shard_map/ppermute | solution.py:30
  37.0 4.4 %collective-permute-start.22 = (bf16[64,2048]{1,0:T(8,128)(2,1)S(1)}, bf16[64,2048]{1,0:T(8,128)(2,1)S(1)}, u32[]{:S(2)}, u32[]{:S(2)}) collective-permute-start(bf16[64,2048]{1,0:T(8,128)(2,1)S(1)} %attend_0_2.1), channel_id=1, source_target_pairs={{0,2},{1,3},{2,0},{3,1},{4,6},{5,7},{6,4},{7,5},{8,10},{9,11},{10,... | collective-permute-start | bytes 786440 | tf_op jit(solution)/shard_map/ppermute | solution.py:30
  37.8 14.7 %collective-permute-start.15 = (bf16[64,2048]{1,0:T(8,128)(2,1)S(1)}, bf16[64,2048]{1,0:T(8,128)(2,1)S(1)}, u32[]{:S(2)}, u32[]{:S(2)}) collective-permute-start(bf16[64,2048]{1,0:T(8,128)(2,1)S(1)} %get-tuple-element.36), channel_id=1, source_target_pairs={{0,2},{1,3},{2,1},{3,0},{4,6},{5,7},{6,5},{7,4},{8,10},{9,11},{10,... | collective-permute-start | bytes 786440 | tf_op jit(solution)/shard_map/ppermute | solution.py:30
  41.5 6.1 %collective-permute-start.26 = (bf16[64,512]{1,0:T(8,128)(2,1)S(1)}, bf16[64,512]{1,0:T(8,128)(2,1)S(1)}, u32[]{:S(2)}, u32[]{:S(2)}) collective-permute-start(bf16[64,512]{1,0:T(8,128)(2,1)S(1)} %get-tuple-element.41.refs_4_), channel_id=1, source_target_pairs={{0,2},{1,3},{2,8},{3,9},{4,6},{5,7},{6,12},{7,13},{8,10},{9,11},{1... | collective-permute-start | bytes 196616 | tf_op jit(solution)/shard_map/ppermute | solution.py:30
  43.3 4.8 %collective-permute-start.24 = (bf16[64,512]{1,0:T(8,128)(2,1)S(1)}, bf16[64,512]{1,0:T(8,128)(2,1)S(1)}, u32[]{:S(2)}, u32[]{:S(2)}) collective-permute-start(bf16[64,512]{1,0:T(8,128)(2,1)S(1)} %get-tuple-element.41.refs_4_), channel_id=1, source_target_pairs={{0,2},{1,3},{2,4},{3,5},{4,6},{5,7},{6,0},{7,1},{8,10},{9,11},{10,... | collective-permute-start | bytes 196616 | tf_op jit(solution)/shard_map/ppermute | solution.py:30
  47.6 1.9 %collective-permute-start.28 = (bf16[64,512]{1,0:T(8,128)(2,1)S(1)}, bf16[64,512]{1,0:T(8,128)(2,1)S(1)}, u32[]{:S(2)}, u32[]{:S(2)}) collective-permute-start(bf16[64,512]{1,0:T(8,128)(2,1)S(1)} %collective-permute-done.26), channel_id=1, source_target_pairs={{0,6},{1,7},{2,0},{3,1},{4,2},{5,3},{6,4},{7,5},{8,14},{9,15},{10,... | collective-permute-start | bytes 196616 | tf_op jit(solution)/shard_map/ppermute | solution.py:30
  47.6 1.9 %collective-permute-start.27 = (bf16[64,512]{1,0:T(8,128)(2,1)S(1)}, bf16[64,512]{1,0:T(8,128)(2,1)S(1)}, u32[]{:S(2)}, u32[]{:S(2)}) collective-permute-start(bf16[64,512]{1,0:T(8,128)(2,1)S(1)} %collective-permute-done.26), channel_id=1, source_target_pairs={{0,2},{1,3},{2,0},{3,1},{4,6},{5,7},{6,4},{7,5},{8,10},{9,11},{10,... | collective-permute-start | bytes 196616 | tf_op jit(solution)/shard_map/ppermute | solution.py:30
  48.1 1.4 %collective-permute-start.25 = (bf16[64,512]{1,0:T(8,128)(2,1)S(1)}, bf16[64,512]{1,0:T(8,128)(2,1)S(1)}, u32[]{:S(2)}, u32[]{:S(2)}) collective-permute-start(bf16[64,512]{1,0:T(8,128)(2,1)S(1)} %collective-permute-done.24), channel_id=1, source_target_pairs={{0,2},{1,3},{2,0},{3,1},{4,6},{5,7},{6,4},{7,5},{8,10},{9,11},{10,... | collective-permute-start | bytes 196616 | tf_op jit(solution)/shard_map/ppermute | solution.py:30
  49.6 5.6 %collective-permute-start.30 = (bf16[32,2048]{1,0:T(8,128)(2,1)S(1)}, bf16[32,2048]{1,0:T(8,128)(2,1)S(1)}, u32[]{:S(2)}, u32[]{:S(2)}) collective-permute-start(bf16[32,2048]{1,0:T(8,128)(2,1)S(1)} %get-tuple-element.45), channel_id=1, source_target_pairs={{0,2},{1,3},{2,1},{3,0},{4,6},{5,7},{6,5},{7,4},{8,10},{9,11},{10,... | collective-permute-start | bytes 393224 | tf_op jit(solution)/shard_map/ppermute | solution.py:30
  52.5 4.1 %collective-permute-start.16 = (bf16[64,2048]{1,0:T(8,128)(2,1)S(1)}, bf16[64,2048]{1,0:T(8,128)(2,1)S(1)}, u32[]{:S(2)}, u32[]{:S(2)}) collective-permute-start(bf16[64,2048]{1,0:T(8,128)(2,1)S(1)} %collective-permute-done.15.refs_2_), channel_id=1, source_target_pairs={{0,2},{1,3},{2,0},{3,1},{4,6},{5,7},{6,4},{7,5},{8,10},{9,11},{10,... | collective-permute-start | bytes 786440 | tf_op jit(solution)/shard_map/ppermute | solution.py:30
  52.6 4.0 %collective-permute-start.14 = (bf16[64,1024]{1,0:T(8,128)(2,1)S(1)}, bf16[64,1024]{1,0:T(8,128)(2,1)S(1)}, u32[]{:S(2)}, u32[]{:S(2)}) collective-permute-start(bf16[64,1024]{1,0:T(8,128)(2,1)S(1)} %get-tuple-element.35), channel_id=1, source_target_pairs={{0,2},{1,3},{2,0},{3,1},{4,6},{5,7},{6,4},{7,5},{8,10},{9,11},{10,... | collective-permute-start | bytes 393224 | tf_op jit(solution)/shard_map/ppermute | solution.py:30
  55.2 1.4 %collective-permute-start.31 = (bf16[32,2048]{1,0:T(8,128)(2,1)S(1)}, bf16[32,2048]{1,0:T(8,128)(2,1)S(1)}, u32[]{:S(2)}, u32[]{:S(2)}) collective-permute-start(bf16[32,2048]{1,0:T(8,128)(2,1)S(1)} %collective-permute-done.30.refs_6_), channel_id=1, source_target_pairs={{0,2},{1,3},{2,0},{3,1},{4,6},{5,7},{6,4},{7,5},{8,10},{9,11},{10,... | collective-permute-start | bytes 393224 | tf_op jit(solution)/shard_map/ppermute | solution.py:30
  55.2 1.4 %collective-permute-start.29 = (bf16[32,1024]{1,0:T(8,128)(2,1)S(1)}, bf16[32,1024]{1,0:T(8,128)(2,1)S(1)}, u32[]{:S(2)}, u32[]{:S(2)}) collective-permute-start(bf16[32,1024]{1,0:T(8,128)(2,1)S(1)} %get-tuple-element.44), channel_id=1, source_target_pairs={{0,2},{1,3},{2,0},{3,1},{4,6},{5,7},{6,4},{7,5},{8,10},{9,11},{10,... | collective-permute-start | bytes 196616 | tf_op jit(solution)/shard_map/ppermute | solution.py:30

commit v6 on v5

--- a/solution.py
+++ b/solution.py
@@ -251,10 +251,11 @@
 
 
 def final_body(spans, rows, n_head, n_sec, final_ref, *refs):
-    out_ref = refs[-1]
+    out_hbm, held, sems = refs[-3:]
+    copies = []
     per = 2 + 2 * (n_head - 1)
     share = rows // n_head
-    part = out_ref.shape[2]
+    part = held.shape[2]
     last = jnp.broadcast_to(place("section"), (share, part)) == n_sec - 1
     for i, (low, high) in enumerate(spans):
         keep, given = refs[i * per : i * per + 2]
@@ -268,7 +269,11 @@
                 here = here + relay[k][at, (n_sec - 1) * part :].astype(F32)
                 there = there + came[k][at, :part].astype(F32)
             live = final_ref[g * share : (g + 1) * share]
-            out_ref[g] = keep_live(jnp.where(last, here, there), live)
+            held[g] = keep_live(jnp.where(last, here, there), live)
+            copies.append(pltpu.make_async_copy(held.at[g], out_hbm.at[g], sems.at[g]))
+            copies[-1].start()
+    for copy in copies:
+        copy.wait()
 
 
 def in_hbm(value):
@@ -485,7 +490,11 @@
         functools.partial(final_body, nexts, rows, n_head, n_sec),
         out_shape=array(F32, groups, share, part_width),
         in_specs=[VMEM] * (1 + len(ends)),
-        out_specs=VMEM,
+        out_specs=HBM,
+        scratch_shapes=[
+            pltpu.VMEM((groups, share, part_width), F32),
+            pltpu.SemaphoreType.DMA((groups,)),
+        ],
         compiler_params=params(12),
         name="final",
     )(final_live, *ends)

time: 57.6 us -> 57.8 us (level)
  no operation moved by 1% of the time
where the time goes in v6:
time: 57.8 us; the launch traced here: 57.6 us
  starting transfers between devices  30.3 us (52%)
  waiting for transfers between devices  12.9 us (22%)
  Pallas kernels  11.6 us (20%)
  between operations  1.07 us (2%)
  local copies, waits for them, and re-layouts  1.04 us (2%)
  other arithmetic  0.77 us (1%)
    ppermute x32, starting transfers between devices, permute(): return lax.ppermute(value, AXES, pairs)  30.3 us
    ppermute x32, waiting for transfers between devices, permute(): return lax.ppermute(value, AXES, pairs)  12.9 us
    pallas_call x3, Pallas kernels, attend(): pl.pallas_call(functools.partial(attend_body, which, own, rows, n_seq, of...  5.55 us
    pallas_call x1, Pallas kernels, first_latent(): pl.pallas_call(functools.partial(first_latent_body, firsts, rows, cuts),...  2.36 us
    pallas_call x3, Pallas kernels, project(): pl.pallas_call(functools.partial(query_body, 1.0 / HD ** 0.5, section), o...  1.52 us
  transfers between devices with their start and end apart: 32, of which 9 were waited for; matrix products, arithmetic and copies ran while one was open for 1% of the time, Pallas kernels for 12%

profile of v6, /device:TPU:0, one launch (start us, length us, event | category | flops | bytes accessed | tf_op | source)
XLA Modules:
  0.0 57.6 jit_solution(15832363561250384160)
XLA Ops:
  0.6 2.4 %first_latent.1 = (bf16[192,2048]{1,0:T(8,128)(2,1)S(1)}, f32[192,512]{1,0:T(8,128)S(1)}, bf16[128,512]{1,0:T(8,128)(2,1)S(1)}, bf16[64,512]{1,0:T(8,128)(2,1)S(1)}) custom-call(bf16[192,2048]{1,0:T(8,128)(2,1)} %bitcast.26, f32[1,2048]{1,0:T(1,128)} %refs_3_.3, bf16[2048,512]{1,0:T(8,128)(2,1)} %bitcast.20, f32[1,512]{1,0:T(1,128)} %refs_5_.3), custom_call_target="tpu_custom_call" | custom-call | tf_op jit(solution)/shard_map/first_latent/pallas_call | solution.py:342
  3.0 1.4 %collective-permute-start.2 = (bf16[128,512]{1,0:T(8,128)(2,1)S(1)}, bf16[128,512]{1,0:T(8,128)(2,1)S(1)}, u32[]{:S(2)}, u32[]{:S(2)}) collective-permute-start(bf16[128,512]{1,0:T(8,128)(2,1)S(1)} %get-tuple-element.28.refs_0_), channel_id=1, source_target_pairs={{0,10},{1,11},{2,0},{3,1},{4,14},{5,15},{6,4},{7,5},{8,2},{9,3},{1... | collective-permute-start | bytes 393224 | tf_op jit(solution)/shard_map/ppermute | solution.py:30
  4.4 1.9 %collective-permute-start = (bf16[128,512]{1,0:T(8,128)(2,1)S(1)}, bf16[128,512]{1,0:T(8,128)(2,1)S(1)}, u32[]{:S(2)}, u32[]{:S(2)}) collective-permute-start(bf16[128,512]{1,0:T(8,128)(2,1)S(1)} %get-tuple-element.28.refs_0_), channel_id=1, source_target_pairs={{0,6},{1,7},{2,0},{3,1},{4,2},{5,3},{6,4},{7,5},{8,14},{9,15},{10,... | collective-permute-start | bytes 393224 | tf_op jit(solution)/shard_map/ppermute | solution.py:30
  6.2 0.7 %collective-permute-done.2 = bf16[128,512]{1,0:T(8,128)(2,1)S(1)} collective-permute-done((bf16[128,512]{1,0:T(8,128)(2,1)S(1)}, bf16[128,512]{1,0:T(8,128)(2,1)S(1)}, u32[]{:S(2)}, u32[]{:S(2)}) %collective-permute-start.2) | collective-permute-done | bytes 131104 | tf_op jit(solution)/shard_map/ppermute | solution.py:30
  6.9 4.5 %collective-permute-start.4 = (bf16[128,512]{1,0:T(8,128)(2,1)S(1)}, bf16[128,512]{1,0:T(8,128)(2,1)S(1)}, u32[]{:S(2)}, u32[]{:S(2)}) collective-permute-start(bf16[128,512]{1,0:T(8,128)(2,1)S(1)} %collective-permute-done.2), channel_id=1, source_target_pairs={{0,2},{1,3},{2,4},{3,5},{4,6},{5,7},{6,0},{7,1},{8,10},{9,11},{10,... | collective-permute-start | bytes 393224 | tf_op jit(solution)/shard_map/ppermute | solution.py:30
  11.4 0.5 collective-permute-start.1
  11.9 0.7 %prepare.1 = (f32[64,1024]{1,0:T(8,128)S(1)}, f32[192,128]{1,0:T(8,128)S(1)}, f32[96,128]{1,0:T(8,128)S(1)}) custom-call(s32[3]{0:T(128)} %lengths_ref.1), custom_call_target="tpu_custom_call" | custom-call | flops 6000000000 | bytes 1048576 | tf_op jit(solution)/shard_map/prepare/pallas_call | solution.py:327
  12.6 1.4 %shard_map.104.absorbed_ref = bf16[8,192,512]{2,1,0:T(8,128)(2,1)S(1)} custom-call(bf16[192,2048]{1,0:T(8,128)(2,1)S(1)} %get-tuple-element.26.normed_ref, bf16[2048,1024]{1,0:T(8,128)(2,1)S(1)} %bitcast.12, bf16[512,1024]{1,0:T(8,128)(2,1)S(1)} %bitcast.23), custom_call_target="tpu_custom_call" | custom-call | flops 1006632960 | bytes 5636096 | tf_op jit(solution)/shard_map/pallas_call | solution.py:383
  14.1 0.7 %copy-done = bf16[1,1024,2048]{2,1,0:T(8,128)(2,1)S(1)} copy-done((bf16[1,1024,2048]{2,1,0:T(8,128)(2,1)S(1)}, bf16[1,1024,2048]{2,1,0:T(8,128)(2,1)}, u32[]{:S(2)}) %copy-start) | copy-done | bytes 4194328
  14.8 0.3 copy-done.2
  15.1 1.5 %attend_0_0.1 = bf16[64,2048]{1,0:T(8,128)(2,1)S(1)} custom-call(bf16[8,192,512]{2,1,0:T(8,128)(2,1)S(1)} %shard_map.104.absorbed_ref, f32[64,1024]{1,0:T(8,128)S(1)} %get-tuple-element.27.bias_ref, bf16[128,512]{1,0:T(8,128)(2,1)S(1)} %get-tuple-element.28.refs_0_, bf16[128,512]{1,0:T(8,128)(2,1)S(1)} %collective-permute-done.1.refs_1_, ...), custom_call_target="tpu_custom_call" | custom-call | flops 268435456 | bytes 5242880 | tf_op jit(solution)/shard_map/attend_0_0/pallas_call | solution.py:414
  16.7 0.1 collective-permute-start.6
  16.7 0.5 collective-permute-start.5
  17.2 1.8 %attend_0_1.1 = bf16[64,2048]{1,0:T(8,128)(2,1)S(1)} custom-call(bf16[8,192,512]{2,1,0:T(8,128)(2,1)S(1)} %shard_map.104.absorbed_ref, f32[64,1024]{1,0:T(8,128)S(1)} %get-tuple-element.27.bias_ref, bf16[128,512]{1,0:T(8,128)(2,1)S(1)} %get-tuple-element.28.refs_0_, bf16[128,512]{1,0:T(8,128)(2,1)S(1)} %collective-permute-done.1.refs_1_, ...), custom_call_target="tpu_custom_call" | custom-call | flops 536870912 | bytes 5242880 | tf_op jit(solution)/shard_map/attend_0_1/pallas_call | solution.py:414
  19.0 0.1 collective-permute-start.8
  19.1 0.5 collective-permute-start.7
  19.6 1.0 %collective-permute-done.6.refs_2_ = bf16[64,2048]{1,0:T(8,128)(2,1)S(1)} collective-permute-done((bf16[64,2048]{1,0:T(8,128)(2,1)S(1)}, bf16[64,2048]{1,0:T(8,128)(2,1)S(1)}, u32[]{:S(2)}, u32[]{:S(2)}) %collective-permute-start.6) | collective-permute-done | bytes 262176 | tf_op jit(solution)/shard_map/ppermute | solution.py:30
  20.6 2.8 %collective-permute-done.8.refs_4_ = bf16[64,2048]{1,0:T(8,128)(2,1)S(1)} collective-permute-done((bf16[64,2048]{1,0:T(8,128)(2,1)S(1)}, bf16[64,2048]{1,0:T(8,128)(2,1)S(1)}, u32[]{:S(2)}, u32[]{:S(2)}) %collective-permute-start.8) | collective-permute-done | bytes 262176 | tf_op jit(solution)/shard_map/ppermute | solution.py:30
  23.4 0.2 shard_map.105
  23.7 2.5 %collective-permute-start.11 = (bf16[128,512]{1,0:T(8,128)(2,1)S(1)}, bf16[128,512]{1,0:T(8,128)(2,1)S(1)}, u32[]{:S(2)}, u32[]{:S(2)}) collective-permute-start(bf16[128,512]{1,0:T(8,128)(2,1)S(1)} %get-tuple-element.32.refs_0_), channel_id=1, source_target_pairs={{0,2},{1,3},{2,8},{3,9},{4,6},{5,7},{6,12},{7,13},{8,10},{9,11},{1... | collective-permute-start | bytes 393224 | tf_op jit(solution)/shard_map/ppermute | solution.py:30
  26.1 0.7 %collective-permute-start.19 = (bf16[64,512]{1,0:T(8,128)(2,1)S(1)}, bf16[64,512]{1,0:T(8,128)(2,1)S(1)}, u32[]{:S(2)}, u32[]{:S(2)}) collective-permute-start(bf16[64,512]{1,0:T(8,128)(2,1)S(1)} %get-tuple-element.37.refs_4_), channel_id=1, source_target_pairs={{0,10},{1,11},{2,0},{3,1},{4,14},{5,15},{6,4},{7,5},{8,2},{9,3},{1... | collective-permute-start | bytes 196616 | tf_op jit(solution)/shard_map/ppermute | solution.py:30
  26.9 1.7 %collective-permute-start.17 = (bf16[64,512]{1,0:T(8,128)(2,1)S(1)}, bf16[64,512]{1,0:T(8,128)(2,1)S(1)}, u32[]{:S(2)}, u32[]{:S(2)}) collective-permute-start(bf16[64,512]{1,0:T(8,128)(2,1)S(1)} %get-tuple-element.37.refs_4_), channel_id=1, source_target_pairs={{0,6},{1,7},{2,0},{3,1},{4,2},{5,3},{6,4},{7,5},{8,14},{9,15},{10,... | collective-permute-start | bytes 196616 | tf_op jit(solution)/shard_map/ppermute | solution.py:30
  28.6 0.2 collective-permute-done.19
  28.8 3.7 %collective-permute-start.21 = (bf16[64,512]{1,0:T(8,128)(2,1)S(1)}, bf16[64,512]{1,0:T(8,128)(2,1)S(1)}, u32[]{:S(2)}, u32[]{:S(2)}) collective-permute-start(bf16[64,512]{1,0:T(8,128)(2,1)S(1)} %collective-permute-done.19), channel_id=1, source_target_pairs={{0,2},{1,3},{2,4},{3,5},{4,6},{5,7},{6,0},{7,1},{8,10},{9,11},{10,... | collective-permute-start | bytes 196616 | tf_op jit(solution)/shard_map/ppermute | solution.py:30
  32.5 0.7 %collective-permute-start.18 = (bf16[64,512]{1,0:T(8,128)(2,1)S(1)}, bf16[64,512]{1,0:T(8,128)(2,1)S(1)}, u32[]{:S(2)}, u32[]{:S(2)}) collective-permute-start(bf16[64,512]{1,0:T(8,128)(2,1)S(1)} %collective-permute-done.17), channel_id=1, source_target_pairs={{0,2},{1,3},{2,0},{3,1},{4,6},{5,7},{6,4},{7,5},{8,10},{9,11},{10,... | collective-permute-start | bytes 196616 | tf_op jit(solution)/shard_map/ppermute | solution.py:30
  33.2 0.2 collective-permute-start.13
  33.3 0.9 %collective-permute-done.21.refs_7_ = bf16[64,512]{1,0:T(8,128)(2,1)S(1)} collective-permute-done((bf16[64,512]{1,0:T(8,128)(2,1)S(1)}, bf16[64,512]{1,0:T(8,128)(2,1)S(1)}, u32[]{:S(2)}, u32[]{:S(2)}) %collective-permute-start.21) | collective-permute-done | bytes 65568 | tf_op jit(solution)/shard_map/ppermute | solution.py:30
  34.2 0.5 collective-permute-start.10
  34.7 2.2 %attend_0_2.1 = bf16[64,2048]{1,0:T(8,128)(2,1)S(1)} custom-call(bf16[8,192,512]{2,1,0:T(8,128)(2,1)S(1)} %shard_map.104.absorbed_ref, f32[64,1024]{1,0:T(8,128)S(1)} %get-tuple-element.27.bias_ref, bf16[128,512]{1,0:T(8,128)(2,1)S(1)} %get-tuple-element.28.refs_0_, bf16[128,512]{1,0:T(8,128)(2,1)S(1)} %collective-permute-done.1.refs_1_, ...), custom_call_target="tpu_custom_call" | custom-call | flops 805306368 | bytes 5242880 | tf_op jit(solution)/shard_map/attend_0_2/pallas_call | solution.py:414
  36.9 0.1 collective-permute-start.23
  37.0 0.5 collective-permute-start.22
  37.5 0.1 shard_map.106.absorbed_ref
  37.6 0.2 attend_1_0.1
  37.8 3.6 %collective-permute-start.15 = (bf16[64,2048]{1,0:T(8,128)(2,1)S(1)}, bf16[64,2048]{1,0:T(8,128)(2,1)S(1)}, u32[]{:S(2)}, u32[]{:S(2)}) collective-permute-start(bf16[64,2048]{1,0:T(8,128)(2,1)S(1)} %get-tuple-element.36), channel_id=1, source_target_pairs={{0,2},{1,3},{2,1},{3,0},{4,6},{5,7},{6,5},{7,4},{8,10},{9,11},{10,... | collective-permute-start | bytes 786440 | tf_op jit(solution)/shard_map/ppermute | solution.py:30
  41.4 0.1 shard_map.107
  41.5 1.8 %collective-permute-start.26 = (bf16[64,512]{1,0:T(8,128)(2,1)S(1)}, bf16[64,512]{1,0:T(8,128)(2,1)S(1)}, u32[]{:S(2)}, u32[]{:S(2)}) collective-permute-start(bf16[64,512]{1,0:T(8,128)(2,1)S(1)} %get-tuple-element.41.refs_4_), channel_id=1, source_target_pairs={{0,2},{1,3},{2,8},{3,9},{4,6},{5,7},{6,12},{7,13},{8,10},{9,11},{1... | collective-permute-start | bytes 196616 | tf_op jit(solution)/shard_map/ppermute | solution.py:30
  43.3 0.6 collective-permute-start.24
  43.9 3.7 %collective-permute-done.26 = bf16[64,512]{1,0:T(8,128)(2,1)S(1)} collective-permute-done((bf16[64,512]{1,0:T(8,128)(2,1)S(1)}, bf16[64,512]{1,0:T(8,128)(2,1)S(1)}, u32[]{:S(2)}, u32[]{:S(2)}) %collective-permute-start.26) | collective-permute-done | bytes 65568 | tf_op jit(solution)/shard_map/ppermute | solution.py:30
  47.6 0.5 collective-permute-start.27
  48.2 1.4 %collective-permute-done.28.refs_7_ = bf16[64,512]{1,0:T(8,128)(2,1)S(1)} collective-permute-done((bf16[64,512]{1,0:T(8,128)(2,1)S(1)}, bf16[64,512]{1,0:T(8,128)(2,1)S(1)}, u32[]{:S(2)}, u32[]{:S(2)}) %collective-permute-start.28) | collective-permute-done | bytes 65568 | tf_op jit(solution)/shard_map/ppermute | solution.py:30
  49.6 3.0 %collective-permute-start.30 = (bf16[32,2048]{1,0:T(8,128)(2,1)S(1)}, bf16[32,2048]{1,0:T(8,128)(2,1)S(1)}, u32[]{:S(2)}, u32[]{:S(2)}) collective-permute-start(bf16[32,2048]{1,0:T(8,128)(2,1)S(1)} %get-tuple-element.45), channel_id=1, source_target_pairs={{0,2},{1,3},{2,1},{3,0},{4,6},{5,7},{6,5},{7,4},{8,10},{9,11},{10,... | collective-permute-start | bytes 393224 | tf_op jit(solution)/shard_map/ppermute | solution.py:30
  52.5 0.1 collective-permute-start.16
  52.6 0.4 collective-permute-start.14
  53.0 2.1 %collective-permute-done.30.refs_6_ = bf16[32,2048]{1,0:T(8,128)(2,1)S(1)} collective-permute-done((bf16[32,2048]{1,0:T(8,128)(2,1)S(1)}, bf16[32,2048]{1,0:T(8,128)(2,1)S(1)}, u32[]{:S(2)}, u32[]{:S(2)}) %collective-permute-start.30) | collective-permute-done | bytes 131104 | tf_op jit(solution)/shard_map/ppermute | solution.py:30
  55.2 0.5 collective-permute-start.29
  55.7 0.8 %pad_maximum_fusion = f32[192,512]{1,0:T(8,128)} fusion(f32[64,512]{1,0:T(8,128)S(1)} %get-tuple-element.47, f32[128,512]{1,0:T(8,128)S(1)} %get-tuple-element.46), kind=kLoop, calls=%fused_computation | loop fusion | flops 98304 | bytes 786432 | tf_op jit(solution)/shard_map/concatenate | solution.py:501
  56.5 0.2 collective-permute-done.29.refs_5_
  56.6 0.8 %final.1 = f32[3,32,1024]{2,1,0:T(8,128)} custom-call(f32[96,128]{1,0:T(8,128)S(1)} %get-tuple-element.25.final_ref, f32[64,1024]{1,0:T(8,128)S(1)} %get-tuple-element.34.refs_0_, bf16[64,1024]{1,0:T(8,128)(2,1)S(1)} %collective-permute-done.14.refs_1_, bf16[64,2048]{1,0:T(8,128)(2,1)S(1)} %collective-permute-done.15.refs_2_, ...), custom_call_target="tpu_custom_call" | custom-call | tf_op jit(solution)/shard_map/final/pallas_call | solution.py:489
  (46 shorter events, 0.2 us)
Async XLA Ops:
  3.0 9.6 %copy-start.1 = (bf16[1,2048,1024]{2,1,0:T(8,128)(2,1)S(1)}, bf16[1,2048,1024]{2,1,0:T(8,128)(2,1)}, u32[]{:S(2)}) copy-start(bf16[1,2048,1024]{2,1,0:T(8,128)(2,1)} %param.12) | copy-start | bytes 12582916
  3.0 9.6 %copy-start.4 = (bf16[1,512,1024]{2,1,0:T(8,128)(2,1)S(1)}, bf16[1,512,1024]{2,1,0:T(8,128)(2,1)}, u32[]{:S(2)}) copy-start(bf16[1,512,1024]{2,1,0:T(8,128)(2,1)} %param.15) | copy-start | bytes 3145732
  3.0 3.9 %collective-permute-start.2 = (bf16[128,512]{1,0:T(8,128)(2,1)S(1)}, bf16[128,512]{1,0:T(8,128)(2,1)S(1)}, u32[]{:S(2)}, u32[]{:S(2)}) collective-permute-start(bf16[128,512]{1,0:T(8,128)(2,1)S(1)} %get-tuple-element.28.refs_0_), channel_id=1, source_target_pairs={{0,10},{1,11},{2,0},{3,1},{4,14},{5,15},{6,4},{7,5},{8,2},{9,3},{1... | collective-permute-start | bytes 393224 | tf_op jit(solution)/shard_map/ppermute | solution.py:30
  4.4 7.0 %collective-permute-start = (bf16[128,512]{1,0:T(8,128)(2,1)S(1)}, bf16[128,512]{1,0:T(8,128)(2,1)S(1)}, u32[]{:S(2)}, u32[]{:S(2)}) collective-permute-start(bf16[128,512]{1,0:T(8,128)(2,1)S(1)} %get-tuple-element.28.refs_0_), channel_id=1, source_target_pairs={{0,6},{1,7},{2,0},{3,1},{4,2},{5,3},{6,4},{7,5},{8,14},{9,15},{10,... | collective-permute-start | bytes 393224 | tf_op jit(solution)/shard_map/ppermute | solution.py:30
  6.9 7.1 %collective-permute-start.4 = (bf16[128,512]{1,0:T(8,128)(2,1)S(1)}, bf16[128,512]{1,0:T(8,128)(2,1)S(1)}, u32[]{:S(2)}, u32[]{:S(2)}) collective-permute-start(bf16[128,512]{1,0:T(8,128)(2,1)S(1)} %collective-permute-done.2), channel_id=1, source_target_pairs={{0,2},{1,3},{2,4},{3,5},{4,6},{5,7},{6,0},{7,1},{8,10},{9,11},{10,... | collective-permute-start | bytes 393224 | tf_op jit(solution)/shard_map/ppermute | solution.py:30
  11.4 2.7 %collective-permute-start.3 = (bf16[128,512]{1,0:T(8,128)(2,1)S(1)}, bf16[128,512]{1,0:T(8,128)(2,1)S(1)}, u32[]{:S(2)}, u32[]{:S(2)}) collective-permute-start(bf16[128,512]{1,0:T(8,128)(2,1)S(1)} %collective-permute-done.2), channel_id=1, source_target_pairs={{0,2},{1,3},{2,0},{3,1},{4,6},{5,7},{6,4},{7,5},{8,10},{9,11},{10,... | collective-permute-start | bytes 393224 | tf_op jit(solution)/shard_map/ppermute | solution.py:30
  11.4 2.7 %collective-permute-start.1 = (bf16[128,512]{1,0:T(8,128)(2,1)S(1)}, bf16[128,512]{1,0:T(8,128)(2,1)S(1)}, u32[]{:S(2)}, u32[]{:S(2)}) collective-permute-start(bf16[128,512]{1,0:T(8,128)(2,1)S(1)} %collective-permute-done), channel_id=1, source_target_pairs={{0,2},{1,3},{2,0},{3,1},{4,6},{5,7},{6,4},{7,5},{8,10},{9,11},{10,... | collective-permute-start | bytes 393224 | tf_op jit(solution)/shard_map/ppermute | solution.py:30
  12.6 2.2 %copy-start = (bf16[1,1024,2048]{2,1,0:T(8,128)(2,1)S(1)}, bf16[1,1024,2048]{2,1,0:T(8,128)(2,1)}, u32[]{:S(2)}) copy-start(bf16[1,1024,2048]{2,1,0:T(8,128)(2,1)} %param.17) | copy-start | bytes 12582916
  12.6 2.5 %copy-start.2 = (bf16[1,512,1024]{2,1,0:T(8,128)(2,1)S(1)}, bf16[1,512,1024]{2,1,0:T(8,128)(2,1)}, u32[]{:S(2)}) copy-start(bf16[1,512,1024]{2,1,0:T(8,128)(2,1)} %param.16) | copy-start | bytes 3145732
  16.6 6.8 %copy-start.3 = (bf16[1,2048,512]{2,1,0:T(8,128)(2,1)S(1)}, bf16[1,2048,512]{2,1,0:T(8,128)(2,1)}, u32[]{:S(2)}) copy-start(bf16[1,2048,512]{2,1,0:T(8,128)(2,1)} %param.13) | copy-start | bytes 6291460
  16.6 6.8 %copy-start.5 = (bf16[3,64,2048]{2,1,0:T(8,128)(2,1)S(1)}, bf16[3,64,2048]{2,1,0:T(8,128)(2,1)}, u32[]{:S(2)}) copy-start(bf16[3,64,2048]{2,1,0:T(8,128)(2,1)} %param.9) | copy-start | bytes 2359300
  16.6 6.8 %copy-start.6 = (f32[1,2048]{1,0:T(1,128)S(1)}, f32[1,2048]{1,0:T(1,128)}, u32[]{:S(2)}) copy-start(f32[1,2048]{1,0:T(1,128)} %refs_3_.3) | copy-start | bytes 24580
  16.7 6.8 %copy-start.7 = (f32[1,512]{1,0:T(1,128)S(1)}, f32[1,512]{1,0:T(1,128)}, u32[]{:S(2)}) copy-start(f32[1,512]{1,0:T(1,128)} %refs_5_.3) | copy-start | bytes 6148
  16.7 3.9 %collective-permute-start.6 = (bf16[64,2048]{1,0:T(8,128)(2,1)S(1)}, bf16[64,2048]{1,0:T(8,128)(2,1)S(1)}, u32[]{:S(2)}, u32[]{:S(2)}) collective-permute-start(bf16[64,2048]{1,0:T(8,128)(2,1)S(1)} %attend_0_0.1), channel_id=1, source_target_pairs={{0,3},{1,2},{2,0},{3,1},{4,7},{5,6},{6,4},{7,5},{8,11},{9,10},{10,... | collective-permute-start | bytes 786440 | tf_op jit(solution)/shard_map/ppermute | solution.py:30
  16.7 3.9 %collective-permute-start.5 = (bf16[64,2048]{1,0:T(8,128)(2,1)S(1)}, bf16[64,2048]{1,0:T(8,128)(2,1)S(1)}, u32[]{:S(2)}, u32[]{:S(2)}) collective-permute-start(bf16[64,2048]{1,0:T(8,128)(2,1)S(1)} %attend_0_0.1), channel_id=1, source_target_pairs={{0,2},{1,3},{2,0},{3,1},{4,6},{5,7},{6,4},{7,5},{8,10},{9,11},{10,... | collective-permute-start | bytes 786440 | tf_op jit(solution)/shard_map/ppermute | solution.py:30
  19.0 4.4 %collective-permute-start.8 = (bf16[64,2048]{1,0:T(8,128)(2,1)S(1)}, bf16[64,2048]{1,0:T(8,128)(2,1)S(1)}, u32[]{:S(2)}, u32[]{:S(2)}) collective-permute-start(bf16[64,2048]{1,0:T(8,128)(2,1)S(1)} %attend_0_1.1), channel_id=1, source_target_pairs={{0,3},{1,2},{2,0},{3,1},{4,7},{5,6},{6,4},{7,5},{8,11},{9,10},{10,... | collective-permute-start | bytes 786440 | tf_op jit(solution)/shard_map/ppermute | solution.py:30
  19.1 4.3 %collective-permute-start.7 = (bf16[64,2048]{1,0:T(8,128)(2,1)S(1)}, bf16[64,2048]{1,0:T(8,128)(2,1)S(1)}, u32[]{:S(2)}, u32[]{:S(2)}) collective-permute-start(bf16[64,2048]{1,0:T(8,128)(2,1)S(1)} %attend_0_1.1), channel_id=1, source_target_pairs={{0,2},{1,3},{2,0},{3,1},{4,6},{5,7},{6,4},{7,5},{8,10},{9,11},{10,... | collective-permute-start | bytes 786440 | tf_op jit(solution)/shard_map/ppermute | solution.py:30
  23.7 9.5 %collective-permute-start.11 = (bf16[128,512]{1,0:T(8,128)(2,1)S(1)}, bf16[128,512]{1,0:T(8,128)(2,1)S(1)}, u32[]{:S(2)}, u32[]{:S(2)}) collective-permute-start(bf16[128,512]{1,0:T(8,128)(2,1)S(1)} %get-tuple-element.32.refs_0_), channel_id=1, source_target_pairs={{0,2},{1,3},{2,8},{3,9},{4,6},{5,7},{6,12},{7,13},{8,10},{9,11},{1... | collective-permute-start | bytes 393224 | tf_op jit(solution)/shard_map/ppermute | solution.py:30
  26.1 2.6 %collective-permute-start.19 = (bf16[64,512]{1,0:T(8,128)(2,1)S(1)}, bf16[64,512]{1,0:T(8,128)(2,1)S(1)}, u32[]{:S(2)}, u32[]{:S(2)}) collective-permute-start(bf16[64,512]{1,0:T(8,128)(2,1)S(1)} %get-tuple-element.37.refs_4_), channel_id=1, source_target_pairs={{0,10},{1,11},{2,0},{3,1},{4,14},{5,15},{6,4},{7,5},{8,2},{9,3},{1... | collective-permute-start | bytes 196616 | tf_op jit(solution)/shard_map/ppermute | solution.py:30
  26.9 7.3 %collective-permute-start.9 = (bf16[128,512]{1,0:T(8,128)(2,1)S(1)}, bf16[128,512]{1,0:T(8,128)(2,1)S(1)}, u32[]{:S(2)}, u32[]{:S(2)}) collective-permute-start(bf16[128,512]{1,0:T(8,128)(2,1)S(1)} %get-tuple-element.32.refs_0_), channel_id=1, source_target_pairs={{0,2},{1,3},{2,4},{3,5},{4,6},{5,7},{6,0},{7,1},{8,10},{9,11},{10,... | collective-permute-start | bytes 393224 | tf_op jit(solution)/shard_map/ppermute | solution.py:30
  26.9 5.6 %collective-permute-start.17 = (bf16[64,512]{1,0:T(8,128)(2,1)S(1)}, bf16[64,512]{1,0:T(8,128)(2,1)S(1)}, u32[]{:S(2)}, u32[]{:S(2)}) collective-permute-start(bf16[64,512]{1,0:T(8,128)(2,1)S(1)} %get-tuple-element.37.refs_4_), channel_id=1, source_target_pairs={{0,6},{1,7},{2,0},{3,1},{4,2},{5,3},{6,4},{7,5},{8,14},{9,15},{10,... | collective-permute-start | bytes 196616 | tf_op jit(solution)/shard_map/ppermute | solution.py:30
  28.8 5.4 %collective-permute-start.21 = (bf16[64,512]{1,0:T(8,128)(2,1)S(1)}, bf16[64,512]{1,0:T(8,128)(2,1)S(1)}, u32[]{:S(2)}, u32[]{:S(2)}) collective-permute-start(bf16[64,512]{1,0:T(8,128)(2,1)S(1)} %collective-permute-done.19), channel_id=1, source_target_pairs={{0,2},{1,3},{2,4},{3,5},{4,6},{5,7},{6,0},{7,1},{8,10},{9,11},{10,... | collective-permute-start | bytes 196616 | tf_op jit(solution)/shard_map/ppermute | solution.py:30
  32.5 2.2 %collective-permute-start.20 = (bf16[64,512]{1,0:T(8,128)(2,1)S(1)}, bf16[64,512]{1,0:T(8,128)(2,1)S(1)}, u32[]{:S(2)}, u32[]{:S(2)}) collective-permute-start(bf16[64,512]{1,0:T(8,128)(2,1)S(1)} %collective-permute-done.19), channel_id=1, source_target_pairs={{0,2},{1,3},{2,0},{3,1},{4,6},{5,7},{6,4},{7,5},{8,10},{9,11},{10,... | collective-permute-start | bytes 196616 | tf_op jit(solution)/shard_map/ppermute | solution.py:30
  32.5 2.2 %collective-permute-start.18 = (bf16[64,512]{1,0:T(8,128)(2,1)S(1)}, bf16[64,512]{1,0:T(8,128)(2,1)S(1)}, u32[]{:S(2)}, u32[]{:S(2)}) collective-permute-start(bf16[64,512]{1,0:T(8,128)(2,1)S(1)} %collective-permute-done.17), channel_id=1, source_target_pairs={{0,2},{1,3},{2,0},{3,1},{4,6},{5,7},{6,4},{7,5},{8,10},{9,11},{10,... | collective-permute-start | bytes 196616 | tf_op jit(solution)/shard_map/ppermute | solution.py:30
  33.2 4.4 %collective-permute-start.13 = (bf16[128,512]{1,0:T(8,128)(2,1)S(1)}, bf16[128,512]{1,0:T(8,128)(2,1)S(1)}, u32[]{:S(2)}, u32[]{:S(2)}) collective-permute-start(bf16[128,512]{1,0:T(8,128)(2,1)S(1)} %collective-permute-done.11), channel_id=1, source_target_pairs={{0,6},{1,7},{2,0},{3,1},{4,2},{5,3},{6,4},{7,5},{8,14},{9,15},{10,... | collective-permute-start | bytes 393224 | tf_op jit(solution)/shard_map/ppermute | solution.py:30
  34.2 3.4 %collective-permute-start.12 = (bf16[128,512]{1,0:T(8,128)(2,1)S(1)}, bf16[128,512]{1,0:T(8,128)(2,1)S(1)}, u32[]{:S(2)}, u32[]{:S(2)}) collective-permute-start(bf16[128,512]{1,0:T(8,128)(2,1)S(1)} %collective-permute-done.11), channel_id=1, source_target_pairs={{0,2},{1,3},{2,0},{3,1},{4,6},{5,7},{6,4},{7,5},{8,10},{9,11},{10,... | collective-permute-start | bytes 393224 | tf_op jit(solution)/shard_map/ppermute | solution.py:30
  34.2 3.4 %collective-permute-start.10 = (bf16[128,512]{1,0:T(8,128)(2,1)S(1)}, bf16[128,512]{1,0:T(8,128)(2,1)S(1)}, u32[]{:S(2)}, u32[]{:S(2)}) collective-permute-start(bf16[128,512]{1,0:T(8,128)(2,1)S(1)} %collective-permute-done.9), channel_id=1, source_target_pairs={{0,2},{1,3},{2,0},{3,1},{4,6},{5,7},{6,4},{7,5},{8,10},{9,11},{10,... | collective-permute-start | bytes 393224 | tf_op jit(solution)/shard_map/ppermute | solution.py:30
  36.9 4.5 %collective-permute-start.23 = (bf16[64,2048]{1,0:T(8,128)(2,1)S(1)}, bf16[64,2048]{1,0:T(8,128)(2,1)S(1)}, u32[]{:S(2)}, u32[]{:S(2)}) collective-permute-start(bf16[64,2048]{1,0:T(8,128)(2,1)S(1)} %attend_0_2.1), channel_id=1, source_target_pairs={{0,3},{1,2},{2,0},{3,1},{4,7},{5,6},{6,4},{7,5},{8,11},{9,10},{10,... | collective-permute-start | bytes 786440 | tf_op jit(solution)/shard_map/ppermute | solution.py:30
  37.0 4.4 %collective-permute-start.22 = (bf16[64,2048]{1,0:T(8,128)(2,1)S(1)}, bf16[64,2048]{1,0:T(8,128)(2,1)S(1)}, u32[]{:S(2)}, u32[]{:S(2)}) collective-permute-start(bf16[64,2048]{1,0:T(8,128)(2,1)S(1)} %attend_0_2.1), channel_id=1, source_target_pairs={{0,2},{1,3},{2,0},{3,1},{4,6},{5,7},{6,4},{7,5},{8,10},{9,11},{10,... | collective-permute-start | bytes 786440 | tf_op jit(solution)/shard_map/ppermute | solution.py:30
  37.8 14.7 %collective-permute-start.15 = (bf16[64,2048]{1,0:T(8,128)(2,1)S(1)}, bf16[64,2048]{1,0:T(8,128)(2,1)S(1)}, u32[]{:S(2)}, u32[]{:S(2)}) collective-permute-start(bf16[64,2048]{1,0:T(8,128)(2,1)S(1)} %get-tuple-element.36), channel_id=1, source_target_pairs={{0,2},{1,3},{2,1},{3,0},{4,6},{5,7},{6,5},{7,4},{8,10},{9,11},{10,... | collective-permute-start | bytes 786440 | tf_op jit(solution)/shard_map/ppermute | solution.py:30
  41.5 6.1 %collective-permute-start.26 = (bf16[64,512]{1,0:T(8,128)(2,1)S(1)}, bf16[64,512]{1,0:T(8,128)(2,1)S(1)}, u32[]{:S(2)}, u32[]{:S(2)}) collective-permute-start(bf16[64,512]{1,0:T(8,128)(2,1)S(1)} %get-tuple-element.41.refs_4_), channel_id=1, source_target_pairs={{0,2},{1,3},{2,8},{3,9},{4,6},{5,7},{6,12},{7,13},{8,10},{9,11},{1... | collective-permute-start | bytes 196616 | tf_op jit(solution)/shard_map/ppermute | solution.py:30
  43.3 4.8 %collective-permute-start.24 = (bf16[64,512]{1,0:T(8,128)(2,1)S(1)}, bf16[64,512]{1,0:T(8,128)(2,1)S(1)}, u32[]{:S(2)}, u32[]{:S(2)}) collective-permute-start(bf16[64,512]{1,0:T(8,128)(2,1)S(1)} %get-tuple-element.41.refs_4_), channel_id=1, source_target_pairs={{0,2},{1,3},{2,4},{3,5},{4,6},{5,7},{6,0},{7,1},{8,10},{9,11},{10,... | collective-permute-start | bytes 196616 | tf_op jit(solution)/shard_map/ppermute | solution.py:30
  47.6 1.9 %collective-permute-start.28 = (bf16[64,512]{1,0:T(8,128)(2,1)S(1)}, bf16[64,512]{1,0:T(8,128)(2,1)S(1)}, u32[]{:S(2)}, u32[]{:S(2)}) collective-permute-start(bf16[64,512]{1,0:T(8,128)(2,1)S(1)} %collective-permute-done.26), channel_id=1, source_target_pairs={{0,6},{1,7},{2,0},{3,1},{4,2},{5,3},{6,4},{7,5},{8,14},{9,15},{10,... | collective-permute-start | bytes 196616 | tf_op jit(solution)/shard_map/ppermute | solution.py:30
  47.6 1.9 %collective-permute-start.27 = (bf16[64,512]{1,0:T(8,128)(2,1)S(1)}, bf16[64,512]{1,0:T(8,128)(2,1)S(1)}, u32[]{:S(2)}, u32[]{:S(2)}) collective-permute-start(bf16[64,512]{1,0:T(8,128)(2,1)S(1)} %collective-permute-done.26), channel_id=1, source_target_pairs={{0,2},{1,3},{2,0},{3,1},{4,6},{5,7},{6,4},{7,5},{8,10},{9,11},{10,... | collective-permute-start | bytes 196616 | tf_op jit(solution)/shard_map/ppermute | solution.py:30
  48.1 1.4 %collective-permute-start.25 = (bf16[64,512]{1,0:T(8,128)(2,1)S(1)}, bf16[64,512]{1,0:T(8,128)(2,1)S(1)}, u32[]{:S(2)}, u32[]{:S(2)}) collective-permute-start(bf16[64,512]{1,0:T(8,128)(2,1)S(1)} %collective-permute-done.24), channel_id=1, source_target_pairs={{0,2},{1,3},{2,0},{3,1},{4,6},{5,7},{6,4},{7,5},{8,10},{9,11},{10,... | collective-permute-start | bytes 196616 | tf_op jit(solution)/shard_map/ppermute | solution.py:30
  49.6 5.6 %collective-permute-start.30 = (bf16[32,2048]{1,0:T(8,128)(2,1)S(1)}, bf16[32,2048]{1,0:T(8,128)(2,1)S(1)}, u32[]{:S(2)}, u32[]{:S(2)}) collective-permute-start(bf16[32,2048]{1,0:T(8,128)(2,1)S(1)} %get-tuple-element.45), channel_id=1, source_target_pairs={{0,2},{1,3},{2,1},{3,0},{4,6},{5,7},{6,5},{7,4},{8,10},{9,11},{10,... | collective-permute-start | bytes 393224 | tf_op jit(solution)/shard_map/ppermute | solution.py:30
  52.5 4.1 %collective-permute-start.16 = (bf16[64,2048]{1,0:T(8,128)(2,1)S(1)}, bf16[64,2048]{1,0:T(8,128)(2,1)S(1)}, u32[]{:S(2)}, u32[]{:S(2)}) collective-permute-start(bf16[64,2048]{1,0:T(8,128)(2,1)S(1)} %collective-permute-done.15.refs_2_), channel_id=1, source_target_pairs={{0,2},{1,3},{2,0},{3,1},{4,6},{5,7},{6,4},{7,5},{8,10},{9,11},{10,... | collective-permute-start | bytes 786440 | tf_op jit(solution)/shard_map/ppermute | solution.py:30
  52.6 4.0 %collective-permute-start.14 = (bf16[64,1024]{1,0:T(8,128)(2,1)S(1)}, bf16[64,1024]{1,0:T(8,128)(2,1)S(1)}, u32[]{:S(2)}, u32[]{:S(2)}) collective-permute-start(bf16[64,1024]{1,0:T(8,128)(2,1)S(1)} %get-tuple-element.35), channel_id=1, source_target_pairs={{0,2},{1,3},{2,0},{3,1},{4,6},{5,7},{6,4},{7,5},{8,10},{9,11},{10,... | collective-permute-start | bytes 393224 | tf_op jit(solution)/shard_map/ppermute | solution.py:30
  55.2 1.4 %collective-permute-start.31 = (bf16[32,2048]{1,0:T(8,128)(2,1)S(1)}, bf16[32,2048]{1,0:T(8,128)(2,1)S(1)}, u32[]{:S(2)}, u32[]{:S(2)}) collective-permute-start(bf16[32,2048]{1,0:T(8,128)(2,1)S(1)} %collective-permute-done.30.refs_6_), channel_id=1, source_target_pairs={{0,2},{1,3},{2,0},{3,1},{4,6},{5,7},{6,4},{7,5},{8,10},{9,11},{10,... | collective-permute-start | bytes 393224 | tf_op jit(solution)/shard_map/ppermute | solution.py:30
  55.2 1.4 %collective-permute-start.29 = (bf16[32,1024]{1,0:T(8,128)(2,1)S(1)}, bf16[32,1024]{1,0:T(8,128)(2,1)S(1)}, u32[]{:S(2)}, u32[]{:S(2)}) collective-permute-start(bf16[32,1024]{1,0:T(8,128)(2,1)S(1)} %get-tuple-element.44), channel_id=1, source_target_pairs={{0,2},{1,3},{2,0},{3,1},{4,6},{5,7},{6,4},{7,5},{8,10},{9,11},{10,... | collective-permute-start | bytes 196616 | tf_op jit(solution)/shard_map/ppermute | solution.py:30
